TPU v7x, 32 devices: a whole 2x2x4 slice. The times are simulated.
32 devices in a mesh: ha: 8 (over z, core), wa: 2 (over y), ba: 2 (over x).
Axes of the slice: x: 2, y: 2, z: 4, core: 2. Of those that a mesh axis runs over, the one named last changes fastest.
Arguments:
- tokens: bfloat16 [2, 128, 64, 384], P('ba', 'ha', 'wa'), may hold values from -6 to 6
- cotangent: bfloat16 [2, 128, 64, 384], P('ba', 'ha', 'wa'), may hold values from -6 to 6
- w_qkv: bfloat16 [384, 1152], replicated, may hold values from -0.20412415 to 0.20412415
- w_proj: bfloat16 [384, 384], replicated, may hold values from -0.3125 to 0.3125
- table_logits: float32 [12, 225], replicated, may hold values from -6 to 6
- logit_scale: float32 [12], replicated, may hold values from 1 to 5.5
- gain: float32 [384], replicated, may hold values from 0.5 to 1.5
Outputs:
- d_tokens: bfloat16 [2, 128, 64, 384], P('ba', 'ha', 'wa')
- d_wqkv: float32 [384, 1152], P(None, 'ba')
- d_wproj: float32 [384, 384], P(None, 'ba')
- d_table: float32 [12, 225], replicated
- d_scale: float32 [12], replicated
- d_gain: float32 [384], replicated
All inputs are finite; a program needn't handle non-finite values.
Results may differ from a plain program's by a relative error of at most 0.01.
The roundings to bfloat16 on the way count: a program that leaves them out, or rounds other values in their place, can miss the bound.
Values may be sent and summed in bfloat16 or wider, within the bound.
No kernel may reach another device: no remote copies, remote signals or barrier semaphores. Data moves between devices by JAX's collectives and lax.ppermute only.
A program may use at most 64 MiB of HBM per device.

v0:
```python
import math

import jax
import jax.numpy as jnp
from jax import lax
from jax.sharding import PartitionSpec as P

WIN = 8


EPS_NORM = 1e-05
MASK_FILL = -100.0
SCALE_CAP = math.log(100.0)
BIAS_RANGE = 16.0
HIGHEST = lax.Precision.HIGHEST


def from_behind(block, axis, distance):
    devices = range(lax.axis_size(axis))
    route = [((i - distance) % len(devices), i) for i in devices]
    return lax.ppermute(block, axis, route)


def coarse_product(form, left, right):
    return jnp.einsum(form, left, right, preferred_element_type=jnp.float32)


def fine_product(form, left, right):
    return jnp.einsum(form, left, right, precision=HIGHEST)


def to_windows(block, window):
    images, height, width, depth = block.shape
    tiles = block.reshape(images, height // window, window, width // window, window, depth)
    tiles = tiles.transpose(0, 1, 3, 2, 4, 5)
    return tiles.reshape(images, height // window * (width // window), window * window, depth)


def from_windows(tiles, images, height, width, window):
    depth = tiles.shape[-1]
    grid = tiles.reshape(images, height // window, width // window, window, window, depth)
    return grid.transpose(0, 1, 3, 2, 4, 5).reshape(images, height, width, depth)


def position_onehot(window):
    places = jnp.arange(window * window, dtype=jnp.int32)
    row_of = places // window
    col_of = places % window
    offset = (row_of[:, None] - row_of[None, :] + window - 1) * (2 * window - 1) + (
        col_of[:, None] - col_of[None, :] + window - 1
    )
    entries = jnp.arange((2 * window - 1) ** 2, dtype=jnp.int32)
    return (offset.reshape(-1)[:, None] == entries[None, :]).astype(jnp.float32)


def region_of(coords, extent, window):
    return (coords >= extent - window).astype(jnp.int32) + (coords >= extent - window // 2).astype(
        jnp.int32
    )


def region_mask(row_start, col_start, rows, cols, height, width, window):
    row_label = region_of(row_start + jnp.arange(rows, dtype=jnp.int32), height, window)
    col_label = region_of(col_start + jnp.arange(cols, dtype=jnp.int32), width, window)
    labels = row_label[:, None] * 3 + col_label[None, :]
    labels = labels.reshape(rows // window, window, cols // window, window).transpose(0, 2, 1, 3)
    labels = labels.reshape(-1, window * window)
    return jnp.where(labels[:, :, None] != labels[:, None, :], MASK_FILL, 0.0).astype(jnp.float32)


def grads_region(block, grad_block, row_start, col_start, height, width, window, params):
    w_qkv, w_proj, table_logits, logit_scale, gain = params
    images, rows, cols, depth = block.shape
    heads = logit_scale.shape[0]
    head_dim = depth // heads
    tiles = to_windows(block, window)
    grad_tiles = to_windows(grad_block, window)
    count = tiles.shape[1]
    length = window * window
    flat = tiles.reshape(-1, depth)
    qkv = jnp.dot(flat, w_qkv, preferred_element_type=jnp.float32).astype(jnp.bfloat16)
    qkv = qkv.reshape(images, count, length, 3, heads, head_dim)
    query = qkv[:, :, :, 0].astype(jnp.float32)
    keys = qkv[:, :, :, 1].astype(jnp.float32)
    values = qkv[:, :, :, 2]
    query_inv = lax.rsqrt(jnp.sum(query * query, -1, keepdims=True) + 1.0)
    key_inv = lax.rsqrt(jnp.sum(keys * keys, -1, keepdims=True) + 1.0)
    unit_query = query * query_inv
    unit_key = keys * key_inv
    scale = jnp.exp(jnp.minimum(logit_scale, SCALE_CAP))
    onehot = position_onehot(window)
    sigma = jax.nn.sigmoid(table_logits)
    rel_bias = jnp.dot(sigma * BIAS_RANGE, onehot.T, precision=HIGHEST).reshape(
        heads, length, length
    )
    mask = region_mask(row_start, col_start, rows, cols, height, width, window)
    cosine = fine_product("bnqhd,bnkhd->bnhqk", unit_query, unit_key)
    scores = scale[:, None, None] * cosine + rel_bias[None, None] + mask[None, :, None]
    top = jnp.max(scores, -1, keepdims=True)
    expo = jnp.exp(scores - top)
    probs = expo / jnp.sum(expo, -1, keepdims=True)
    probs_low = probs.astype(jnp.bfloat16)
    attended = (
        coarse_product("bnhqk,bnkhd->bnqhd", probs_low, values)
        .astype(jnp.bfloat16)
        .reshape(-1, depth)
    )
    proj = jnp.dot(attended, w_proj, preferred_element_type=jnp.float32)
    centre = proj - jnp.mean(proj, -1, keepdims=True)
    inv_std = lax.rsqrt(jnp.mean(centre * centre, -1, keepdims=True) + EPS_NORM)
    normed = centre * inv_std
    upstream = grad_tiles.reshape(-1, depth).astype(jnp.float32)
    d_gain = jnp.sum(upstream * normed, 0)
    scaled = upstream * gain
    d_proj = inv_std * (
        scaled
        - jnp.mean(scaled, -1, keepdims=True)
        - normed * jnp.mean(scaled * normed, -1, keepdims=True)
    )
    d_proj = d_proj.astype(jnp.bfloat16)
    d_wproj = jnp.dot(attended.T, d_proj, preferred_element_type=jnp.float32)
    d_att = jnp.dot(d_proj, w_proj.T, preferred_element_type=jnp.float32).astype(jnp.bfloat16)
    d_att = d_att.reshape(images, count, length, heads, head_dim)
    d_probs = coarse_product("bnqhd,bnkhd->bnhqk", d_att, values)
    d_values = coarse_product("bnhqk,bnqhd->bnkhd", probs_low, d_att)
    d_scores = probs * (d_probs - jnp.sum(d_probs * probs, -1, keepdims=True))
    d_bias = jnp.sum(d_scores, (0, 1)).reshape(heads, length * length)
    d_table = jnp.dot(d_bias, onehot, precision=HIGHEST) * (BIAS_RANGE * sigma * (1.0 - sigma))
    live = (logit_scale < SCALE_CAP).astype(jnp.float32)
    d_scale = jnp.sum(d_scores * cosine, (0, 1, 3, 4)) * scale * live
    d_cos = d_scores * scale[:, None, None]
    d_unit_q = fine_product("bnhqk,bnkhd->bnqhd", d_cos, unit_key)
    d_unit_k = fine_product("bnhqk,bnqhd->bnkhd", d_cos, unit_query)
    d_query = query_inv * (
        d_unit_q - unit_query * jnp.sum(unit_query * d_unit_q, -1, keepdims=True)
    )
    d_key = key_inv * (d_unit_k - unit_key * jnp.sum(unit_key * d_unit_k, -1, keepdims=True))
    d_qkv = jnp.stack([d_query, d_key, d_values], 3).astype(jnp.bfloat16).reshape(-1, 3 * depth)
    d_wqkv = jnp.dot(flat.T, d_qkv, preferred_element_type=jnp.float32)
    d_flat = jnp.dot(d_qkv, w_qkv.T, preferred_element_type=jnp.float32).astype(jnp.bfloat16)
    d_block = from_windows(d_flat.reshape(images, count, length, depth), images, rows, cols, window)
    return (d_block, (d_wqkv, d_wproj, d_table, d_scale, d_gain))


def shift_in(tokens, cotangent, shift):
    stacked = jnp.stack([tokens, cotangent])
    below = from_behind(stacked[:, :, :shift], "ha", -1)
    tall = jnp.concatenate([stacked[:, :, shift:], below], 2)
    beside = from_behind(tall[:, :, :, :shift], "wa", -1)
    moved = jnp.concatenate([tall[:, :, :, shift:], beside], 3)
    return (moved[0], moved[1])


def shift_out(grads, shift):
    rows = grads.shape[1]
    cols = grads.shape[2]
    right = from_behind(grads[:, :, cols - shift :], "wa", 1)
    wide = jnp.concatenate([right, grads[:, :, : cols - shift]], 2)
    lower = from_behind(wide[:, rows - shift :], "ha", 1)
    return jnp.concatenate([lower, wide[:, : rows - shift]], 1)


def shards(tokens, cotangent, w_qkv, w_proj, table_logits, logit_scale, gain):
    rows = tokens.shape[1]
    cols = tokens.shape[2]
    shift = WIN // 2
    height = rows * lax.axis_size("ha")
    width = cols * lax.axis_size("wa")
    row_base = lax.axis_index("ha") * rows
    col_base = lax.axis_index("wa") * cols
    params = (w_qkv, w_proj, table_logits, logit_scale, gain)
    moved, moved_grad = shift_in(tokens, cotangent, shift)
    d_moved, parts = grads_region(moved, moved_grad, row_base, col_base, height, width, WIN, params)
    back = shift_out(d_moved, shift)
    d_tokens = (cotangent.astype(jnp.float32) + back.astype(jnp.float32)).astype(jnp.bfloat16)
    d_wqkv, d_wproj, d_table, d_scale, d_gain = parts
    half_qkv, half_proj = (
        lax.psum_scatter(d_wqkv.astype(jnp.bfloat16), "ba", scatter_dimension=1, tiled=True).astype(
            jnp.float32
        ),
        lax.psum_scatter(
            d_wproj.astype(jnp.bfloat16), "ba", scatter_dimension=1, tiled=True
        ).astype(jnp.float32),
    )
    half_qkv, half_proj = lax.psum((half_qkv, half_proj), ("ha", "wa"))
    d_table, d_scale, d_gain = lax.psum((d_table, d_scale, d_gain), ("ha", "wa", "ba"))
    return (d_tokens, half_qkv, half_proj, d_table, d_scale, d_gain)


def solution(mesh):
    return jax.shard_map(
        shards,
        mesh=mesh,
        in_specs=(P("ba", "ha", "wa", None), P("ba", "ha", "wa", None), P(), P(), P(), P(), P()),
        out_specs=(P("ba", "ha", "wa", None), P(None, "ba"), P(None, "ba"), P(), P(), P()),
        check_vma=False,
    )
```

profile of v0, /device:TPU:0, one launch (start us, length us, event | category | flops | bytes accessed | tf_op | source)
XLA Modules:
  0.0 213.7 jit_solution(15621993046436900654)
XLA Ops:
  7.2 1.0 pad_maximum_fusion.2
  8.3 4.6 %collective-permute-start = (bf16[2,1,4,32,384]{4,3,2,1,0:T(8,128)(2,1)S(1)}, bf16[2,1,4,32,384]{4,3,2,1,0:T(8,128)(2,1)S(1)}, u32[]{:S(2)}, u32[]{:S(2)}) collective-permute-start(bf16[2,1,4,32,384]{4,3,2,1,0:T(8,128)(2,1)S(1)} %pad_maximum_fusion.2), channel_id=1, source_target_pairs={{4,0},{8,4},{12,8},{16,12},{20,16},{24,20},{28,24},{0,28},{5,1},{9... | collective-permute-start | bytes 589832 | tf_op jit(solution)/shard_map/ppermute | solution.py:21
  12.8 1.1 fusion.52
  15.2 2.0 fusion.2
  18.3 1.6 collective-permute-start.1
  20.2 2.8 %collective-permute-done.1 = bf16[2,1,16,4,384]{4,3,2,1,0:T(4,128)(2,1)S(1)} collective-permute-done((bf16[2,1,16,4,384]{4,3,2,1,0:T(4,128)(2,1)S(1)}, bf16[2,1,16,4,384]{4,3,2,1,0:T(4,128)(2,1)S(1)}, u32[]{:S(2)}, u32[]{:S(2)}) %collective-permute-start.1) | collective-permute-done | bytes 98336 | tf_op jit(solution)/shard_map/ppermute | solution.py:21
  26.1 2.7 %reshape.449 = bf16[1,8,64,3,12,32]{2,1,5,4,3,0:T(8,128)(2,1)} reshape(bf16[512,1152]{0,1:T(8,128)(2,1)S(1)} %copy.82) | data formatting | bytes 2359296 | tf_op jit(solution)/shard_map/reshape | solution.py:82
  28.9 1.8 fusion.67
  31.4 5.2 %fusion.29 = f32[8,12,64,64]{2,3,1,0:T(8,128)S(1)} fusion(f32[8,64,12]{1,2,0:T(8,128)S(1)} %add_rsqrt_fusion.1, f32[8,64,12]{1,2,0:T(8,128)S(1)} %add_rsqrt_fusion, bf16[1,8,64,1,12,32]{2,1,5,4,3,0:T(8,128)(2,1)S(1)} %get-tuple-element.16, bf16[1,8,64,1,12,32]{2,1,5,4,3,0:T(8,128)(2,1)S(1)} %get-tuple-element.17), kind=kOutput, calls=%fused_computation.41 | convolution fusion | flops 151781376 | bytes 2408448 | tf_op jit(solution)/shard_map/bnqhd,bnkhd->bnhqk/dot_general | solution.py:29
  36.6 1.2 fusion.68
  38.9 1.1 copy-done.3
  40.5 1.3 reshape.451
  41.8 1.5 fusion.69
  44.5 2.3 %copy.90 = f32[512,384]{0,1:T(8,128)} copy(f32[512,384]{1,0:T(8,128)} %bitcast.140) | data formatting | bytes 1572864 | tf_op jit(solution)/shard_map/convert_element_type | solution.py:112
  46.8 1.2 fusion.42
  47.9 1.4 multiply_reduce_fusion.2
  49.5 1.4 multiply_convert_fusion
  51.4 1.1 convolution_convert_fusion.5
  52.7 1.3 reshape.452
  54.0 3.7 %multiply_reduce_fusion.1 = (f32[8,12,64]{2,1,0:T(8,128)S(1)}, f32[8,12,64,64]{2,3,1,0:T(8,128)S(1)}) fusion(f32[8,12,64,64]{2,3,1,0:T(8,128)} %copy-done.3, f32[8,12,64]{2,1,0:T(8,128)S(1)} %get-tuple-element.21, bf16[1,8,64,1,12,32]{2,1,5,4,3,0:T(8,128)(2,1)} %copy-done.14, bf16[8,64,12,32]{1,0,3,2:T(8,128)(2,1)} %reshape.452), kind=kOutput, calls=%fused_computation.7 | convolution fusion | flops 26339328 | bytes 3981312 | tf_op jit(solution)/shard_map/bnqhd,bnkhd->bnhqk/dot_general | solution.py:25
  58.3 2.2 %multiply_reduce_fusion = (f32[12]{0:T(128)S(1)}, f32[12,64,64]{1,2,0:T(8,128)}, f32[8,12,64,64]{2,3,1,0:T(8,128)S(1)}) fusion(f32[8,12,64,64]{2,3,1,0:T(8,128)S(1)} %copy-done.2, f32[8,12,64,64]{2,3,1,0:T(8,128)S(1)} %get-tuple-element.26, f32[8,12,64]{2,1,0:T(8,128)S(1)} %get-tuple-element.25, f32[8,12,64,64]{2,3,1,0:T(8,128)S(1)} %copy-done.4, ...), kind=kLoop, calls=%fused_computation.5 | loop fusion | flops 2310132 | bytes 6537264 | tf_op jit(solution)/shard_map/reduce_sum | solution.py:130
  60.4 4.3 %fusion.22 = (f32[8,64,12]{1,2,0:T(8,128)S(1)}, f32[8,12,32,64]{3,2,1,0:T(8,128)}) fusion(f32[8,64,12]{1,2,0:T(8,128)S(1)} %add_rsqrt_fusion.1, bf16[1,8,64,1,12,32]{2,1,5,4,3,0:T(8,128)(2,1)S(1)} %get-tuple-element.17, f32[8,12,64,64]{2,3,1,0:T(8,128)S(1)} %get-tuple-element.15, f32[12]{0:T(128)S(1)} %minimum_exponential_fusion, ...), kind=kOutput, calls=%fused_computation.35 | convolution fusion | flops 152561664 | bytes 3219504 | tf_op jit(solution)/shard_map/bnhqk,bnkhd->bnqhd/dot_general | solution.py:29
  64.7 6.8 %fusion.18 = (f32[8,64,12]{1,2,0:T(8,128)}, f32[8,12,32,64]{3,2,1,0:T(8,128)}) fusion(f32[8,64,12]{1,2,0:T(8,128)S(1)} %add_rsqrt_fusion, bf16[1,8,64,1,12,32]{2,1,5,4,3,0:T(8,128)(2,1)S(1)} %get-tuple-element.16, f32[8,12,64,64]{2,3,1,0:T(8,128)S(1)} %get-tuple-element.15, f32[12]{0:T(128)S(1)} %minimum_exponential_fusion, ...), kind=kOutput, calls=%fused_computation.31 | convolution fusion | flops 152561664 | bytes 3219504 | tf_op jit(solution)/shard_map/bnhqk,bnqhd->bnkhd/dot_general | solution.py:29
  72.8 2.6 %fusion.21 = (bf16[1,8,64,1,12,32]{2,5,4,1,3,0:T(8,128)(2,1)S(1)}, bf16[1,8,64,1,12,32]{2,5,4,1,3,0:T(8,128)(2,1)S(1)}) fusion(f32[8,12,32,64]{3,2,1,0:T(8,128)} %get-tuple-element.28, f32[8,64,12]{1,2,0:T(8,128)} %get-tuple-element.27, f32[8,64,12]{1,2,0:T(8,128)S(1)} %add_rsqrt_fusion, bf16[1,8,64,1,12,32]{2,1,5,4,3,0:T(8,128)(2,1)S(1)} %get-tuple-element.16, ...), kind=kLoop, calls=%fused_computation.34 | loop fusion | flops 2359296 | bytes 3244032 | tf_op jit(solution)/shard_map/stack | solution.py:138
  76.1 2.7 %copy.98 = bf16[1,8,64,3,12,32]{2,1,5,4,3,0:T(8,128)(2,1)S(1)} copy(bf16[1,8,64,3,12,32]{2,5,4,1,3,0:T(8,128)(2,1)S(1)} %maximum_convert_fusion) | data formatting | bytes 2359296 | tf_op jit(solution)/shard_map/convert_element_type | solution.py:138
  78.8 2.4 %convert_element_type.207 = bf16[512,1152]{0,1:T(8,128)(2,1)} reshape(bf16[1,8,64,3,12,32]{2,1,5,4,3,0:T(8,128)(2,1)S(1)} %copy.98) | data formatting | bytes 2359296 | tf_op jit(solution)/shard_map/convert_element_type | solution.py:138
  81.2 3.1 %convolution_convert_fusion.1 = bf16[384,1152]{0,1:T(8,128)(2,1)} fusion(bf16[512,1152]{0,1:T(8,128)(2,1)} %convert_element_type.207, bf16[512,384]{1,0:T(8,128)(2,1)} %bitcast.142), kind=kOutput, calls=%fused_computation.15 | convolution fusion | flops 453427200 | bytes 2457600 | tf_op jit(solution)/shard_map/dot_general | solution.py:139
  86.5 1.6 collective-permute-start.2
  88.1 1.4 fusion.41
  89.6 1.1 collective-permute-done.2
  90.8 39.5 %all-reduce = (f32[12,225]{1,0:T(8,128)}, f32[12]{0:T(128)}, f32[384]{0:T(512)}) all-reduce(f32[12,225]{1,0:T(8,128)S(1)} %fusion.41, f32[12]{0:T(128)S(1)} %compare_select_fusion.1, f32[384]{0:T(512)S(1)} %get-tuple-element.8), channel_id=1, replica_groups=mesh['ha'=8,'wa'=2,'ba'=2] {'ha','wa','ba'}, use_global_device_ids=true, to_apply=%region_16.17 | all-reduce | flops 3096 | bytes 24768 | tf_op jit(solution)/shard_map/psum | solution.py:186
  131.2 75.2 %all-reduce.3 = (f32[384,576]{0,1:T(8,128)}, f32[384,192]{0,1:T(8,128)}) all-reduce(bf16[384,576]{0,1:T(8,128)(2,1)} %reduce-scatter.3.cloned.1.call-done, bf16[384,192]{0,1:T(8,128)(2,1)} %reduce-scatter.5.cloned.1.call-done), channel_id=1, replica_groups=mesh['ha'=8,'wa'=2,'ba'=2] {'ha','wa'}, use_global_device_ids=true, to_apply=%region_12.13 | all-reduce | flops 294912 | bytes 1769472 | tf_op jit(solution)/shard_map/psum | solution.py:185
  (91 shorter events, 15.4 us)
Async XLA Ops:
  7.2 17.5 %copy-start = (bf16[384,1152]{1,0:T(8,128)(2,1)S(1)}, bf16[384,1152]{1,0:T(8,128)(2,1)}, u32[]{:S(2)}) copy-start(bf16[384,1152]{1,0:T(8,128)(2,1)} %param.9) | copy-start | bytes 2654212
  7.2 8.0 %copy-start.17 = (f32[12,225]{1,0:T(8,128)S(1)}, f32[12,225]{1,0:T(8,128)}, u32[]{:S(2)}) copy-start(f32[12,225]{1,0:T(8,128)} %param.11) | copy-start | bytes 32404
  7.2 124.1 %reduce-scatter.5.cloned.1.call-start = ((), (), s32[]{:S(2)}) async-start(), calls=%async_computation.3 | async-start | bytes 442368 | tf_op jit(solution)/shard_map/reduce_scatter | solution.py:181
  8.3 10.0 %collective-permute-start = (bf16[2,1,4,32,384]{4,3,2,1,0:T(8,128)(2,1)S(1)}, bf16[2,1,4,32,384]{4,3,2,1,0:T(8,128)(2,1)S(1)}, u32[]{:S(2)}, u32[]{:S(2)}) collective-permute-start(bf16[2,1,4,32,384]{4,3,2,1,0:T(8,128)(2,1)S(1)} %pad_maximum_fusion.2), channel_id=1, source_target_pairs={{4,0},{8,4},{12,8},{16,12},{20,16},{24,20},{28,24},{0,28},{5,1},{9... | collective-permute-start | bytes 589832 | tf_op jit(solution)/shard_map/ppermute | solution.py:21
  14.0 4.3 %copy-start.18 = (f32[12]{0:T(128)S(1)}, f32[12]{0:T(128)}, u32[]{:S(2)}) copy-start(f32[12]{0:T(128)} %param.12) | copy-start | bytes 148
  18.3 4.7 %collective-permute-start.1 = (bf16[2,1,16,4,384]{4,3,2,1,0:T(4,128)(2,1)S(1)}, bf16[2,1,16,4,384]{4,3,2,1,0:T(4,128)(2,1)S(1)}, u32[]{:S(2)}, u32[]{:S(2)}) collective-permute-start(bf16[2,1,16,4,384]{4,3,2,1,0:T(4,128)(2,1)S(1)} %pad_maximum_fusion.4), channel_id=1, source_target_pairs={{2,0},{0,2},{3,1},{1,3},{6,4},{4,6},{7,5},{5,7},{10,8},{8,10},{11,... | collective-permute-start | bytes 294920 | tf_op jit(solution)/shard_map/ppermute | solution.py:21
  24.0 0.7 copy-start.9
  30.7 7.7 %copy-start.14 = (bf16[1,8,64,1,12,32]{2,1,5,4,3,0:T(8,128)(2,1)}, bf16[1,8,64,1,12,32]{2,1,5,4,3,0:T(8,128)(2,1)S(1)}, u32[]{:S(2)}) copy-start(bf16[1,8,64,1,12,32]{2,1,5,4,3,0:T(8,128)(2,1)S(1)} %get-tuple-element.18) | copy-start | bytes 1179652
  31.4 5.2 %copy-start.10 = (f32[12,64,64]{1,2,0:T(8,128)S(1)}, f32[12,64,64]{1,2,0:T(8,128)}, u32[]{:S(2)}) copy-start(f32[12,64,64]{1,2,0:T(8,128)} %copy.85) | copy-start | bytes 589828
  31.4 5.2 %copy-start.13 = (f32[8,64,64]{1,2,0:T(8,128)S(1)}, f32[8,64,64]{1,2,0:T(8,128)}, u32[]{:S(2)}) copy-start(f32[8,64,64]{1,2,0:T(8,128)} %compare_select_fusion) | copy-start | bytes 393220
  36.6 1.7 copy-start.1
  38.3 1.7 copy-start.3
  41.8 1.7 copy-start.6
  43.6 3.2 %copy-start.16 = (f32[384]{0:T(512)S(1)}, f32[384]{0:T(512)}, u32[]{:S(2)}) copy-start(f32[384]{0:T(512)} %param.13) | copy-start | bytes 4612
  49.5 1.4 copy-start.12
  49.5 1.9 copy-start.5
  54.0 3.7 %copy-start.2 = (f32[8,12,64,64]{2,3,1,0:T(8,128)S(1)}, f32[8,12,64,64]{2,3,1,0:T(8,128)}, u32[]{:S(2)}) copy-start(f32[8,12,64,64]{2,3,1,0:T(8,128)} %copy-done.1) | copy-start | bytes 4718596
  54.0 4.3 %copy-start.4 = (f32[8,12,64,64]{2,3,1,0:T(8,128)S(1)}, f32[8,12,64,64]{2,3,1,0:T(8,128)}, u32[]{:S(2)}) copy-start(f32[8,12,64,64]{2,3,1,0:T(8,128)} %copy-done.3) | copy-start | bytes 4718596
  64.7 6.8 %copy-start.15 = (bf16[8,64,12,32]{1,0,3,2:T(8,128)(2,1)S(1)}, bf16[8,64,12,32]{1,0,3,2:T(8,128)(2,1)}, u32[]{:S(2)}) copy-start(bf16[8,64,12,32]{1,0,3,2:T(8,128)(2,1)} %reshape.452) | copy-start | bytes 1179652
  72.5 58.7 %reduce-scatter.3.cloned.1.call-start = ((), (), s32[]{:S(2)}) async-start(), calls=%async_computation.2 | async-start | bytes 1327104 | tf_op jit(solution)/shard_map/reduce_scatter | solution.py:178
  81.2 3.1 %copy-start.8 = (f32[12,64,64]{1,2,0:T(8,128)S(1)}, f32[12,64,64]{1,2,0:T(8,128)}, u32[]{:S(2)}) copy-start(f32[12,64,64]{1,2,0:T(8,128)} %get-tuple-element.7) | copy-start | bytes 589828
  84.3 1.3 copy-start.11
  86.4 43.9 %copy-start.7 = (bf16[1,16,32,384]{3,2,1,0:T(8,128)(2,1)S(1)}, bf16[1,16,32,384]{3,2,1,0:T(8,128)(2,1)}, u32[]{:S(2)}) copy-start(bf16[1,16,32,384]{3,2,1,0:T(8,128)(2,1)} %param.8) | copy-start | bytes 1179652
  86.5 4.2 %collective-permute-start.2 = (bf16[1,16,4,384]{3,2,1,0:T(4,128)(2,1)S(1)}, bf16[1,16,4,384]{3,2,1,0:T(4,128)(2,1)S(1)}, u32[]{:S(2)}, u32[]{:S(2)}) collective-permute-start(bf16[1,16,4,384]{3,2,1,0:T(4,128)(2,1)S(1)} %slice.61), channel_id=1, source_target_pairs={{2,0},{0,2},{3,1},{1,3},{6,4},{4,6},{7,5},{5,7},{10,8},{8,10},{11,... | collective-permute-start | bytes 147464 | tf_op jit(solution)/shard_map/ppermute | solution.py:21
  90.7 39.6 %collective-permute-start.3 = (bf16[1,4,32,384]{3,2,1,0:T(8,128)(2,1)S(1)}, bf16[1,4,32,384]{3,2,1,0:T(8,128)(2,1)S(1)}, u32[]{:S(2)}, u32[]{:S(2)}) collective-permute-start(bf16[1,4,32,384]{3,2,1,0:T(8,128)(2,1)S(1)} %pad_maximum_fusion.3), channel_id=1, source_target_pairs={{28,0},{0,4},{4,8},{8,12},{12,16},{16,20},{20,24},{24,28},{29,1},{... | collective-permute-start | bytes 294920 | tf_op jit(solution)/shard_map/ppermute | solution.py:21
Sparse Core Ops, SparseCore 0:
  72.7 11.1 reduce-scatter.4
  86.7 19.1 reduce-scatter.2
where the time goes:
time: 218 us; the launch traced here: 214 us
  blocking collectives  115 us (53%)
  matrix products  32.8 us (15%)
  local copies, waits for them, and re-layouts  22.4 us (10%)
  other arithmetic  16.8 us (8%)
  between operations  14.9 us (7%)
  starting transfers between devices  8.14 us (4%)
  waiting for transfers between devices  4.01 us (2%)
    psum x1, blocking collectives, shards(): half_qkv, half_proj = lax.psum((half_qkv, half_proj), ('ha', 'wa'))  75.2 us
    psum x1, blocking collectives, shards(): lax.psum((d_table, d_scale, d_gain), ('ha', 'wa', 'ba'))  39.5 us
    dot_general x3, matrix products, fine_product(): return jnp.einsum(form, left, right, precision=HIGHEST)  16.3 us
    ppermute x4, starting transfers between devices, from_behind(): return lax.ppermute(block, axis, route)  7.81 us
    dot_general x3, matrix products, coarse_product(): return jnp.einsum(form, left, right, preferred_element_type=jnp.float32)  5.15 us
    convert_element_type x2, local copies, waits for them, and re-layouts, grads_region(): jnp.stack([d_query, d_key, d_values], 3).astype(jnp.bfloat16)  5.15 us
  transfers between devices with their start and end apart: 6, of which 2 were waited for; matrix products, arithmetic and copies ran while one was open for 10% of the time, Pallas kernels for 0%

commit v1 on v0

v1 whole, which is shorter than its diff:
```python
import math

import jax
import jax.numpy as jnp
from jax import lax
from jax.experimental import pallas as pl
from jax.experimental.pallas import tpu as pltpu
from jax.sharding import Mesh
from jax.sharding import PartitionSpec as P

WIN = 8
TOKENS = WIN * WIN
LANES = 128
EPS_NORM = 1e-05
MASK_FILL = -100.0
SCALE_CAP = math.log(100.0)
BIAS_RANGE = 16.0
F32 = jnp.float32
BF16 = jnp.bfloat16


def dot_nn(left, right):
    return lax.dot_general(left, right, (((1,), (0,)), ((), ())), preferred_element_type=F32)


def dot_nt(left, right):
    return lax.dot_general(left, right, (((1,), (1,)), ((), ())), preferred_element_type=F32)


def dot_tn(left, right):
    return lax.dot_general(left, right, (((0,), (0,)), ((), ())), preferred_element_type=F32)


def iota(shape, dim):
    return lax.broadcasted_iota(jnp.int32, shape, dim)


def split(value):
    high = value.astype(BF16)
    return high, (value - high.astype(F32)).astype(BF16)


def group_sum(value, ones):
    high, low = split(value)
    width = ones.shape[0]
    parts = []
    for start in range(0, value.shape[1], width):
        part = slice(start, start + width)
        parts.append(dot_nn(high[:, part], ones) + dot_nn(low[:, part], ones))
    return jnp.concatenate(parts, axis=1)


def make_kernel(rows, cols, depth, heads):
    head_dim = depth // heads
    per_tile = LANES // head_dim
    groups = heads // per_tile
    col_windows = cols // WIN
    row_windows = rows // WIN
    pairs = row_windows * col_windows // 2
    pairs_across = col_windows // 2
    stacked = per_tile * TOKENS
    small_at = 6 * depth

    def kernel(
        flags,
        img,
        w_qkv,
        w_proj,
        table_a,
        table_b,
        gain,
        scale,
        d_img,
        grads,
        xf,
        uf,
        xb,
        qk_raw,
        inv,
        q_hi,
        q_lo,
        k_hi,
        k_lo,
        val,
        prob,
        raw,
        att,
        d_prj,
        d_att,
        d_qkv,
        d_unit,
        bias,
        d_bias,
        d_sc,
        d_gn,
        small,
    ):
        half = iota((1, LANES), 1) < TOKENS
        for i in range(rows):
            for j in range(col_windows):
                at = (i // WIN * col_windows + j) * TOKENS + i % WIN * WIN
                xf[at : at + WIN, :] = img[0, i, j * WIN : (j + 1) * WIN, :].astype(F32)
                uf[at : at + WIN, :] = img[1, i, j * WIN : (j + 1) * WIN, :].astype(F32)
        sub = iota((WIN, LANES), 0)
        lane = iota((WIN, LANES), 1)
        for h in range(heads):
            near = jnp.broadcast_to(table_a[h : h + 1, :], (WIN, LANES))
            far = jnp.broadcast_to(table_b[h : h + 1, :], (WIN, LANES))
            near = pltpu.roll(near, LANES - WIN + 1, 1, stride=1, stride_axis=0)
            far = pltpu.roll(far, 1, 1, stride=1, stride_axis=0)
            line = jnp.where(lane % WIN <= sub, near, far)
            for r in range(WIN):
                first = pltpu.roll(line, (LANES - (WIN - 1 - r) * WIN) % LANES, 1)
                second = pltpu.roll(line, (LANES + TOKENS - (WIN - 1 - r) * WIN) % LANES, 1)
                at = h * TOKENS + r * WIN
                bias[at : at + WIN, :] = jnp.where(half, first, second)
        d_bias[...] = jnp.zeros_like(d_bias)
        d_sc[...] = jnp.zeros_like(d_sc)
        d_gn[...] = jnp.zeros_like(d_gn)

        wide = 2 * LANES
        ones = (iota((wide, wide), 0) // head_dim == iota((wide, wide), 1) // head_dim).astype(F32)
        ones = ones.astype(BF16)
        owner = iota((1, wide), 1) % LANES // head_dim
        head_f32 = [(owner == h).astype(F32) for h in range(per_tile)]
        head_low = [m.astype(BF16) for m in head_f32]
        top_rows = (iota((2 * TOKENS, LANES), 0) < TOKENS).astype(F32)
        top_rows, low_rows = top_rows.astype(BF16), (1.0 - top_rows).astype(BF16)

        key = iota((TOKENS, LANES), 0)
        query = iota((TOKENS, LANES), 1) % TOKENS
        edge = WIN // 2
        split_r = ((key // WIN) >= edge) != ((query // WIN) >= edge)
        split_c = ((key % WIN) >= edge) != ((query % WIN) >= edge)
        split_c = jnp.logical_and(split_c, iota((TOKENS, LANES), 1) >= TOKENS)
        mask_r = jnp.where(split_r, MASK_FILL, 0.0)
        mask_c = jnp.where(split_c, MASK_FILL, 0.0)

        def beside(ref, at, tile):
            one = ref[pl.ds(at, TOKENS), tile]
            two = ref[pl.ds(at + TOKENS, TOKENS), tile]
            return jnp.concatenate([one, two], axis=1)

        def stack(block):
            return jnp.concatenate([block * head_low[h] for h in range(per_tile)], axis=0)

        def diagonal(ref, at, tile):
            block = ref[pl.ds(at, 2 * TOKENS), tile]
            return jnp.concatenate([block * top_rows, block * low_rows], axis=1)

        def gather_heads(out):
            total = out[:TOKENS] * head_f32[0]
            for h in range(1, per_tile):
                total = total + out[h * TOKENS : (h + 1) * TOKENS] * head_f32[h]
            return total

        def forward(p, carry):
            at = pl.multiple_of(p * 2 * TOKENS, 2 * TOKENS)
            span = pl.ds(at, 2 * TOKENS)
            x = xf[span, :].astype(BF16)
            xb[span, :] = x
            qkv = dot_nn(x, w_qkv[...]).astype(BF16)
            val[span, :] = qkv[:, 2 * depth :]
            both = qkv[:, : 2 * depth].astype(F32)
            root = lax.rsqrt(group_sum(both * both, ones) + 1.0)
            unit = both * root
            qk_raw[span, :] = unit
            inv[span, :] = root
            high, low = split(unit[:, :depth] * scale[...])
            q_hi[span, :] = high
            q_lo[span, :] = low
            high, low = split(unit[:, depth:])
            k_hi[span, :] = high
            k_lo[span, :] = low
            row_edge = jnp.where(p // pairs_across == row_windows - 1, flags[0], 0)
            col_edge = jnp.where(p % pairs_across == pairs_across - 1, flags[1], 0)
            mask = jnp.minimum(mask_r * row_edge.astype(F32), mask_c * col_edge.astype(F32))
            for g in range(groups):
                tile = slice(g * LANES, (g + 1) * LANES)
                keys = stack(beside(k_hi, at, tile))
                keys_low = stack(beside(k_lo, at, tile))
                queries = diagonal(q_hi, at, tile)
                score = dot_nt(keys, queries) + (
                    dot_nt(keys_low, queries) + dot_nt(keys, diagonal(q_lo, at, tile))
                )
                raw[p, g] = score
                lows = []
                for h in range(per_tile):
                    place = slice(h * TOKENS, (h + 1) * TOKENS)
                    of = (g * per_tile + h) * TOKENS
                    s = score[place] + bias[of : of + TOKENS, :] + mask
                    e = jnp.exp(s - jnp.max(s, axis=0, keepdims=True))
                    pr = e * (1.0 / jnp.sum(e, axis=0, keepdims=True))
                    prob[p, g, place, :] = pr
                    lows.append(pr.astype(BF16))
                out = dot_tn(jnp.concatenate(lows, axis=0), stack(beside(val, at, tile)))
                att[pl.ds(at, TOKENS), tile] = out[:TOKENS, :LANES].astype(BF16)
                att[pl.ds(at + TOKENS, TOKENS), tile] = out[TOKENS:, LANES:].astype(BF16)
            proj = dot_nn(att[span, :], w_proj[...])
            centre = proj - jnp.mean(proj, -1, keepdims=True)
            std = lax.rsqrt(jnp.mean(centre * centre, -1, keepdims=True) + EPS_NORM)
            normed = centre * std
            up = uf[span, :]
            prod = up * normed
            d_gn[...] += jnp.sum(prod, axis=0, keepdims=True)
            u = up * gain[...]
            d_p = std * (
                u - jnp.mean(u, -1, keepdims=True) - normed * jnp.mean(u * normed, -1, keepdims=True)
            )
            d_p = d_p.astype(BF16)
            d_prj[span, :] = d_p
            d_att[span, :] = dot_nt(d_p, w_proj[...]).astype(BF16)
            return carry

        lax.fori_loop(0, pairs, forward, 0)

        def backward(p, carry):
            at = pl.multiple_of(p * 2 * TOKENS, 2 * TOKENS)
            span = pl.ds(at, 2 * TOKENS)
            for g in range(groups):
                tile = slice(g * LANES, (g + 1) * LANES)
                key_tile = slice(depth + g * LANES, depth + (g + 1) * LANES)
                val_tile = slice(2 * depth + g * LANES, 2 * depth + (g + 1) * LANES)
                values = stack(beside(val, at, tile))
                ups = diagonal(d_att, at, tile)
                d_pr = dot_nt(values, ups)
                lows, d_lows = [], []
                for h in range(per_tile):
                    place = slice(h * TOKENS, (h + 1) * TOKENS)
                    of = (g * per_tile + h) * TOKENS
                    pr = prob[p, g, place, :]
                    pd = pr * d_pr[place]
                    d_s = pd - pr * jnp.sum(pd, axis=0, keepdims=True)
                    d_bias[of : of + TOKENS, :] += d_s
                    by_scale = jnp.sum(d_s * raw[p, g, place, :], axis=0, keepdims=True)
                    head = g * per_tile + h
                    d_sc[head : head + 1, :] += by_scale
                    lows.append(pr.astype(BF16))
                    d_lows.append(d_s.astype(BF16))
                low = jnp.concatenate(lows, axis=0)
                d_low = jnp.concatenate(d_lows, axis=0)
                d_v = gather_heads(dot_nn(low, ups)).astype(BF16)
                d_qkv[pl.ds(at, TOKENS), val_tile] = d_v[:, :LANES]
                d_qkv[pl.ds(at + TOKENS, TOKENS), val_tile] = d_v[:, LANES:]
                d_k = gather_heads(dot_nn(d_low, diagonal(q_hi, at, tile)))
                d_unit[:TOKENS, key_tile] = d_k[:, :LANES]
                d_unit[TOKENS:, key_tile] = d_k[:, LANES:]
                d_q = dot_tn(d_low, stack(beside(k_hi, at, tile)))
                d_unit[:TOKENS, tile] = d_q[:TOKENS, :LANES] * scale[:, tile]
                d_unit[TOKENS:, tile] = d_q[TOKENS:, LANES:] * scale[:, tile]
            unit = qk_raw[span, :]
            d_u = d_unit[...]
            d_qk = inv[span, :] * (d_u - unit * group_sum(unit * d_u, ones))
            d_qkv[span, : 2 * depth] = d_qk.astype(BF16)
            flat = dot_nt(d_qkv[span, :], w_qkv[...])
            row_at = p // pairs_across * WIN
            for w in range(2):
                col_at = pl.multiple_of((p % pairs_across * 2 + w) * WIN, WIN)
                for r in range(WIN):
                    piece = flat[w * TOKENS + r * WIN : w * TOKENS + (r + 1) * WIN]
                    d_img[row_at + r, pl.ds(col_at, WIN), :] = piece.astype(BF16)
            return carry

        lax.fori_loop(0, pairs, backward, 0)

        d_wp = dot_tn(att[...], d_prj[...])
        d_wq = dot_tn(xb[...], d_qkv[...])
        side = 9 * LANES // 2
        full = side // LANES
        turned = pltpu.roll(d_wp[:, LANES : 2 * LANES], TOKENS, 1)
        middle = d_wq[:, full * LANES : (full + 1) * LANES]
        for j in range(full):
            place = slice(j * depth, (j + 1) * depth)
            grads[0, place, :] = d_wq[:, j * LANES : (j + 1) * LANES].astype(BF16)
            other = full + 1 + j
            grads[1, place, :] = d_wq[:, other * LANES : (other + 1) * LANES].astype(BF16)
        place = slice(full * depth, (full + 1) * depth)
        grads[0, place, :] = jnp.where(half, middle, turned).astype(BF16)
        grads[1, place, :] = jnp.where(half, turned, middle).astype(BF16)
        place = slice((full + 1) * depth, (full + 2) * depth)
        grads[0, place, :] = d_wp[:, :LANES].astype(BF16)
        grads[1, place, :] = d_wp[:, 2 * LANES :].astype(BF16)

        small[...] = jnp.zeros_like(small)
        for h in range(heads):
            line = jnp.zeros((WIN, LANES), F32)
            for r in range(WIN):
                at = h * TOKENS + r * WIN
                part = d_bias[at : at + WIN, :]
                part = jnp.where(half, part + pltpu.roll(part, TOKENS, 1), 0.0)
                line = line + pltpu.roll(part, (WIN - 1 - r) * WIN, 1)
            near, far = jnp.zeros_like(line), jnp.zeros_like(line)
            for c in range(WIN):
                own = jnp.where(sub == c, line, 0.0)
                near = near + pltpu.roll(own, WIN - 1 - c, 1)
                far = far + pltpu.roll(own, LANES - 1 - c, 1)
            near = jnp.where(lane % WIN >= WIN - 1 - sub, near, 0.0)
            far = jnp.where(lane % WIN + sub + 1 <= WIN - 1, far, 0.0)
            small[h : h + 1, :] = jnp.sum(near, axis=0, keepdims=True)
            small[heads + h : heads + h + 1, :] = jnp.sum(far, axis=0, keepdims=True)
        for j in range(groups):
            small[2 * heads + j : 2 * heads + j + 1, :] = d_gn[:, j * LANES : (j + 1) * LANES]
        sums = jnp.zeros((1, LANES), F32)
        for h in range(heads):
            total = jnp.sum(d_sc[h : h + 1, :], axis=1, keepdims=True)
            sums = sums + jnp.where(iota((1, LANES), 1) == h, total, 0.0)
        at = 2 * heads + groups
        small[at : at + 1, :] = sums
        grads[0, small_at:, :] = small[...].astype(BF16)
        grads[1, small_at:, :] = small[...].astype(BF16)

    tokens = rows * cols

    def call(flags, img, w_qkv, w_proj, table_a, table_b, gain, scale, sent_rows):
        vmem = pltpu.VMEM
        scratch = [
            vmem((tokens, depth), F32),
            vmem((tokens, depth), F32),
            vmem((tokens, depth), BF16),
            vmem((tokens, 2 * depth), F32),
            vmem((tokens, 2 * depth), F32),
            vmem((tokens, depth), BF16),
            vmem((tokens, depth), BF16),
            vmem((tokens, depth), BF16),
            vmem((tokens, depth), BF16),
            vmem((tokens, depth), BF16),
            vmem((pairs, groups, stacked, LANES), F32),
            vmem((pairs, groups, stacked, LANES), F32),
            vmem((tokens, depth), BF16),
            vmem((tokens, depth), BF16),
            vmem((tokens, depth), BF16),
            vmem((tokens, 3 * depth), BF16),
            vmem((2 * TOKENS, 2 * depth), F32),
            vmem((heads * TOKENS, LANES), F32),
            vmem((heads * TOKENS, LANES), F32),
            vmem((16, LANES), F32),
            vmem((1, depth), F32),
            vmem((sent_rows - small_at, LANES), F32),
        ]
        return pl.pallas_call(
            kernel,
            out_shape=(
                jax.ShapeDtypeStruct((rows, cols, depth), BF16),
                jax.ShapeDtypeStruct((2, sent_rows, LANES), BF16),
            ),
            in_specs=[pl.BlockSpec(memory_space=pltpu.SMEM)]
            + [pl.BlockSpec(memory_space=pltpu.VMEM)] * 7,
            out_specs=(
                pl.BlockSpec(memory_space=pltpu.VMEM),
                pl.BlockSpec(memory_space=pltpu.VMEM),
            ),
            scratch_shapes=scratch,
            name="block_grads",
        )(flags, img, w_qkv, w_proj, table_a, table_b, gain, scale)

    return call


def route(axes, move):
    sizes = [lax.axis_size(a) for a in axes]
    pairs = []
    for flat in range(math.prod(sizes)):
        left, where = flat, []
        for size in reversed(sizes):
            where.append(left % size)
            left //= size
        where = move(where[::-1], sizes)
        target = 0
        for place, size in zip(where, sizes):
            target = target * size + place
        pairs.append((flat, target))
    return pairs


GRID = ("hz", "hc", "wa")


def step(rows, cols):
    def move(where, sizes):
        high = (where[0] * sizes[1] + where[1] + rows) % (sizes[0] * sizes[1])
        return [high // sizes[1], high % sizes[1], (where[2] + cols) % sizes[2]]

    return move


def shards(tokens, cotangent, w_qkv, w_proj, table_logits, logit_scale, gain):
    images, rows, cols, depth = tokens.shape
    heads = logit_scale.shape[0]
    span = 2 * WIN - 1
    edge = WIN // 2
    both = jnp.concatenate([tokens, cotangent], 0)
    below = lax.ppermute(both[:, :edge], GRID, route(GRID, step(-1, 0)))
    beside = lax.ppermute(both[:, :, :edge], GRID, route(GRID, step(0, -1)))
    corner = lax.ppermute(both[:, :edge, :edge], GRID, route(GRID, step(-1, -1)))
    main = jnp.concatenate([both[:, edge:, edge:], beside[:, edge:]], 2)
    last = jnp.concatenate([below[:, :, edge:], corner], 2)
    moved = jnp.concatenate([main, last], 1)

    ha = lax.axis_index("hz") * lax.axis_size("hc") + lax.axis_index("hc")
    flags = jnp.stack(
        [
            (ha == lax.axis_size("hz") * lax.axis_size("hc") - 1).astype(jnp.int32),
            (lax.axis_index("wa") == lax.axis_size("wa") - 1).astype(jnp.int32),
        ]
    )
    scale = jnp.exp(jnp.minimum(logit_scale, SCALE_CAP))
    scale = jnp.repeat(scale, depth // heads)[None]
    sigma = jax.nn.sigmoid(table_logits)
    table = (sigma * BIAS_RANGE).reshape(heads, span, span)
    table_a = table[:, :, :WIN].reshape(heads, span * WIN)
    table_b = jnp.pad(table[:, :, WIN:], ((0, 0), (0, 0), (0, 1))).reshape(heads, span * WIN)
    fill = ((0, 0), (0, LANES - span * WIN))
    table_a, table_b = jnp.pad(table_a, fill), jnp.pad(table_b, fill)

    cores, tall, across = lax.axis_size("hc"), lax.axis_size("hz"), lax.axis_size("wa")
    owners = cores * tall * across
    body = 6 * depth
    used = body + 2 * heads + depth // LANES + 1
    unit = 8 * owners
    sent = -(-used // unit) * unit
    call = make_kernel(rows, cols, depth, heads)
    d_moved, grads = call(
        flags, moved, w_qkv, w_proj, table_a, table_b, gain[None], scale, sent
    )

    right = lax.ppermute(d_moved[: rows - edge, cols - edge :], GRID, route(GRID, step(0, 1)))
    lower = lax.ppermute(d_moved[rows - edge :, : cols - edge], GRID, route(GRID, step(1, 0)))
    cross = lax.ppermute(
        d_moved[rows - edge :, cols - edge :], GRID, route(GRID, step(1, 1))
    )
    upper = jnp.concatenate([cross, lower], 1)
    main = jnp.concatenate([right, d_moved[: rows - edge, : cols - edge]], 1)
    back = jnp.concatenate([upper, main], 0)[None]
    d_tokens = (cotangent.astype(F32) + back.astype(F32)).astype(BF16)

    core = lax.axis_index("hc")
    grads = grads.reshape(2, cores, sent // cores, LANES)
    mine = lax.dynamic_index_in_dim(grads, core, 1, keepdims=False)
    given = lax.dynamic_index_in_dim(grads, 1 - core, 1, keepdims=False)
    swap = route(("hc",), lambda where, sizes: [1 - where[0]])
    taken = lax.ppermute(given, "hc", swap)
    summed = (mine.astype(F32) + taken.astype(F32)).astype(BF16)
    piece = sent // owners
    summed = summed.reshape(2 * tall * across, piece, LANES)
    parts = lax.all_to_all(summed, ("ba", "hz", "wa"), 0, 0, tiled=True)
    total = parts.astype(F32).sum(0).astype(BF16)
    spread = jnp.broadcast_to(total[None], (tall * across, piece, LANES))
    ours = lax.all_to_all(spread, ("hz", "wa"), 0, 0, tiled=True)
    ours = ours.reshape(sent // cores, LANES)
    theirs = lax.ppermute(ours, "hc", swap)
    first = jnp.where(core == 0, ours, theirs)
    second = jnp.where(core == 0, theirs, ours)
    whole = jnp.concatenate([first, second], 0).astype(F32)
    tiles = [whole[j * depth : (j + 1) * depth] for j in range(6)]
    mid = tiles[4]
    low, high = mid[:, :TOKENS], mid[:, TOKENS:]
    image = lax.axis_index("ba")
    d_wqkv = jnp.where(
        image == 0,
        jnp.concatenate(tiles[:4] + [low], 1),
        jnp.concatenate([high] + tiles[:4], 1),
    )
    d_wproj = jnp.where(
        image == 0,
        jnp.concatenate([tiles[5], high], 1),
        jnp.concatenate([low, tiles[5]], 1),
    )
    small = whole[body:]
    near = small[:heads, : span * WIN].reshape(heads, span, WIN)
    far = small[heads : 2 * heads, : span * WIN].reshape(heads, span, WIN)
    d_table = jnp.concatenate([near, far[:, :, : WIN - 1]], 2).reshape(heads, span * span)
    d_table = d_table * (BIAS_RANGE * sigma * (1.0 - sigma))
    d_gain = small[2 * heads : 2 * heads + depth // LANES].reshape(depth)
    d_scale = small[2 * heads + depth // LANES, :heads]
    d_scale = jnp.where(logit_scale < SCALE_CAP, d_scale, 0.0)
    return (d_tokens, d_wqkv, d_wproj, d_table, d_scale, d_gain)


def solution(mesh):
    sizes = mesh.shape
    devices = mesh.devices.reshape(sizes["ha"] // 2, 2, sizes["wa"], sizes["ba"])
    inner = Mesh(devices, ("hz", "hc", "wa", "ba"))
    image = P("ba", ("hz", "hc"), "wa", None)
    return jax.shard_map(
        shards,
        mesh=inner,
        in_specs=(image, image, P(), P(), P(), P(), P()),
        out_specs=(image, P(None, "ba"), P(None, "ba"), P(), P(), P()),
        check_vma=False,
    )
```

time: 218 us -> 87.6 us (0.40); the launches traced: 214 us -> 87.3 us
  blocking collectives: 115 us -> 24.9 us
  matrix products: 32.8 us -> 0 us
  Pallas kernels: 0 us -> 21.8 us
  between operations: 14.9 us -> 0.98 us
  other arithmetic: 16.8 us -> 5.12 us
  local copies, waits for them, and re-layouts: 22.4 us -> 11.2 us
  starting transfers between devices: 8.14 us -> 13.9 us
  waiting for transfers between devices: 4.01 us -> 9.27 us
    psum x2 -> x0, blocking collectives: 115 us -> none  [the longest x1 75.2 us: shards(): half_qkv, half_proj = lax.psum((half_qkv, half_proj), ('ha', 'wa'))]
    dot_general x14 -> x0, matrix products: 32.8 us -> none  [the longest x3 16.3 us: fine_product(): return jnp.einsum(form, left, right, precision=HIGHEST)]
    all_to_all x0 -> x1, blocking collectives: none -> 24.9 us  [shards(): parts = lax.all_to_all(summed, ('ba', 'hz', 'wa'), 0, 0, tiled=True)]
    pallas_call x0 -> x1, Pallas kernels: none -> 21.8 us  [call(): pl.pallas_call(kernel, out_shape=(jax.ShapeDtypeStruct((rows, cols, depth...]
    convert_element_type x7 -> x0, local copies, waits for them, and re-layouts: 9.67 us -> none  [the longest x2 5.15 us: grads_region(): jnp.stack([d_query, d_key, d_values], 3).astype(jnp.bfloat16)]
    all_to_all x0 -> x1, waiting for transfers between devices: none -> 5.69 us  [shards(): ours = lax.all_to_all(spread, ('hz', 'wa'), 0, 0, tiled=True)]
    reduce_sum x6 -> x1, other arithmetic: 5.54 us -> 0.09 us  [shards(): total = parts.astype(F32).sum(0).astype(BF16)]
    another operation x3 -> x1, other arithmetic: 4.77 us -> 0.61 us  [shards(): jnp.stack([(ha == lax.axis_size('hz') * lax.axis_size('hc') - 1).astype(j...]
  transfers between devices with their start and end apart: 6 -> 9, of which waited for: 2 -> 4; matrix products, arithmetic and copies ran while one was open for 10% -> 6% of each run, Pallas kernels for 0% -> 0%
where the time goes in v1:
time: 87.6 us; the launch traced here: 87.3 us
  blocking collectives  24.9 us (28%)
  Pallas kernels  21.8 us (25%)
  starting transfers between devices  13.9 us (16%)
  local copies, waits for them, and re-layouts  11.2 us (13%)
  waiting for transfers between devices  9.27 us (11%)
  other arithmetic  5.12 us (6%)
  between operations  0.98 us (1%)
    all_to_all x1, blocking collectives, shards(): parts = lax.all_to_all(summed, ('ba', 'hz', 'wa'), 0, 0, tiled=True)  24.9 us
    pallas_call x1, Pallas kernels, call(): pl.pallas_call(kernel, out_shape=(jax.ShapeDtypeStruct((rows, cols, depth...  21.8 us
    all_to_all x1, waiting for transfers between devices, shards(): ours = lax.all_to_all(spread, ('hz', 'wa'), 0, 0, tiled=True)  5.69 us
    ppermute x1, starting transfers between devices, shards(): lax.ppermute(both[:, :edge, :edge], GRID, route(GRID, step(-1, -1)))  5.53 us
    all_to_all x1, starting transfers between devices, shards(): ours = lax.all_to_all(spread, ('hz', 'wa'), 0, 0, tiled=True)  3.56 us
    unnamed x22, local copies, waits for them, and re-layouts  3.23 us
    ppermute x1, waiting for transfers between devices, shards(): taken = lax.ppermute(given, 'hc', swap)  2.04 us
    ppermute x1, starting transfers between devices, shards(): lax.ppermute(d_moved[:rows - edge, cols - edge:], GRID, route(GRID, step(...  1.97 us
  transfers between devices with their start and end apart: 9, of which 4 were waited for; matrix products, arithmetic and copies ran while one was open for 6% of the time, Pallas kernels for 0%

profile of v1, /device:TPU:0, one launch (start us, length us, event | category | flops | bytes accessed | tf_op | source)
XLA Modules:
  0.0 87.3 jit_solution(18368379119089466901)
XLA Ops:
  0.7 1.0 %constant_dynamic-update-slice_fusion.1 = bf16[2,16,32,384]{3,2,1,0:T(8,128)(2,1)S(1)} fusion(bf16[1,16,32,384]{3,2,1,0:T(8,128)(2,1)} %param.7), kind=kLoop, calls=%fused_computation.14 | loop fusion | bytes 786432
  1.7 1.1 %constant_dynamic-update-slice_fusion = bf16[2,16,32,384]{3,2,1,0:T(8,128)(2,1)S(1)} fusion(bf16[2,16,32,384]{3,2,1,0:T(8,128)(2,1)S(1)} %constant_dynamic-update-slice_fusion.1, bf16[1,16,32,384]{3,2,1,0:T(8,128)(2,1)} %param.8), kind=kLoop, calls=%fused_computation.13 | loop fusion | bytes 786432 | tf_op jit(solution)/shard_map/concatenate | solution.py:391
  2.8 5.5 %collective-permute-start.2 = (bf16[2,4,4,384]{3,2,1,0:T(4,128)(2,1)S(1)}, bf16[2,4,4,384]{3,2,1,0:T(4,128)(2,1)S(1)}, u32[]{:S(2)}, u32[]{:S(2)}) collective-permute-start(bf16[2,4,4,384]{3,2,1,0:T(4,128)(2,1)S(1)} %slice.109), channel_id=1, source_target_pairs={{0,30},{2,28},{4,2},{6,0},{8,6},{10,4},{12,10},{14,8},{16,14},{18,... | collective-permute-start | bytes 73736 | tf_op jit(solution)/shard_map/ppermute | solution.py:394
  8.4 0.6 collective-permute-start
  9.0 0.6 collective-permute-start.1
  9.6 0.6 add_convert_fusion.1.flags
  10.2 0.2 slice.104
  10.4 0.6 broadcast_in_dim.17.gain
  11.1 0.7 broadcast_in_dim_reshape.3.scale
  12.0 0.6 pad.11.table_a
  12.7 0.6 pad.13.table_b
  13.5 1.0 %maximum_maximum_fusion.img = bf16[2,16,32,384]{3,2,1,0:T(8,128)(2,1)} fusion(bf16[2,4,4,384]{3,2,1,0:T(4,128)(2,1)S(1)} %collective-permute-done.2, bf16[2,4,28,384]{3,2,1,0:T(8,128)(2,1)S(1)} %slice.108, bf16[2,12,4,384]{3,2,1,0:T(4,128)(2,1)S(1)} %slice.106, bf16[2,12,28,384]{3,2,1,0:T(8,128)(2,1)S(1)} %slice.104), kind=kLoop, calls=%fused_computation.2 | loop fusion | flops 3145728 | bytes 1572864 | tf_op jit(solution)/shard_map/concatenate | solution.py:397
  14.5 21.8 %block_grads.1 = (bf16[16,32,384]{2,1,0:T(8,128)(2,1)}, bf16[2,2432,128]{2,1,0:T(8,128)(2,1)}) custom-call(s32[2]{0:T(128)} %add_convert_fusion.1.flags, bf16[2,16,32,384]{3,2,1,0:T(8,128)(2,1)} %maximum_maximum_fusion.img, bf16[384,1152]{1,0:T(8,128)(2,1)} %w_qkv.1, bf16[384,384]{1,0:T(8,128)(2,1)} %w_proj.1, f32[12,128]{1,0:T(8,128)} %pad.11.table_a, ...), custom_call_target="tpu_custom_call" | custom-call | tf_op jit(solution)/shard_map/block_grads/pallas_call | solution.py:340
  36.3 1.2 %dynamic-slice_bitcast_fusion = bf16[2,1216,128]{2,1,0:T(8,128)(2,1)S(1)} fusion(bf16[2,2,1216,128]{3,2,1,0:T(8,128)(2,1)} %bitcast.25, s32[]{:T(128)S(6)} %select_n.42), kind=kLoop, calls=%fused_computation.5 | loop fusion | bytes 1245188 | tf_op jit(solution)/shard_map/jit(dynamic_index_in_dim)/squeeze | solution.py:439
  37.6 2.0 %collective-permute-done.6 = bf16[2,1216,128]{2,1,0:T(8,128)(2,1)S(1)} collective-permute-done((bf16[2,1216,128]{2,1,0:T(8,128)(2,1)S(1)}, bf16[2,1216,128]{2,1,0:T(8,128)(2,1)S(1)}, u32[]{:S(2)}, u32[]{:S(2)}) %collective-permute-start.6) | collective-permute-done | bytes 622624 | tf_op jit(solution)/shard_map/ppermute | solution.py:441
  39.9 24.9 %all_to_all.10 = bf16[16,152,128]{2,1,0:T(8,128)(2,1)S(1)} all-to-all(bf16[16,152,128]{2,1,0:T(8,128)(2,1)S(1)} %bitcast.24), channel_id=1, replica_groups=mesh['hz'=4,'hc'=2,'wa'=2,'ba'=2] {'ba','hz','wa'}, dimensions={0} | all-to-all | bytes 1245184 | tf_op jit(solution)/shard_map/all_to_all | solution.py:445
  64.9 0.8 broadcast_in_dim.19
  65.6 3.6 %all-to-all-start.1 = ((bf16[8,152,128]{2,1,0:T(8,128)(2,1)}), bf16[8,152,128]{2,1,0:T(8,128)(2,1)S(1)}, u32[]{:S(2)}, u32[]{:S(2)}) async-start(bf16[8,152,128]{2,1,0:T(8,128)(2,1)} %broadcast_in_dim.19), calls=%async_computation.1 | async-start | bytes 622592 | tf_op jit(solution)/shard_map/all_to_all | solution.py:448
  69.2 2.0 %collective-permute-start.5 = (bf16[12,4,384]{2,1,0:T(4,128)(2,1)S(1)}, bf16[12,4,384]{2,1,0:T(4,128)(2,1)S(1)}, u32[]{:S(2)}, u32[]{:S(2)}) collective-permute-start(bf16[12,4,384]{2,1,0:T(4,128)(2,1)S(1)} %slice.90), channel_id=1, source_target_pairs={{0,2},{2,0},{4,6},{6,4},{8,10},{10,8},{12,14},{14,12},{16,18},{18,... | collective-permute-start | bytes 110600 | tf_op jit(solution)/shard_map/ppermute | solution.py:426
  71.4 1.6 %collective-permute-start.4 = (bf16[4,28,384]{2,1,0:T(8,128)(2,1)S(1)}, bf16[4,28,384]{2,1,0:T(8,128)(2,1)S(1)}, u32[]{:S(2)}, u32[]{:S(2)}) collective-permute-start(bf16[4,28,384]{2,1,0:T(8,128)(2,1)S(1)} %slice.89), channel_id=1, source_target_pairs={{0,4},{2,6},{4,8},{6,10},{8,12},{10,14},{12,16},{14,18},{16,20},{1... | collective-permute-start | bytes 258056 | tf_op jit(solution)/shard_map/ppermute | solution.py:427
  72.9 0.8 collective-permute-done.5
  73.9 5.7 %all-to-all-done.1 = bf16[8,152,128]{2,1,0:T(8,128)(2,1)S(1)} async-done(((bf16[8,152,128]{2,1,0:T(8,128)(2,1)}), bf16[8,152,128]{2,1,0:T(8,128)(2,1)S(1)}, u32[]{:S(2)}, u32[]{:S(2)}) %all-to-all-start.1) | async-done | bytes 311328 | tf_op jit(solution)/shard_map/all_to_all | solution.py:448
  79.6 0.8 add_convert_fusion
  80.5 0.7 collective-permute-done.7
  81.2 0.5 compare_select_fusion
  81.7 0.6 convert_bitcast_fusion
  82.8 0.6 multiply_multiply_fusion
  83.4 0.8 fusion.2
  84.5 0.2 maximum_select_fusion
  84.6 0.9 copy.18
  85.5 0.4 concatenate.61
  86.0 1.2 %copy.17 = f32[384,576]{0,1:T(8,128)} copy(f32[384,576]{1,0:T(8,128)S(1)} %broadcast_select_fusion) | data formatting | bytes 1769472
  (57 shorter events, 2.1 us)
Async XLA Ops:
  0.6 8.9 %copy-start.5 = (f32[12,225]{1,0:T(8,128)S(1)}, f32[12,225]{1,0:T(8,128)}, u32[]{:S(2)}) copy-start(f32[12,225]{1,0:T(8,128)} %param.11) | copy-start | bytes 32404
  0.6 8.9 %copy-start.7 = (f32[12]{0:T(128)S(1)}, f32[12]{0:T(128)}, u32[]{:S(2)}) copy-start(f32[12]{0:T(128)} %param.12) | copy-start | bytes 148
  1.7 8.7 %copy-start.6 = (f32[384]{0:T(512)S(1)}, f32[384]{0:T(512)}, u32[]{:S(2)}) copy-start(f32[384]{0:T(512)} %param.13) | copy-start | bytes 4612
  2.8 10.6 %collective-permute-start.2 = (bf16[2,4,4,384]{3,2,1,0:T(4,128)(2,1)S(1)}, bf16[2,4,4,384]{3,2,1,0:T(4,128)(2,1)S(1)}, u32[]{:S(2)}, u32[]{:S(2)}) collective-permute-start(bf16[2,4,4,384]{3,2,1,0:T(4,128)(2,1)S(1)} %slice.109), channel_id=1, source_target_pairs={{0,30},{2,28},{4,2},{6,0},{8,6},{10,4},{12,10},{14,8},{16,14},{18,... | collective-permute-start | bytes 73736 | tf_op jit(solution)/shard_map/ppermute | solution.py:394
  8.4 5.0 %collective-permute-start = (bf16[2,16,4,384]{3,2,1,0:T(4,128)(2,1)S(1)}, bf16[2,16,4,384]{3,2,1,0:T(4,128)(2,1)S(1)}, u32[]{:S(2)}, u32[]{:S(2)}) collective-permute-start(bf16[2,16,4,384]{3,2,1,0:T(4,128)(2,1)S(1)} %slice.105), channel_id=1, source_target_pairs={{0,2},{2,0},{4,6},{6,4},{8,10},{10,8},{12,14},{14,12},{16,18},{18,... | collective-permute-start | bytes 294920 | tf_op jit(solution)/shard_map/ppermute | solution.py:393
  9.0 4.4 %collective-permute-start.1 = (bf16[2,4,32,384]{3,2,1,0:T(8,128)(2,1)S(1)}, bf16[2,4,32,384]{3,2,1,0:T(8,128)(2,1)S(1)}, u32[]{:S(2)}, u32[]{:S(2)}) collective-permute-start(bf16[2,4,32,384]{3,2,1,0:T(8,128)(2,1)S(1)} %slice.107), channel_id=1, source_target_pairs={{0,28},{2,30},{4,0},{6,2},{8,4},{10,6},{12,8},{14,10},{16,12},{18,... | collective-permute-start | bytes 589832 | tf_op jit(solution)/shard_map/ppermute | solution.py:392
  36.3 3.3 %copy-start.1 = (bf16[2,2432,128]{2,1,0:T(8,128)(2,1)S(1)}, bf16[2,2432,128]{2,1,0:T(8,128)(2,1)}, u32[]{:S(2)}) copy-start(bf16[2,2432,128]{2,1,0:T(8,128)(2,1)} %get-tuple-element.9) | copy-start | bytes 3735556
  37.6 2.1 %collective-permute-start.6 = (bf16[2,1216,128]{2,1,0:T(8,128)(2,1)S(1)}, bf16[2,1216,128]{2,1,0:T(8,128)(2,1)S(1)}, u32[]{:S(2)}, u32[]{:S(2)}) collective-permute-start(bf16[2,1216,128]{2,1,0:T(8,128)(2,1)S(1)} %dynamic-slice_bitcast_fusion), channel_id=1, source_target_pairs={{0,4},{4,0},{1,5},{5,1},{2,6},{6,2},{3,7},{7,3},{8,12},{12,8},{9,1... | collective-permute-start | bytes 1867784 | tf_op jit(solution)/shard_map/ppermute | solution.py:441
  39.8 29.4 %copy-start.4 = (bf16[16,32,384]{2,1,0:T(8,128)(2,1)S(1)}, bf16[16,32,384]{2,1,0:T(8,128)(2,1)}, u32[]{:S(2)}) copy-start(bf16[16,32,384]{2,1,0:T(8,128)(2,1)} %get-tuple-element.8) | copy-start | bytes 1179652
  65.6 14.0 %copy-start = (bf16[1,16,32,384]{3,2,1,0:T(8,128)(2,1)S(1)}, bf16[1,16,32,384]{3,2,1,0:T(8,128)(2,1)}, u32[]{:S(2)}) copy-start(bf16[1,16,32,384]{3,2,1,0:T(8,128)(2,1)} %param.8) | copy-start | bytes 1179652
  65.6 13.9 %all-to-all-start.1 = ((bf16[8,152,128]{2,1,0:T(8,128)(2,1)}), bf16[8,152,128]{2,1,0:T(8,128)(2,1)S(1)}, u32[]{:S(2)}, u32[]{:S(2)}) async-start(bf16[8,152,128]{2,1,0:T(8,128)(2,1)} %broadcast_in_dim.19), calls=%async_computation.1 | async-start | bytes 622592 | tf_op jit(solution)/shard_map/all_to_all | solution.py:448
  69.2 4.5 %collective-permute-start.5 = (bf16[12,4,384]{2,1,0:T(4,128)(2,1)S(1)}, bf16[12,4,384]{2,1,0:T(4,128)(2,1)S(1)}, u32[]{:S(2)}, u32[]{:S(2)}) collective-permute-start(bf16[12,4,384]{2,1,0:T(4,128)(2,1)S(1)} %slice.90), channel_id=1, source_target_pairs={{0,2},{2,0},{4,6},{6,4},{8,10},{10,8},{12,14},{14,12},{16,18},{18,... | collective-permute-start | bytes 110600 | tf_op jit(solution)/shard_map/ppermute | solution.py:426
  71.3 8.3 %collective-permute-start.3 = (bf16[4,4,384]{2,1,0:T(4,128)(2,1)S(1)}, bf16[4,4,384]{2,1,0:T(4,128)(2,1)S(1)}, u32[]{:S(2)}, u32[]{:S(2)}) collective-permute-start(bf16[4,4,384]{2,1,0:T(4,128)(2,1)S(1)} %slice.88), channel_id=1, source_target_pairs={{0,6},{2,4},{4,10},{6,8},{8,14},{10,12},{12,18},{14,16},{16,22},{1... | collective-permute-start | bytes 36872 | tf_op jit(solution)/shard_map/ppermute | solution.py:428
  71.4 8.2 %collective-permute-start.4 = (bf16[4,28,384]{2,1,0:T(8,128)(2,1)S(1)}, bf16[4,28,384]{2,1,0:T(8,128)(2,1)S(1)}, u32[]{:S(2)}, u32[]{:S(2)}) collective-permute-start(bf16[4,28,384]{2,1,0:T(8,128)(2,1)S(1)} %slice.89), channel_id=1, source_target_pairs={{0,4},{2,6},{4,8},{6,10},{8,12},{10,14},{12,16},{14,18},{16,20},{1... | collective-permute-start | bytes 258056 | tf_op jit(solution)/shard_map/ppermute | solution.py:427
  79.6 1.6 %collective-permute-start.7 = (bf16[1216,128]{1,0:T(8,128)(2,1)S(1)}, bf16[1216,128]{1,0:T(8,128)(2,1)S(1)}, u32[]{:S(2)}, u32[]{:S(2)}) collective-permute-start(bf16[1216,128]{1,0:T(8,128)(2,1)S(1)} %bitcast.27), channel_id=1, source_target_pairs={{0,4},{4,0},{1,5},{5,1},{2,6},{6,2},{3,7},{7,3},{8,12},{12,8},{9,1... | collective-permute-start | bytes 933896 | tf_op jit(solution)/shard_map/ppermute | solution.py:450
  84.5 1.1 %copy-start.2 = (f32[384,128]{1,0:T(8,128)S(1)}, f32[384,128]{1,0:T(8,128)}, u32[]{:S(2)}) copy-start(f32[384,128]{1,0:T(8,128)} %get-tuple-element.29) | copy-start | bytes 589828
  84.5 1.1 %copy-start.3 = (f32[384,128]{1,0:T(8,128)S(1)}, f32[384,128]{1,0:T(8,128)}, u32[]{:S(2)}) copy-start(f32[384,128]{1,0:T(8,128)} %get-tuple-element.30) | copy-start | bytes 589828

commit v2 on v1

v2 whole, which is shorter than its diff:
```python
import math

import jax
import jax.numpy as jnp
from jax import lax
from jax.experimental import pallas as pl
from jax.experimental.pallas import tpu as pltpu
from jax.sharding import Mesh
from jax.sharding import PartitionSpec as P

WIN = 8
TOKENS = WIN * WIN
LANES = 128
EPS_NORM = 1e-05
MASK_FILL = -100.0
SCALE_CAP = math.log(100.0)
BIAS_RANGE = 16.0
PROJECT_UNROLL = 4
FORWARD_UNROLL = 4
NORM_UNROLL = 4
FLATTEN_UNROLL = 4
BACKWARD_UNROLL = 4
F32 = jnp.float32
BF16 = jnp.bfloat16


def dot_nn(left, right):
    return lax.dot_general(left, right, (((1,), (0,)), ((), ())), preferred_element_type=F32)


def dot_nt(left, right):
    return lax.dot_general(left, right, (((1,), (1,)), ((), ())), preferred_element_type=F32)


def dot_tn(left, right):
    return lax.dot_general(left, right, (((0,), (0,)), ((), ())), preferred_element_type=F32)


def iota(shape, dim):
    return lax.broadcasted_iota(jnp.int32, shape, dim)


def split(value):
    high = value.astype(BF16)
    return high, (value - high.astype(F32)).astype(BF16)


def group_sum(value, ones, fine=True):
    high, low = split(value)
    width = ones.shape[0]
    parts = []
    for start in range(0, value.shape[1], width):
        part = slice(start, start + width)
        total = dot_nn(high[:, part], ones)
        parts.append(total + dot_nn(low[:, part], ones) if fine else total)
    return jnp.concatenate(parts, axis=1)


def table_maps(span, used):
    entry = iota((used, LANES), 0)
    lane = iota((used, LANES), 1)
    same_row = entry // span == lane // WIN
    near = jnp.logical_and(same_row, entry % span == lane % WIN)
    far = jnp.logical_and(same_row, entry % span == lane % WIN + WIN)
    return near.astype(F32).astype(BF16), far.astype(F32).astype(BF16)


def make_kernel(rows, cols, depth, heads, sent_rows):
    head_dim = depth // heads
    per_tile = LANES // head_dim
    groups = heads // per_tile
    col_windows = cols // WIN
    row_windows = rows // WIN
    pairs = row_windows * col_windows // 2
    pairs_across = col_windows // 2
    stacked = per_tile * TOKENS
    pair = 2 * TOKENS
    tokens = rows * cols
    span = 2 * WIN - 1
    half_q = 3 * depth // 2
    half_p = depth // 2
    body = half_q + half_p
    small_at = groups * body
    small_rows = sent_rows - small_at
    core_rows = sent_rows // 2

    def kernel(
        limit,
        img,
        w_qkv,
        w_proj,
        logits,
        gain,
        d_img,
        mine,
        given,
        xb,
        uf,
        unit_s,
        inv,
        q_low,
        q_turn,
        k_hi,
        k_lo,
        val,
        prob,
        raw,
        att,
        d_prj,
        d_att,
        d_qkv,
        d_unit,
        bias,
        d_bias,
        d_sc,
        small,
        sums,
        padded,
    ):
        core = lax.axis_index("hc")
        down = lax.axis_index("hz") * lax.axis_size("hc") + core
        last_row = (down == lax.axis_size("hz") * lax.axis_size("hc") - 1).astype(jnp.int32)
        last_col = (lax.axis_index("wa") == lax.axis_size("wa") - 1).astype(jnp.int32)
        half = iota((1, LANES), 1) < TOKENS
        wide = 2 * LANES
        ones = (iota((wide, wide), 0) // head_dim == iota((wide, wide), 1) // head_dim).astype(F32)
        ones = ones.astype(BF16)
        owner = iota((1, wide), 1) % LANES // head_dim
        head_f32 = [(owner == h).astype(F32) for h in range(per_tile)]
        head_low = [m.astype(BF16) for m in head_f32]
        top_rows = (iota((pair, LANES), 0) < TOKENS).astype(F32)
        top_rows, low_rows = top_rows.astype(BF16), (1.0 - top_rows).astype(BF16)
        left_lanes = half.astype(F32)
        left_lanes, right_lanes = left_lanes.astype(BF16), (1.0 - left_lanes).astype(BF16)
        by_head = iota((1, depth), 1) // head_dim
        scale = jnp.zeros((1, depth), F32)
        for h in range(heads):
            scale = jnp.where(by_head == h, limit[h], scale)
        scale = jnp.exp(jnp.minimum(scale, SCALE_CAP))

        def project(p, carry):
            place = pl.ds(pl.multiple_of(p * pair, pair), pair)
            pieces, ups = [], []
            for w in range(2):
                i0 = p // pairs_across * WIN
                j0 = pl.multiple_of((p % pairs_across * 2 + w) * WIN, WIN)
                for r in range(WIN):
                    pieces.append(img[0, i0 + r, pl.ds(j0, WIN), :].astype(F32))
                    ups.append(img[1, i0 + r, pl.ds(j0, WIN), :].astype(F32))
            x = jnp.concatenate(pieces, axis=0).astype(BF16)
            uf[place, :] = jnp.concatenate(ups, axis=0)
            xb[place, :] = x
            qkv = dot_nn(x, w_qkv[...]).astype(BF16)
            val[place, :] = qkv[:, 2 * depth :]
            both = qkv[:, : 2 * depth].astype(F32)
            root = lax.rsqrt(group_sum(both * both, ones) + 1.0)
            unit = both * root
            unit_s[place, :] = unit
            inv[place, :] = root[:, depth:]
            q_low[place, :] = qkv[:, :depth]
            q_turn[p] = (root[:, :depth] * scale).T
            k_hi[place, :], k_lo[place, :] = split(unit[:, depth:])
            return carry

        lax.fori_loop(0, pairs, project, 0, unroll=PROJECT_UNROLL)

        sub = iota((WIN, LANES), 0)
        lane = iota((WIN, LANES), 1)
        near_map, far_map = table_maps(span, 2 * LANES)
        padded[...] = jnp.zeros_like(padded)
        padded[:heads, : span * span] = jax.nn.sigmoid(logits[...]) * BIAS_RANGE
        table = padded[...]
        first = table.astype(BF16)
        second, third = split(table - first.astype(F32))
        table_a = dot_nn(first, near_map) + (dot_nn(second, near_map) + dot_nn(third, near_map))
        table_b = dot_nn(first, far_map) + (dot_nn(second, far_map) + dot_nn(third, far_map))
        for h in range(heads):
            near = jnp.broadcast_to(table_a[h : h + 1, :], (WIN, LANES))
            far = jnp.broadcast_to(table_b[h : h + 1, :], (WIN, LANES))
            near = pltpu.roll(near, LANES - WIN + 1, 1, stride=1, stride_axis=0)
            far = pltpu.roll(far, 1, 1, stride=1, stride_axis=0)
            line = jnp.where(lane % WIN <= sub, near, far)
            for r in range(WIN):
                one = pltpu.roll(line, (LANES - (WIN - 1 - r) * WIN) % LANES, 1)
                two = pltpu.roll(line, (LANES + TOKENS - (WIN - 1 - r) * WIN) % LANES, 1)
                at = h * TOKENS + r * WIN
                bias[at : at + WIN, :] = jnp.where(half, one, two)
        d_bias[...] = jnp.zeros_like(d_bias)
        d_sc[...] = jnp.zeros_like(d_sc)

        key = iota((TOKENS, LANES), 0)
        query = iota((TOKENS, LANES), 1) % TOKENS
        edge = WIN // 2
        split_r = ((key // WIN) >= edge) != ((query // WIN) >= edge)
        split_c = ((key % WIN) >= edge) != ((query % WIN) >= edge)
        split_c = jnp.logical_and(split_c, iota((TOKENS, LANES), 1) >= TOKENS)
        mask_r = jnp.where(split_r, MASK_FILL, 0.0)
        mask_c = jnp.where(split_c, MASK_FILL, 0.0)

        def beside(ref, at, tile):
            one = ref[pl.ds(at, TOKENS), tile]
            two = ref[pl.ds(at + TOKENS, TOKENS), tile]
            return jnp.concatenate([one, two], axis=1)

        def stack(block):
            return jnp.concatenate([block * head_low[h] for h in range(per_tile)], axis=0)

        def diagonal(ref, at, tile):
            block = ref[pl.ds(at, pair), tile]
            return jnp.concatenate([block * top_rows, block * low_rows], axis=1)

        def turned(ref, at, tile):
            block = ref[pl.ds(at, pair), tile].T
            return jnp.concatenate([block * left_lanes, block * right_lanes], axis=0)

        def gather_heads(out):
            total = out[:TOKENS] * head_f32[0]
            for h in range(1, per_tile):
                total = total + out[h * TOKENS : (h + 1) * TOKENS] * head_f32[h]
            return total

        def forward(p, carry):
            at = pl.multiple_of(p * pair, pair)
            row_edge = jnp.where(p // pairs_across == row_windows - 1, last_row, 0)
            col_edge = jnp.where(p % pairs_across == pairs_across - 1, last_col, 0)
            mask = jnp.minimum(mask_r * row_edge.astype(F32), mask_c * col_edge.astype(F32))
            for g in range(groups):
                tile = slice(g * LANES, (g + 1) * LANES)
                keys = stack(beside(k_hi, at, tile))
                keys_low = stack(beside(k_lo, at, tile))
                queries = turned(q_low, at, tile)
                score = dot_nn(keys, queries) + dot_nn(keys_low, queries)
                lows = []
                for h in range(per_tile):
                    place = slice(h * TOKENS, (h + 1) * TOKENS)
                    of = (g * per_tile + h) * TOKENS
                    line = (g * per_tile + h) * head_dim
                    s = score[place] * q_turn[p, line : line + 1, :]
                    raw[p, g, place, :] = s
                    s = s + (bias[of : of + TOKENS, :] + mask)
                    e = jnp.exp(s - jnp.max(s, axis=0, keepdims=True))
                    pr = e * (1.0 / jnp.sum(e, axis=0, keepdims=True))
                    prob[p, g, place, :] = pr
                    lows.append(pr.astype(BF16))
                out = dot_tn(jnp.concatenate(lows, axis=0), stack(beside(val, at, tile)))
                att[pl.ds(at, TOKENS), tile] = out[:TOKENS, :LANES].astype(BF16)
                att[pl.ds(at + TOKENS, TOKENS), tile] = out[TOKENS:, LANES:].astype(BF16)
            return carry

        lax.fori_loop(0, pairs, forward, 0, unroll=FORWARD_UNROLL)

        gains = gain[...].reshape(1, depth)

        def norm(p, d_gain):
            place = pl.ds(pl.multiple_of(p * pair, pair), pair)
            proj = dot_nn(att[place, :], w_proj[...])
            centre = proj - jnp.mean(proj, -1, keepdims=True)
            std = lax.rsqrt(jnp.mean(centre * centre, -1, keepdims=True) + EPS_NORM)
            normed = centre * std
            up = uf[place, :]
            d_gain = d_gain + jnp.sum(up * normed, axis=0, keepdims=True)
            u = up * gains
            d_p = std * (
                u - jnp.mean(u, -1, keepdims=True) - normed * jnp.mean(u * normed, -1, keepdims=True)
            )
            d_p = d_p.astype(BF16)
            d_prj[place, :] = d_p
            return d_gain

        d_gain = lax.fori_loop(0, pairs, norm, jnp.zeros((1, depth), F32), unroll=NORM_UNROLL)

        w_proj_turned = w_proj[...].T

        def spread(p, carry):
            place = pl.ds(pl.multiple_of(p * pair, pair), pair)
            d_att[place, :] = dot_nn(d_prj[place, :], w_proj_turned).astype(BF16)
            return carry

        lax.fori_loop(0, pairs, spread, 0, unroll=NORM_UNROLL)

        def backward(p, carry):
            at = pl.multiple_of(p * pair, pair)
            for g in range(groups):
                tile = slice(g * LANES, (g + 1) * LANES)
                key_tile = slice(depth + g * LANES, depth + (g + 1) * LANES)
                val_tile = slice(2 * depth + g * LANES, 2 * depth + (g + 1) * LANES)
                values = stack(beside(val, at, tile))
                ups = diagonal(d_att, at, tile)
                d_pr = dot_nn(values, turned(d_att, at, tile))
                lows, d_lows = [], []
                for h in range(per_tile):
                    place = slice(h * TOKENS, (h + 1) * TOKENS)
                    of = (g * per_tile + h) * TOKENS
                    pr = prob[p, g, place, :]
                    pd = pr * d_pr[place]
                    d_s = pd - pr * jnp.sum(pd, axis=0, keepdims=True)
                    d_bias[of : of + TOKENS, :] += d_s
                    by_scale = (d_s * raw[p, g, place, :]).reshape(WIN, WIN, LANES)
                    head = g * per_tile + h
                    d_sc[head * WIN : (head + 1) * WIN, :] += jnp.sum(by_scale, axis=0)
                    lows.append(pr.astype(BF16))
                    line = head * head_dim
                    d_lows.append((d_s * q_turn[p, line : line + 1, :]).astype(BF16))
                low = jnp.concatenate(lows, axis=0)
                d_low = jnp.concatenate(d_lows, axis=0)
                d_v = gather_heads(dot_nn(low, ups)).astype(BF16)
                d_qkv[pl.ds(at, TOKENS), val_tile] = d_v[:, :LANES]
                d_qkv[pl.ds(at + TOKENS, TOKENS), val_tile] = d_v[:, LANES:]
                d_k = gather_heads(dot_nn(d_low, diagonal(q_low, at, tile)))
                d_unit[pl.ds(at, TOKENS), key_tile] = d_k[:, :LANES]
                d_unit[pl.ds(at + TOKENS, TOKENS), key_tile] = d_k[:, LANES:]
                d_q = dot_tn(d_low, stack(beside(k_hi, at, tile)))
                d_unit[pl.ds(at, TOKENS), tile] = d_q[:TOKENS, :LANES]
                d_unit[pl.ds(at + TOKENS, TOKENS), tile] = d_q[TOKENS:, LANES:]
            return carry

        lax.fori_loop(0, pairs, backward, 0, unroll=BACKWARD_UNROLL)

        w_qkv_turned = w_qkv[...].T

        def flatten(p, carry):
            place = pl.ds(pl.multiple_of(p * pair, pair), pair)
            unit = unit_s[place, :]
            d_u = d_unit[place, :]
            d_u = d_u - unit * group_sum(unit * d_u, ones, False)
            d_qkv[place, :depth] = d_u[:, :depth].astype(BF16)
            d_qkv[place, depth : 2 * depth] = (inv[place, :] * d_u[:, depth:]).astype(BF16)
            flat = dot_nn(d_qkv[place, :], w_qkv_turned)
            for w in range(2):
                i0 = p // pairs_across * WIN
                j0 = pl.multiple_of((p % pairs_across * 2 + w) * WIN, WIN)
                for r in range(WIN):
                    piece = flat[w * TOKENS + r * WIN : w * TOKENS + (r + 1) * WIN]
                    d_img[i0 + r, pl.ds(j0, WIN), :] = piece.astype(BF16)
            return carry

        lax.fori_loop(0, pairs, flatten, 0, unroll=FLATTEN_UNROLL)

        d_wp = dot_tn(d_prj[...], att[...])
        d_wq = dot_tn(d_qkv[...], xb[...])
        for b in range(2):
            for j in range(groups):
                tile = slice(j * LANES, (j + 1) * LANES)
                at = j * body
                sums[b, at : at + half_q, :] = d_wq[b * half_q : (b + 1) * half_q, tile].astype(BF16)
                at = at + half_q
                sums[b, at : at + half_p, :] = d_wp[b * half_p : (b + 1) * half_p, tile].astype(BF16)

        small[...] = jnp.zeros_like(small)
        for h in range(heads):
            line = jnp.zeros((WIN, LANES), F32)
            for r in range(WIN):
                at = h * TOKENS + r * WIN
                part = d_bias[at : at + WIN, :]
                part = jnp.where(half, part + pltpu.roll(part, TOKENS, 1), 0.0)
                line = line + pltpu.roll(part, (WIN - 1 - r) * WIN, 1)
            near, far = jnp.zeros_like(line), jnp.zeros_like(line)
            for c in range(WIN):
                own = jnp.where(sub == c, line, 0.0)
                near = near + pltpu.roll(own, WIN - 1 - c, 1)
                far = far + pltpu.roll(own, LANES - 1 - c, 1)
            near = jnp.where(lane % WIN >= WIN - 1 - sub, near, 0.0)
            far = jnp.where(lane % WIN + sub + 1 <= WIN - 1, far, 0.0)
            small[h : h + 1, :] = jnp.sum(near, axis=0, keepdims=True)
            small[heads + h : heads + h + 1, :] = jnp.sum(far, axis=0, keepdims=True)
        for j in range(groups):
            small[2 * heads + j : 2 * heads + j + 1, :] = d_gain[:, j * LANES : (j + 1) * LANES]
        line = jnp.zeros((1, LANES), F32)
        for h in range(heads):
            total = jnp.sum(d_sc[h * WIN : (h + 1) * WIN, :], axis=0, keepdims=True)
            total = jnp.sum(total, axis=1, keepdims=True)
            line = line + jnp.where(iota((1, LANES), 1) == h, total, 0.0)
        at = 2 * heads + groups
        small[at : at + 1, :] = line
        for b in range(2):
            sums[b, small_at:, :] = small[...].astype(BF16)
        own = pl.multiple_of(core * core_rows, 8)
        other = pl.multiple_of((1 - core) * core_rows, 8)
        for b in range(2):
            mine[b] = sums[b, pl.ds(own, core_rows), :]
            given[b] = sums[b, pl.ds(other, core_rows), :]

    def call(limit, img, w_qkv, w_proj, logits, gain):
        vmem = pltpu.VMEM
        scratch = [
            vmem((tokens, depth), BF16),
            vmem((tokens, depth), F32),
            vmem((tokens, 2 * depth), F32),
            vmem((tokens, depth), F32),
            vmem((tokens, depth), BF16),
            vmem((pairs, depth, pair), F32),
            vmem((tokens, depth), BF16),
            vmem((tokens, depth), BF16),
            vmem((tokens, depth), BF16),
            vmem((pairs, groups, stacked, LANES), F32),
            vmem((pairs, groups, stacked, LANES), F32),
            vmem((tokens, depth), BF16),
            vmem((tokens, depth), BF16),
            vmem((tokens, depth), BF16),
            vmem((tokens, 3 * depth), BF16),
            vmem((tokens, 2 * depth), F32),
            vmem((heads * TOKENS, LANES), F32),
            vmem((heads * TOKENS, LANES), F32),
            vmem((heads * WIN, LANES), F32),
            vmem((small_rows, LANES), F32),
            vmem((2, sent_rows, LANES), BF16),
            vmem((16, 2 * LANES), F32),
        ]
        part = jax.ShapeDtypeStruct((2, core_rows, LANES), BF16)
        return pl.pallas_call(
            kernel,
            out_shape=(jax.ShapeDtypeStruct((rows, cols, depth), BF16), part, part),
            in_specs=[pl.BlockSpec(memory_space=pltpu.SMEM)]
            + [pl.BlockSpec(memory_space=pltpu.VMEM)] * 5,
            out_specs=tuple([pl.BlockSpec(memory_space=pltpu.VMEM)] * 3),
            scratch_shapes=scratch,
            name="block_grads",
        )(limit, img, w_qkv, w_proj, logits, gain)

    return call


def finish(ours, theirs, logits, limit, depth, heads):
    core_rows = ours.shape[0]
    groups = depth // LANES
    half_q = 3 * depth // 2
    half_p = depth // 2
    body = half_q + half_p
    small_at = groups * body
    span = 2 * WIN - 1

    def kernel(limit, ours, theirs, logits, d_wq, d_wp, d_table, d_scale, d_gain, whole):
        core = lax.axis_index("hc")
        whole[pl.ds(pl.multiple_of(core * core_rows, 8), core_rows), :] = ours[...].astype(F32)
        other = pl.multiple_of((1 - core) * core_rows, 8)
        whole[pl.ds(other, core_rows), :] = theirs[...].astype(F32)
        for j in range(groups):
            tile = slice(j * LANES, (j + 1) * LANES)
            d_wq[:, tile] = whole[j * body : j * body + half_q, :]
            d_wp[:, tile] = whole[j * body + half_q : (j + 1) * body, :]
        small = whole[small_at : small_at + 32, :]
        near_map, far_map = table_maps(span, 2 * LANES)
        table = dot_nt(small[:16].astype(BF16), near_map)
        table = table + dot_nt(small[heads : heads + 16].astype(BF16), far_map)
        table = table[:heads, : span * span]
        sigma = jax.nn.sigmoid(logits[...])
        d_table[...] = table * (BIAS_RANGE * sigma * (1.0 - sigma))
        gains = [small[2 * heads + j : 2 * heads + j + 1, :] for j in range(groups)]
        d_gain[...] = jnp.concatenate(gains, axis=1).reshape(depth)
        lane = iota((1, LANES), 1)
        kept = jnp.zeros((1, LANES), F32)
        for h in range(heads):
            kept = jnp.where(lane == h, jnp.where(limit[h] < SCALE_CAP, 1.0, 0.0), kept)
        row = small[2 * heads + groups : 2 * heads + groups + 1, :] * kept
        d_scale[...] = row[:, :heads].reshape(heads)

    vmem = pl.BlockSpec(memory_space=pltpu.VMEM)
    return pl.pallas_call(
        kernel,
        out_shape=(
            jax.ShapeDtypeStruct((half_q, depth), F32),
            jax.ShapeDtypeStruct((half_p, depth), F32),
            jax.ShapeDtypeStruct(logits.shape, F32),
            jax.ShapeDtypeStruct((heads,), F32),
            jax.ShapeDtypeStruct((depth,), F32),
        ),
        in_specs=[pl.BlockSpec(memory_space=pltpu.SMEM), vmem, vmem, vmem],
        out_specs=(vmem,) * 5,
        scratch_shapes=[pltpu.VMEM((2 * core_rows, LANES), F32)],
        name="finish",
    )(limit, ours, theirs, logits)


def route(axes, move):
    sizes = [lax.axis_size(a) for a in axes]
    pairs = []
    for flat in range(math.prod(sizes)):
        left, where = flat, []
        for size in reversed(sizes):
            where.append(left % size)
            left //= size
        where = move(where[::-1], sizes)
        target = 0
        for place, size in zip(where, sizes):
            target = target * size + place
        pairs.append((flat, target))
    return pairs


GRID = ("hz", "hc", "wa")


def step(rows, cols):
    def move(where, sizes):
        high = (where[0] * sizes[1] + where[1] + rows) % (sizes[0] * sizes[1])
        return [high // sizes[1], high % sizes[1], (where[2] + cols) % sizes[2]]

    return move


def shards(tokens, cotangent, w_qkv, w_proj, table_logits, logit_scale, gain):
    images, rows, cols, depth = tokens.shape
    heads = logit_scale.shape[0]
    edge = WIN // 2
    both = jnp.concatenate([tokens, cotangent], 0)
    below = lax.ppermute(both[:, :edge], GRID, route(GRID, step(-1, 0)))
    beside = lax.ppermute(both[:, :, :edge], GRID, route(GRID, step(0, -1)))
    corner = lax.ppermute(both[:, :edge, :edge], GRID, route(GRID, step(-1, -1)))
    main = jnp.concatenate([both[:, edge:, edge:], beside[:, edge:]], 2)
    last = jnp.concatenate([below[:, :, edge:], corner], 2)
    moved = jnp.concatenate([main, last], 1)

    cores, tall, across = lax.axis_size("hc"), lax.axis_size("hz"), lax.axis_size("wa")
    owners = cores * tall * across
    used = 2 * depth // LANES * depth + 2 * heads + depth // LANES + 1
    unit = 8 * owners
    sent = -(-used // unit) * unit
    call = make_kernel(rows, cols, depth, heads, sent)
    d_moved, mine, given = call(logit_scale, moved, w_qkv, w_proj, table_logits, gain)

    right = lax.ppermute(d_moved[: rows - edge, cols - edge :], GRID, route(GRID, step(0, 1)))
    lower = lax.ppermute(d_moved[rows - edge :, : cols - edge], GRID, route(GRID, step(1, 0)))
    cross = lax.ppermute(
        d_moved[rows - edge :, cols - edge :], GRID, route(GRID, step(1, 1))
    )
    upper = jnp.concatenate([cross, lower], 1)
    main = jnp.concatenate([right, d_moved[: rows - edge, : cols - edge]], 1)
    back = jnp.concatenate([upper, main], 0)[None]
    d_tokens = (cotangent.astype(F32) + back.astype(F32)).astype(BF16)

    swap = route(("hc",), lambda where, sizes: [1 - where[0]])
    taken = lax.ppermute(given, "hc", swap)
    summed = (mine.astype(F32) + taken.astype(F32)).astype(BF16)
    piece = sent // owners
    summed = summed.reshape(2 * tall * across, piece, LANES)
    parts = lax.all_to_all(summed, ("ba", "hz", "wa"), 0, 0, tiled=True)
    total = parts.astype(F32).sum(0).astype(BF16)
    spread = jnp.broadcast_to(total[None], (tall * across, piece, LANES))
    ours = lax.all_to_all(spread, ("hz", "wa"), 0, 0, tiled=True)
    ours = ours.reshape(sent // cores, LANES)
    theirs = lax.ppermute(ours, "hc", swap)
    d_wq, d_wp, d_table, d_scale, d_gain = finish(
        ours, theirs, table_logits, logit_scale, depth, heads
    )
    return (d_tokens, d_wq.T, d_wp.T, d_table, d_scale, d_gain)


def solution(mesh):
    sizes = mesh.shape
    devices = mesh.devices.reshape(sizes["ha"] // 2, 2, sizes["wa"], sizes["ba"])
    inner = Mesh(devices, ("hz", "hc", "wa", "ba"))
    image = P("ba", ("hz", "hc"), "wa", None)
    return jax.shard_map(
        shards,
        mesh=inner,
        in_specs=(image, image, P(), P(), P(), P(), P()),
        out_specs=(image, P(None, "ba"), P(None, "ba"), P(), P(), P()),
        check_vma=False,
    )
```

time: 87.6 us -> 74.4 us (0.85)
  local copies, waits for them, and re-layouts: 11.2 us -> 3.03 us
  Pallas kernels: 21.8 us -> 17.2 us
  waiting for transfers between devices: 9.27 us -> 12.2 us
  other arithmetic: 5.12 us -> 3.33 us
  blocking collectives: 24.9 us -> 23.9 us
    pallas_call x1, Pallas kernels: 21.8 us -> 15 us  [call(): pl.pallas_call(kernel, out_shape=(jax.ShapeDtypeStruct((rows, cols, depth...]
    ppermute x1, starting transfers between devices: 5.53 us -> 0.39 us  [shards(): lax.ppermute(both[:, :edge, :edge], GRID, route(GRID, step(-1, -1)))]
    ppermute x1, starting transfers between devices: 0.62 us -> 4.57 us  [shards(): below = lax.ppermute(both[:, :edge], GRID, route(GRID, step(-1, 0)))]
    ppermute x1, waiting for transfers between devices: 0.01 us -> 2.56 us  [shards(): beside = lax.ppermute(both[:, :, :edge], GRID, route(GRID, step(0, -1)))]
    pallas_call x0 -> x1, Pallas kernels: none -> 2.28 us  [finish(): pl.pallas_call(kernel, out_shape=(jax.ShapeDtypeStruct((half_q, depth), F...]
    unnamed x22 -> x9, local copies, waits for them, and re-layouts: 3.23 us -> 1.82 us
    pad x3 -> x0, local copies, waits for them, and re-layouts: 1.22 us -> none  [the longest x2 1.21 us: shards(): table_a, table_b = (jnp.pad(table_a, fill), jnp.pad(table_b, fill))]
    squeeze x1 -> x0, local copies, waits for them, and re-layouts: 1.22 us -> none  [shards(): given = lax.dynamic_index_in_dim(grads, 1 - core, 1, keepdims=False)]
  transfers between devices with their start and end apart: 9 -> 9, of which waited for: 4 -> 6; matrix products, arithmetic and copies ran while one was open for 6% -> 2% of each run, Pallas kernels for 0% -> 0%
where the time goes in v2:
time: 74.4 us; the launch traced here: 74 us
  blocking collectives  23.9 us (32%)
  Pallas kernels  17.2 us (23%)
  starting transfers between devices  13.6 us (18%)
  waiting for transfers between devices  12.2 us (16%)
  other arithmetic  3.33 us (4%)
  local copies, waits for them, and re-layouts  3.03 us (4%)
  between operations  0.77 us (1%)
    all_to_all x1, blocking collectives, shards(): parts = lax.all_to_all(summed, ('ba', 'hz', 'wa'), 0, 0, tiled=True)  23.9 us
    pallas_call x1, Pallas kernels, call(): pl.pallas_call(kernel, out_shape=(jax.ShapeDtypeStruct((rows, cols, depth...  15 us
    all_to_all x1, waiting for transfers between devices, shards(): ours = lax.all_to_all(spread, ('hz', 'wa'), 0, 0, tiled=True)  5.7 us
    ppermute x1, starting transfers between devices, shards(): below = lax.ppermute(both[:, :edge], GRID, route(GRID, step(-1, 0)))  4.57 us
    all_to_all x1, starting transfers between devices, shards(): ours = lax.all_to_all(spread, ('hz', 'wa'), 0, 0, tiled=True)  3.43 us
    ppermute x1, waiting for transfers between devices, shards(): beside = lax.ppermute(both[:, :, :edge], GRID, route(GRID, step(0, -1)))  2.56 us
    pallas_call x1, Pallas kernels, finish(): pl.pallas_call(kernel, out_shape=(jax.ShapeDtypeStruct((half_q, depth), F...  2.28 us
    ppermute x1, waiting for transfers between devices, shards(): taken = lax.ppermute(given, 'hc', swap)  2.26 us
  transfers between devices with their start and end apart: 9, of which 6 were waited for; matrix products, arithmetic and copies ran while one was open for 2% of the time, Pallas kernels for 0%

profile of v2, /device:TPU:0, one launch (start us, length us, event | category | flops | bytes accessed | tf_op | source)
XLA Modules:
  0.0 74.0 jit_solution(11605591832543332065)
XLA Ops:
  0.6 1.1 %constant_dynamic-update-slice_fusion.1 = bf16[2,16,32,384]{3,2,1,0:T(8,128)(2,1)S(1)} fusion(bf16[1,16,32,384]{3,2,1,0:T(8,128)(2,1)} %param.7), kind=kLoop, calls=%fused_computation.6 | loop fusion | bytes 786432
  1.7 0.0 copy-done
  1.7 0.1 constant_dynamic-update-slice_fusion
  1.8 4.6 %collective-permute-start.1 = (bf16[2,4,32,384]{3,2,1,0:T(8,128)(2,1)S(1)}, bf16[2,4,32,384]{3,2,1,0:T(8,128)(2,1)S(1)}, u32[]{:S(2)}, u32[]{:S(2)}) collective-permute-start(bf16[2,4,32,384]{3,2,1,0:T(8,128)(2,1)S(1)} %slice.43), channel_id=1, source_target_pairs={{0,28},{2,30},{4,0},{6,2},{8,4},{10,6},{12,8},{14,10},{16,12},{18,... | collective-permute-start | bytes 589832 | tf_op jit(solution)/shard_map/ppermute | solution.py:506
  6.4 1.6 %collective-permute-start = (bf16[2,16,4,384]{3,2,1,0:T(4,128)(2,1)S(1)}, bf16[2,16,4,384]{3,2,1,0:T(4,128)(2,1)S(1)}, u32[]{:S(2)}, u32[]{:S(2)}) collective-permute-start(bf16[2,16,4,384]{3,2,1,0:T(4,128)(2,1)S(1)} %slice.41), channel_id=1, source_target_pairs={{0,2},{2,0},{4,6},{6,4},{8,10},{10,8},{12,14},{14,12},{16,18},{18,... | collective-permute-start | bytes 294920 | tf_op jit(solution)/shard_map/ppermute | solution.py:507
  8.0 0.4 collective-permute-start.2
  8.4 0.2 slice.40
  8.6 2.6 %collective-permute-done = bf16[2,16,4,384]{3,2,1,0:T(4,128)(2,1)S(1)} collective-permute-done((bf16[2,16,4,384]{3,2,1,0:T(4,128)(2,1)S(1)}, bf16[2,16,4,384]{3,2,1,0:T(4,128)(2,1)S(1)}, u32[]{:S(2)}, u32[]{:S(2)}) %collective-permute-start) | collective-permute-done | bytes 98336 | tf_op jit(solution)/shard_map/ppermute | solution.py:507
  11.2 0.0 collective-permute-done.1
  11.2 0.1 slice.44
  11.3 0.1 collective-permute-done.2
  11.4 1.0 %maximum_maximum_fusion.img = bf16[2,16,32,384]{3,2,1,0:T(8,128)(2,1)} fusion(bf16[2,4,4,384]{3,2,1,0:T(4,128)(2,1)S(1)} %collective-permute-done.2, bf16[2,4,28,384]{3,2,1,0:T(8,128)(2,1)S(1)} %slice.44, bf16[2,12,4,384]{3,2,1,0:T(4,128)(2,1)S(1)} %slice.42, bf16[2,12,28,384]{3,2,1,0:T(8,128)(2,1)S(1)} %slice.40), kind=kLoop, calls=%fused_computation.1 | loop fusion | flops 3145728 | bytes 1572864 | tf_op jit(solution)/shard_map/concatenate | solution.py:511
  12.4 15.0 %block_grads.1 = (bf16[16,32,384]{2,1,0:T(8,128)(2,1)}, bf16[2,1216,128]{2,1,0:T(8,128)(2,1)}, bf16[2,1216,128]{2,1,0:T(8,128)(2,1)}) custom-call(f32[12]{0:T(128)} %limit.3, bf16[2,16,32,384]{3,2,1,0:T(8,128)(2,1)} %maximum_maximum_fusion.img, bf16[384,1152]{1,0:T(8,128)(2,1)} %w_qkv.1, bf16[384,384]{1,0:T(8,128)(2,1)} %w_proj.1, f32[12,225]{1,0:T(8,128)} %logits.3, ...), custom_call_target="tpu_custom_call" | custom-call | tf_op jit(solution)/shard_map/block_grads/pallas_call | solution.py:410
  27.4 0.0 collective-permute-start.6
  27.4 2.3 %collective-permute-done.6 = bf16[2,1216,128]{2,1,0:T(8,128)(2,1)S(1)} collective-permute-done((bf16[2,1216,128]{2,1,0:T(8,128)(2,1)}, bf16[2,1216,128]{2,1,0:T(8,128)(2,1)S(1)}, u32[]{:S(2)}, u32[]{:S(2)}) %collective-permute-start.6) | collective-permute-done | bytes 622624 | tf_op jit(solution)/shard_map/ppermute | solution.py:532
  29.6 1.2 %add_convert_fusion = bf16[2,1216,128]{2,1,0:T(8,128)(2,1)S(1)} fusion(bf16[2,1216,128]{2,1,0:T(8,128)(2,1)S(1)} %collective-permute-done.6, bf16[2,1216,128]{2,1,0:T(8,128)(2,1)} %get-tuple-element.15), kind=kLoop, calls=%fused_computation | loop fusion | flops 1245184 | bytes 1867776 | tf_op jit(solution)/shard_map/convert_element_type | solution.py:533
  30.9 23.9 %all_to_all.10 = bf16[16,152,128]{2,1,0:T(8,128)(2,1)S(1)} all-to-all(bf16[16,152,128]{2,1,0:T(8,128)(2,1)S(1)} %bitcast.8), channel_id=1, replica_groups=mesh['hz'=4,'hc'=2,'wa'=2,'ba'=2] {'ba','hz','wa'}, dimensions={0} | all-to-all | bytes 1245184 | tf_op jit(solution)/shard_map/all_to_all | solution.py:536
  54.8 0.1 reduce_sum.12
  54.9 0.8 %broadcast_in_dim.2 = bf16[8,152,128]{2,1,0:T(8,128)(2,1)} broadcast(bf16[152,128]{1,0:T(8,128)(2,1)S(1)} %reduce_sum.12), dimensions={1,2} | broadcast | bytes 350208 | tf_op jit(solution)/shard_map/broadcast_in_dim | solution.py:538
  55.6 3.4 %all-to-all-start.1 = ((bf16[8,152,128]{2,1,0:T(8,128)(2,1)}), bf16[8,152,128]{2,1,0:T(8,128)(2,1)S(1)}, u32[]{:S(2)}, u32[]{:S(2)}) async-start(bf16[8,152,128]{2,1,0:T(8,128)(2,1)} %broadcast_in_dim.2), calls=%async_computation.1 | async-start | bytes 622592 | tf_op jit(solution)/shard_map/all_to_all | solution.py:539
  59.1 2.0 %collective-permute-start.5 = (bf16[12,4,384]{2,1,0:T(4,128)(2,1)S(1)}, bf16[12,4,384]{2,1,0:T(4,128)(2,1)S(1)}, u32[]{:S(2)}, u32[]{:S(2)}) collective-permute-start(bf16[12,4,384]{2,1,0:T(4,128)(2,1)S(1)} %slice.38), channel_id=1, source_target_pairs={{0,2},{2,0},{4,6},{6,4},{8,10},{10,8},{12,14},{14,12},{16,18},{18,... | collective-permute-start | bytes 110600 | tf_op jit(solution)/shard_map/ppermute | solution.py:521
  61.2 0.1 collective-permute-start.3
  61.2 1.6 %collective-permute-start.4 = (bf16[4,28,384]{2,1,0:T(8,128)(2,1)S(1)}, bf16[4,28,384]{2,1,0:T(8,128)(2,1)S(1)}, u32[]{:S(2)}, u32[]{:S(2)}) collective-permute-start(bf16[4,28,384]{2,1,0:T(8,128)(2,1)S(1)} %slice.37), channel_id=1, source_target_pairs={{0,4},{2,6},{4,8},{6,10},{8,12},{10,14},{12,16},{14,18},{16,20},{1... | collective-permute-start | bytes 258056 | tf_op jit(solution)/shard_map/ppermute | solution.py:522
  62.8 0.8 %collective-permute-done.5 = bf16[12,4,384]{2,1,0:T(4,128)(2,1)S(1)} collective-permute-done((bf16[12,4,384]{2,1,0:T(4,128)(2,1)S(1)}, bf16[12,4,384]{2,1,0:T(4,128)(2,1)S(1)}, u32[]{:S(2)}, u32[]{:S(2)}) %collective-permute-start.5) | collective-permute-done | bytes 36896 | tf_op jit(solution)/shard_map/ppermute | solution.py:521
  63.6 0.1 maximum_bitcast_fusion
  63.7 5.7 %all-to-all-done.1 = bf16[8,152,128]{2,1,0:T(8,128)(2,1)S(1)} async-done(((bf16[8,152,128]{2,1,0:T(8,128)(2,1)}), bf16[8,152,128]{2,1,0:T(8,128)(2,1)S(1)}, u32[]{:S(2)}, u32[]{:S(2)}) %all-to-all-start.1) | async-done | bytes 311328 | tf_op jit(solution)/shard_map/all_to_all | solution.py:539
  69.4 0.0 collective-permute-start.7
  69.4 0.0 collective-permute-done.3
  69.5 0.8 %add_convert_fusion.1 = bf16[1,16,32,384]{3,2,1,0:T(8,128)(2,1)} fusion(bf16[1,16,32,384]{3,2,1,0:T(8,128)(2,1)S(1)} %copy-done, bf16[1,12,32,384]{3,2,1,0:T(8,128)(2,1)S(1)} %maximum_bitcast_fusion, bf16[1,4,32,384]{3,2,1,0:T(8,128)(2,1)S(1)} %maximum_bitcast_fusion.1), kind=kLoop, calls=%fused_computation.2 | loop fusion | flops 983040 | bytes 1179648 | tf_op jit(solution)/shard_map/convert_element_type | solution.py:529
  70.3 0.7 collective-permute-done.7.theirs
  71.0 0.7 copy-done.3
  71.8 2.3 %finish.1 = (f32[576,384]{1,0:T(8,128)}, f32[192,384]{1,0:T(8,128)}, f32[12,225]{1,0:T(8,128)}, f32[12]{0:T(128)}, f32[384]{0:T(512)}) custom-call(f32[12]{0:T(128)} %limit.3, bf16[1216,128]{1,0:T(8,128)(2,1)} %bitcast.10, bf16[1216,128]{1,0:T(8,128)(2,1)} %copy-done.3, f32[12,225]{1,0:T(8,128)} %logits.3), custom_call_target="tpu_custom_call" | custom-call | tf_op jit(solution)/shard_map/finish/pallas_call | solution.py:458
  (16 shorter events, 0.2 us)
Async XLA Ops:
  0.6 1.1 %copy-start = (bf16[1,16,32,384]{3,2,1,0:T(8,128)(2,1)S(1)}, bf16[1,16,32,384]{3,2,1,0:T(8,128)(2,1)}, u32[]{:S(2)}) copy-start(bf16[1,16,32,384]{3,2,1,0:T(8,128)(2,1)} %param.8) | copy-start | bytes 1179652
  1.8 9.4 %collective-permute-start.1 = (bf16[2,4,32,384]{3,2,1,0:T(8,128)(2,1)S(1)}, bf16[2,4,32,384]{3,2,1,0:T(8,128)(2,1)S(1)}, u32[]{:S(2)}, u32[]{:S(2)}) collective-permute-start(bf16[2,4,32,384]{3,2,1,0:T(8,128)(2,1)S(1)} %slice.43), channel_id=1, source_target_pairs={{0,28},{2,30},{4,0},{6,2},{8,4},{10,6},{12,8},{14,10},{16,12},{18,... | collective-permute-start | bytes 589832 | tf_op jit(solution)/shard_map/ppermute | solution.py:506
  6.4 4.7 %collective-permute-start = (bf16[2,16,4,384]{3,2,1,0:T(4,128)(2,1)S(1)}, bf16[2,16,4,384]{3,2,1,0:T(4,128)(2,1)S(1)}, u32[]{:S(2)}, u32[]{:S(2)}) collective-permute-start(bf16[2,16,4,384]{3,2,1,0:T(4,128)(2,1)S(1)} %slice.41), channel_id=1, source_target_pairs={{0,2},{2,0},{4,6},{6,4},{8,10},{10,8},{12,14},{14,12},{16,18},{18,... | collective-permute-start | bytes 294920 | tf_op jit(solution)/shard_map/ppermute | solution.py:507
  8.0 3.3 %collective-permute-start.2 = (bf16[2,4,4,384]{3,2,1,0:T(4,128)(2,1)S(1)}, bf16[2,4,4,384]{3,2,1,0:T(4,128)(2,1)S(1)}, u32[]{:S(2)}, u32[]{:S(2)}) collective-permute-start(bf16[2,4,4,384]{3,2,1,0:T(4,128)(2,1)S(1)} %slice.45), channel_id=1, source_target_pairs={{0,30},{2,28},{4,2},{6,0},{8,6},{10,4},{12,10},{14,8},{16,14},{18,... | collective-permute-start | bytes 73736 | tf_op jit(solution)/shard_map/ppermute | solution.py:508
  27.4 2.3 %collective-permute-start.6 = (bf16[2,1216,128]{2,1,0:T(8,128)(2,1)}, bf16[2,1216,128]{2,1,0:T(8,128)(2,1)S(1)}, u32[]{:S(2)}, u32[]{:S(2)}) collective-permute-start(bf16[2,1216,128]{2,1,0:T(8,128)(2,1)} %get-tuple-element.16), channel_id=1, source_target_pairs={{0,4},{4,0},{1,5},{5,1},{2,6},{6,2},{3,7},{7,3},{8,12},{12,8},{9,1... | collective-permute-start | bytes 1867784 | tf_op jit(solution)/shard_map/ppermute | solution.py:532
  54.8 4.3 %copy-start.2 = (bf16[16,32,384]{2,1,0:T(8,128)(2,1)S(1)}, bf16[16,32,384]{2,1,0:T(8,128)(2,1)}, u32[]{:S(2)}) copy-start(bf16[16,32,384]{2,1,0:T(8,128)(2,1)} %get-tuple-element.14) | copy-start | bytes 1179652
  55.6 13.8 %all-to-all-start.1 = ((bf16[8,152,128]{2,1,0:T(8,128)(2,1)}), bf16[8,152,128]{2,1,0:T(8,128)(2,1)S(1)}, u32[]{:S(2)}, u32[]{:S(2)}) async-start(bf16[8,152,128]{2,1,0:T(8,128)(2,1)} %broadcast_in_dim.2), calls=%async_computation.1 | async-start | bytes 622592 | tf_op jit(solution)/shard_map/all_to_all | solution.py:539
  59.1 4.5 %collective-permute-start.5 = (bf16[12,4,384]{2,1,0:T(4,128)(2,1)S(1)}, bf16[12,4,384]{2,1,0:T(4,128)(2,1)S(1)}, u32[]{:S(2)}, u32[]{:S(2)}) collective-permute-start(bf16[12,4,384]{2,1,0:T(4,128)(2,1)S(1)} %slice.38), channel_id=1, source_target_pairs={{0,2},{2,0},{4,6},{6,4},{8,10},{10,8},{12,14},{14,12},{16,18},{18,... | collective-permute-start | bytes 110600 | tf_op jit(solution)/shard_map/ppermute | solution.py:521
  61.2 8.3 %collective-permute-start.3 = (bf16[4,4,384]{2,1,0:T(4,128)(2,1)S(1)}, bf16[4,4,384]{2,1,0:T(4,128)(2,1)S(1)}, u32[]{:S(2)}, u32[]{:S(2)}) collective-permute-start(bf16[4,4,384]{2,1,0:T(4,128)(2,1)S(1)} %slice.36), channel_id=1, source_target_pairs={{0,6},{2,4},{4,10},{6,8},{8,14},{10,12},{12,18},{14,16},{16,22},{1... | collective-permute-start | bytes 36872 | tf_op jit(solution)/shard_map/ppermute | solution.py:523
  61.2 8.2 %collective-permute-start.4 = (bf16[4,28,384]{2,1,0:T(8,128)(2,1)S(1)}, bf16[4,28,384]{2,1,0:T(8,128)(2,1)S(1)}, u32[]{:S(2)}, u32[]{:S(2)}) collective-permute-start(bf16[4,28,384]{2,1,0:T(8,128)(2,1)S(1)} %slice.37), channel_id=1, source_target_pairs={{0,4},{2,6},{4,8},{6,10},{8,12},{10,14},{12,16},{14,18},{16,20},{1... | collective-permute-start | bytes 258056 | tf_op jit(solution)/shard_map/ppermute | solution.py:522
  69.4 1.6 %copy-start.1 = (bf16[8,152,128]{2,1,0:T(8,128)(2,1)}, bf16[8,152,128]{2,1,0:T(8,128)(2,1)S(1)}, u32[]{:S(2)}) copy-start(bf16[8,152,128]{2,1,0:T(8,128)(2,1)S(1)} %all-to-all-done.1) | copy-start | bytes 933892
  69.4 1.6 %collective-permute-start.7 = (bf16[1216,128]{1,0:T(8,128)(2,1)S(1)}, bf16[1216,128]{1,0:T(8,128)(2,1)S(1)}, u32[]{:S(2)}, u32[]{:S(2)}) collective-permute-start(bf16[1216,128]{1,0:T(8,128)(2,1)S(1)} %bitcast.9), channel_id=1, source_target_pairs={{0,4},{4,0},{1,5},{5,1},{2,6},{6,2},{3,7},{7,3},{8,12},{12,8},{9,1... | collective-permute-start | bytes 933896 | tf_op jit(solution)/shard_map/ppermute | solution.py:541
  71.0 0.7 copy-start.3

commit v3 on v2

--- a/solution.py
+++ b/solution.py
@@ -1,3 +1,4 @@
+import functools
 import math
 
 import jax
@@ -15,11 +16,9 @@
 MASK_FILL = -100.0
 SCALE_CAP = math.log(100.0)
 BIAS_RANGE = 16.0
-PROJECT_UNROLL = 4
-FORWARD_UNROLL = 4
-NORM_UNROLL = 4
-FLATTEN_UNROLL = 4
-BACKWARD_UNROLL = 4
+LOG2_E = math.log2(math.e)
+VMEM_MAIN = 36 << 20
+VMEM_LAST = 12 << 20
 F32 = jnp.float32
 BF16 = jnp.bfloat16
 
@@ -65,7 +64,20 @@
     return near.astype(F32).astype(BF16), far.astype(F32).astype(BF16)
 
 
-def make_kernel(rows, cols, depth, heads, sent_rows):
+def repeat(count, step, carry=0):
+    for p in range(count):
+        carry = step(p, carry)
+    return carry
+
+
+def pipeline(items, stages):
+    for start in range(len(items) + len(stages) - 1):
+        for back, stage in enumerate(stages):
+            if 0 <= start - back < len(items):
+                stage(*items[start - back])
+
+
+def make_kernel(rows, cols, depth, heads, sent_rows, across, order):
     head_dim = depth // heads
     per_tile = LANES // head_dim
     groups = heads // per_tile
@@ -83,10 +95,18 @@
     small_at = groups * body
     small_rows = sent_rows - small_at
     core_rows = sent_rows // 2
+    edge = WIN // 2
+    pitch = cols + WIN
+    outer, inner, crossed = order
+    chunk = core_rows // across
 
     def kernel(
         limit,
-        img,
+        tok,
+        cot,
+        below,
+        right,
+        corner,
         w_qkv,
         w_proj,
         logits,
@@ -104,7 +124,10 @@
         k_lo,
         val,
         prob,
+        prob_low,
         raw,
+        d_prob,
+        d_low,
         att,
         d_prj,
         d_att,
@@ -116,6 +139,8 @@
         small,
         sums,
         padded,
+        wide_x,
+        wide_u,
     ):
         core = lax.axis_index("hc")
         down = lax.axis_index("hz") * lax.axis_size("hc") + core
@@ -126,8 +151,7 @@
         ones = (iota((wide, wide), 0) // head_dim == iota((wide, wide), 1) // head_dim).astype(F32)
         ones = ones.astype(BF16)
         owner = iota((1, wide), 1) % LANES // head_dim
-        head_f32 = [(owner == h).astype(F32) for h in range(per_tile)]
-        head_low = [m.astype(BF16) for m in head_f32]
+        head_low = [(owner == h).astype(F32).astype(BF16) for h in range(per_tile)]
         top_rows = (iota((pair, LANES), 0) < TOKENS).astype(F32)
         top_rows, low_rows = top_rows.astype(BF16), (1.0 - top_rows).astype(BF16)
         left_lanes = half.astype(F32)
@@ -138,17 +162,39 @@
             scale = jnp.where(by_head == h, limit[h], scale)
         scale = jnp.exp(jnp.minimum(scale, SCALE_CAP))
 
+        for which, (own, wide_of) in enumerate(((tok, wide_x), (cot, wide_u))):
+            edges = right[which].astype(F32)
+            ends = corner[which].astype(F32)
+            for i in range(rows):
+                if i + edge < rows:
+                    row = own[0, i + edge].astype(F32)
+                    side = edges[(i + edge) * edge : (i + edge + 1) * edge]
+                else:
+                    row = below[which, i + edge - rows].astype(F32)
+                    side = ends[(i + edge - rows) * edge : (i + edge - rows + 1) * edge]
+                at = i * pitch
+                for j in range(groups):
+                    tile = slice(j * LANES, (j + 1) * LANES)
+                    wide_of[j, at : at + cols, :] = row[:, tile]
+                    wide_of[j, at + cols : at + cols + edge, :] = side[:, tile]
+
+        def window_rows(wide_of, p):
+            tiles = []
+            for j in range(groups):
+                pieces = []
+                for w in range(2):
+                    i0 = p // pairs_across * WIN
+                    j0 = (p % pairs_across * 2 + w) * WIN + edge
+                    for r in range(WIN):
+                        at = (i0 + r) * pitch + j0
+                        pieces.append(wide_of[j, at : at + WIN, :])
+                tiles.append(jnp.concatenate(pieces, axis=0))
+            return jnp.concatenate(tiles, axis=1)
+
         def project(p, carry):
-            place = pl.ds(pl.multiple_of(p * pair, pair), pair)
-            pieces, ups = [], []
-            for w in range(2):
-                i0 = p // pairs_across * WIN
-                j0 = pl.multiple_of((p % pairs_across * 2 + w) * WIN, WIN)
-                for r in range(WIN):
-                    pieces.append(img[0, i0 + r, pl.ds(j0, WIN), :].astype(F32))
-                    ups.append(img[1, i0 + r, pl.ds(j0, WIN), :].astype(F32))
-            x = jnp.concatenate(pieces, axis=0).astype(BF16)
-            uf[place, :] = jnp.concatenate(ups, axis=0)
+            place = pl.ds(p * pair, pair)
+            x = window_rows(wide_x, p).astype(BF16)
+            uf[place, :] = window_rows(wide_u, p)
             xb[place, :] = x
             qkv = dot_nn(x, w_qkv[...]).astype(BF16)
             val[place, :] = qkv[:, 2 * depth :]
@@ -162,13 +208,13 @@
             k_hi[place, :], k_lo[place, :] = split(unit[:, depth:])
             return carry
 
-        lax.fori_loop(0, pairs, project, 0, unroll=PROJECT_UNROLL)
+        repeat(pairs, project)
 
         sub = iota((WIN, LANES), 0)
         lane = iota((WIN, LANES), 1)
         near_map, far_map = table_maps(span, 2 * LANES)
         padded[...] = jnp.zeros_like(padded)
-        padded[:heads, : span * span] = jax.nn.sigmoid(logits[...]) * BIAS_RANGE
+        padded[:heads, : span * span] = jax.nn.sigmoid(logits[...]) * (BIAS_RANGE * LOG2_E)
         table = padded[...]
         first = table.astype(BF16)
         second, third = split(table - first.astype(F32))
@@ -185,17 +231,14 @@
                 two = pltpu.roll(line, (LANES + TOKENS - (WIN - 1 - r) * WIN) % LANES, 1)
                 at = h * TOKENS + r * WIN
                 bias[at : at + WIN, :] = jnp.where(half, one, two)
-        d_bias[...] = jnp.zeros_like(d_bias)
-        d_sc[...] = jnp.zeros_like(d_sc)
 
         key = iota((TOKENS, LANES), 0)
         query = iota((TOKENS, LANES), 1) % TOKENS
-        edge = WIN // 2
         split_r = ((key // WIN) >= edge) != ((query // WIN) >= edge)
         split_c = ((key % WIN) >= edge) != ((query % WIN) >= edge)
         split_c = jnp.logical_and(split_c, iota((TOKENS, LANES), 1) >= TOKENS)
-        mask_r = jnp.where(split_r, MASK_FILL, 0.0)
-        mask_c = jnp.where(split_c, MASK_FILL, 0.0)
+        mask_r = jnp.where(split_r, MASK_FILL * LOG2_E, 0.0)
+        mask_c = jnp.where(split_c, MASK_FILL * LOG2_E, 0.0)
 
         def beside(ref, at, tile):
             one = ref[pl.ds(at, TOKENS), tile]
@@ -214,45 +257,53 @@
             return jnp.concatenate([block * left_lanes, block * right_lanes], axis=0)
 
         def gather_heads(out):
-            total = out[:TOKENS] * head_f32[0]
+            total = out[:TOKENS]
             for h in range(1, per_tile):
-                total = total + out[h * TOKENS : (h + 1) * TOKENS] * head_f32[h]
+                total = jnp.where(owner == h, out[h * TOKENS : (h + 1) * TOKENS], total)
             return total
 
-        def forward(p, carry):
-            at = pl.multiple_of(p * pair, pair)
-            row_edge = jnp.where(p // pairs_across == row_windows - 1, last_row, 0)
-            col_edge = jnp.where(p % pairs_across == pairs_across - 1, last_col, 0)
-            mask = jnp.minimum(mask_r * row_edge.astype(F32), mask_c * col_edge.astype(F32))
-            for g in range(groups):
-                tile = slice(g * LANES, (g + 1) * LANES)
-                keys = stack(beside(k_hi, at, tile))
-                keys_low = stack(beside(k_lo, at, tile))
-                queries = turned(q_low, at, tile)
-                score = dot_nn(keys, queries) + dot_nn(keys_low, queries)
-                lows = []
-                for h in range(per_tile):
-                    place = slice(h * TOKENS, (h + 1) * TOKENS)
-                    of = (g * per_tile + h) * TOKENS
-                    line = (g * per_tile + h) * head_dim
-                    s = score[place] * q_turn[p, line : line + 1, :]
-                    raw[p, g, place, :] = s
-                    s = s + (bias[of : of + TOKENS, :] + mask)
-                    e = jnp.exp(s - jnp.max(s, axis=0, keepdims=True))
-                    pr = e * (1.0 / jnp.sum(e, axis=0, keepdims=True))
-                    prob[p, g, place, :] = pr
-                    lows.append(pr.astype(BF16))
-                out = dot_tn(jnp.concatenate(lows, axis=0), stack(beside(val, at, tile)))
-                att[pl.ds(at, TOKENS), tile] = out[:TOKENS, :LANES].astype(BF16)
-                att[pl.ds(at + TOKENS, TOKENS), tile] = out[TOKENS:, LANES:].astype(BF16)
-            return carry
-
-        lax.fori_loop(0, pairs, forward, 0, unroll=FORWARD_UNROLL)
+        tiles = [(p, g) for p in range(pairs) for g in range(groups)]
+
+        def lanes_of(g):
+            return slice(g * LANES, (g + 1) * LANES)
+
+        def score(p, g):
+            keys = stack(beside(k_hi, p * pair, lanes_of(g)))
+            keys_low = stack(beside(k_lo, p * pair, lanes_of(g)))
+            queries = turned(q_low, p * pair, lanes_of(g))
+            raw[p, g] = dot_nn(keys, queries) + dot_nn(keys_low, queries)
+
+        def soften(p, g):
+            masks = []
+            if p // pairs_across == row_windows - 1:
+                masks.append(mask_r * last_row.astype(F32))
+            if p % pairs_across == pairs_across - 1:
+                masks.append(mask_c * last_col.astype(F32))
+            for h in range(per_tile):
+                place = slice(h * TOKENS, (h + 1) * TOKENS)
+                head = g * per_tile + h
+                line = q_turn[p, head * head_dim : head * head_dim + 1, :] * LOG2_E
+                added = bias[head * TOKENS : (head + 1) * TOKENS, :]
+                if masks:
+                    added = added + functools.reduce(jnp.minimum, masks)
+                s = raw[p, g, place, :] * line + added
+                e = jnp.exp2(s - jnp.max(s, axis=0, keepdims=True))
+                pr = e * (1.0 / jnp.sum(e, axis=0, keepdims=True))
+                prob[p, g, place, :] = pr
+                prob_low[p, g, place, :] = pr.astype(BF16)
+
+        def attend(p, g):
+            at, tile = p * pair, lanes_of(g)
+            out = dot_tn(prob_low[p, g], stack(beside(val, at, tile)))
+            att[at : at + TOKENS, tile] = out[:TOKENS, :LANES].astype(BF16)
+            att[at + TOKENS : at + pair, tile] = out[TOKENS:, LANES:].astype(BF16)
+
+        pipeline(tiles, (score, soften, attend))
 
         gains = gain[...].reshape(1, depth)
 
         def norm(p, d_gain):
-            place = pl.ds(pl.multiple_of(p * pair, pair), pair)
+            place = pl.ds(p * pair, pair)
             proj = dot_nn(att[place, :], w_proj[...])
             centre = proj - jnp.mean(proj, -1, keepdims=True)
             std = lax.rsqrt(jnp.mean(centre * centre, -1, keepdims=True) + EPS_NORM)
@@ -267,59 +318,62 @@
             d_prj[place, :] = d_p
             return d_gain
 
-        d_gain = lax.fori_loop(0, pairs, norm, jnp.zeros((1, depth), F32), unroll=NORM_UNROLL)
+        d_gain = repeat(pairs, norm, jnp.zeros((1, depth), F32))
 
         w_proj_turned = w_proj[...].T
 
         def spread(p, carry):
-            place = pl.ds(pl.multiple_of(p * pair, pair), pair)
+            place = pl.ds(p * pair, pair)
             d_att[place, :] = dot_nn(d_prj[place, :], w_proj_turned).astype(BF16)
             return carry
 
-        lax.fori_loop(0, pairs, spread, 0, unroll=NORM_UNROLL)
-
-        def backward(p, carry):
-            at = pl.multiple_of(p * pair, pair)
-            for g in range(groups):
-                tile = slice(g * LANES, (g + 1) * LANES)
-                key_tile = slice(depth + g * LANES, depth + (g + 1) * LANES)
-                val_tile = slice(2 * depth + g * LANES, 2 * depth + (g + 1) * LANES)
-                values = stack(beside(val, at, tile))
-                ups = diagonal(d_att, at, tile)
-                d_pr = dot_nn(values, turned(d_att, at, tile))
-                lows, d_lows = [], []
-                for h in range(per_tile):
-                    place = slice(h * TOKENS, (h + 1) * TOKENS)
-                    of = (g * per_tile + h) * TOKENS
-                    pr = prob[p, g, place, :]
-                    pd = pr * d_pr[place]
-                    d_s = pd - pr * jnp.sum(pd, axis=0, keepdims=True)
-                    d_bias[of : of + TOKENS, :] += d_s
-                    by_scale = (d_s * raw[p, g, place, :]).reshape(WIN, WIN, LANES)
-                    head = g * per_tile + h
-                    d_sc[head * WIN : (head + 1) * WIN, :] += jnp.sum(by_scale, axis=0)
-                    lows.append(pr.astype(BF16))
-                    line = head * head_dim
-                    d_lows.append((d_s * q_turn[p, line : line + 1, :]).astype(BF16))
-                low = jnp.concatenate(lows, axis=0)
-                d_low = jnp.concatenate(d_lows, axis=0)
-                d_v = gather_heads(dot_nn(low, ups)).astype(BF16)
-                d_qkv[pl.ds(at, TOKENS), val_tile] = d_v[:, :LANES]
-                d_qkv[pl.ds(at + TOKENS, TOKENS), val_tile] = d_v[:, LANES:]
-                d_k = gather_heads(dot_nn(d_low, diagonal(q_low, at, tile)))
-                d_unit[pl.ds(at, TOKENS), key_tile] = d_k[:, :LANES]
-                d_unit[pl.ds(at + TOKENS, TOKENS), key_tile] = d_k[:, LANES:]
-                d_q = dot_tn(d_low, stack(beside(k_hi, at, tile)))
-                d_unit[pl.ds(at, TOKENS), tile] = d_q[:TOKENS, :LANES]
-                d_unit[pl.ds(at + TOKENS, TOKENS), tile] = d_q[TOKENS:, LANES:]
-            return carry
-
-        lax.fori_loop(0, pairs, backward, 0, unroll=BACKWARD_UNROLL)
+        repeat(pairs, spread)
+
+        def rise(p, g):
+            values = stack(beside(val, p * pair, lanes_of(g)))
+            d_prob[p, g] = dot_nn(values, turned(d_att, p * pair, lanes_of(g)))
+
+        def harden(p, g):
+            for h in range(per_tile):
+                place = slice(h * TOKENS, (h + 1) * TOKENS)
+                head = g * per_tile + h
+                of = slice(head * TOKENS, (head + 1) * TOKENS)
+                pr = prob[p, g, place, :]
+                pd = pr * d_prob[p, g, place, :]
+                d_s = pd - pr * jnp.sum(pd, axis=0, keepdims=True)
+                if p == 0:
+                    d_bias[of, :] = d_s
+                else:
+                    d_bias[of, :] += d_s
+                d_s = d_s * q_turn[p, head * head_dim : head * head_dim + 1, :]
+                by_scale = (d_s * raw[p, g, place, :]).reshape(WIN, WIN, LANES)
+                of = slice(head * WIN, (head + 1) * WIN)
+                if p == 0:
+                    d_sc[of, :] = jnp.sum(by_scale, axis=0)
+                else:
+                    d_sc[of, :] += jnp.sum(by_scale, axis=0)
+                d_low[p, g, place, :] = d_s.astype(BF16)
+
+        def fall(p, g):
+            at, tile = p * pair, lanes_of(g)
+            key_tile = slice(depth + g * LANES, depth + (g + 1) * LANES)
+            val_tile = slice(2 * depth + g * LANES, 2 * depth + (g + 1) * LANES)
+            d_v = gather_heads(dot_nn(prob_low[p, g], diagonal(d_att, at, tile))).astype(BF16)
+            d_qkv[at : at + TOKENS, val_tile] = d_v[:, :LANES]
+            d_qkv[at + TOKENS : at + pair, val_tile] = d_v[:, LANES:]
+            d_k = gather_heads(dot_nn(d_low[p, g], diagonal(q_low, at, tile)))
+            d_unit[at : at + TOKENS, key_tile] = d_k[:, :LANES]
+            d_unit[at + TOKENS : at + pair, key_tile] = d_k[:, LANES:]
+            d_q = dot_tn(d_low[p, g], stack(beside(k_hi, at, tile)))
+            d_unit[at : at + TOKENS, tile] = d_q[:TOKENS, :LANES]
+            d_unit[at + TOKENS : at + pair, tile] = d_q[TOKENS:, LANES:]
+
+        pipeline(tiles, (rise, harden, fall))
 
         w_qkv_turned = w_qkv[...].T
 
         def flatten(p, carry):
-            place = pl.ds(pl.multiple_of(p * pair, pair), pair)
+            place = pl.ds(p * pair, pair)
             unit = unit_s[place, :]
             d_u = d_unit[place, :]
             d_u = d_u - unit * group_sum(unit * d_u, ones, False)
@@ -328,23 +382,23 @@
             flat = dot_nn(d_qkv[place, :], w_qkv_turned)
             for w in range(2):
                 i0 = p // pairs_across * WIN
-                j0 = pl.multiple_of((p % pairs_across * 2 + w) * WIN, WIN)
+                j0 = (p % pairs_across * 2 + w) * WIN
                 for r in range(WIN):
                     piece = flat[w * TOKENS + r * WIN : w * TOKENS + (r + 1) * WIN]
                     d_img[i0 + r, pl.ds(j0, WIN), :] = piece.astype(BF16)
             return carry
 
-        lax.fori_loop(0, pairs, flatten, 0, unroll=FLATTEN_UNROLL)
+        repeat(pairs, flatten)
 
         d_wp = dot_tn(d_prj[...], att[...])
         d_wq = dot_tn(d_qkv[...], xb[...])
         for b in range(2):
             for j in range(groups):
                 tile = slice(j * LANES, (j + 1) * LANES)
-                at = j * body
-                sums[b, at : at + half_q, :] = d_wq[b * half_q : (b + 1) * half_q, tile].astype(BF16)
+                at = b * sent_rows + j * body
+                sums[at : at + half_q, :] = d_wq[b * half_q : (b + 1) * half_q, tile].astype(BF16)
                 at = at + half_q
-                sums[b, at : at + half_p, :] = d_wp[b * half_p : (b + 1) * half_p, tile].astype(BF16)
+                sums[at : at + half_p, :] = d_wp[b * half_p : (b + 1) * half_p, tile].astype(BF16)
 
         small[...] = jnp.zeros_like(small)
         for h in range(heads):
@@ -373,14 +427,18 @@
         at = 2 * heads + groups
         small[at : at + 1, :] = line
         for b in range(2):
-            sums[b, small_at:, :] = small[...].astype(BF16)
-        own = pl.multiple_of(core * core_rows, 8)
-        other = pl.multiple_of((1 - core) * core_rows, 8)
-        for b in range(2):
-            mine[b] = sums[b, pl.ds(own, core_rows), :]
-            given[b] = sums[b, pl.ds(other, core_rows), :]
-
-    def call(limit, img, w_qkv, w_proj, logits, gain):
+            at = b * sent_rows + small_at
+            sums[at : at + small_rows, :] = small[...].astype(BF16)
+        for out, whose in ((mine, core), (given, 1 - core)):
+            turn = whose if crossed else 0
+            for f in range(outer):
+                for n in range(inner):
+                    image = f + (n - f) * turn
+                    column = n + (f - n) * turn
+                    at = image * sent_rows + whose * core_rows + column * chunk
+                    out[f, n] = sums[pl.ds(pl.multiple_of(at, 8), chunk), :]
+
+    def call(limit, tok, cot, below, right, corner, w_qkv, w_proj, logits, gain):
         vmem = pltpu.VMEM
         scratch = [
             vmem((tokens, depth), BF16),
@@ -393,7 +451,10 @@
             vmem((tokens, depth), BF16),
             vmem((tokens, depth), BF16),
             vmem((pairs, groups, stacked, LANES), F32),
+            vmem((pairs, groups, stacked, LANES), BF16),
             vmem((pairs, groups, stacked, LANES), F32),
+            vmem((pairs, groups, stacked, LANES), F32),
+            vmem((pairs, groups, stacked, LANES), BF16),
             vmem((tokens, depth), BF16),
             vmem((tokens, depth), BF16),
             vmem((tokens, depth), BF16),
@@ -403,19 +464,22 @@
             vmem((heads * TOKENS, LANES), F32),
             vmem((heads * WIN, LANES), F32),
             vmem((small_rows, LANES), F32),
-            vmem((2, sent_rows, LANES), BF16),
+            vmem((2 * sent_rows, LANES), BF16),
             vmem((16, 2 * LANES), F32),
+            vmem((groups, rows * pitch, LANES), F32),
+            vmem((groups, rows * pitch, LANES), F32),
         ]
-        part = jax.ShapeDtypeStruct((2, core_rows, LANES), BF16)
+        part = jax.ShapeDtypeStruct((outer, inner, chunk, LANES), BF16)
         return pl.pallas_call(
             kernel,
             out_shape=(jax.ShapeDtypeStruct((rows, cols, depth), BF16), part, part),
             in_specs=[pl.BlockSpec(memory_space=pltpu.SMEM)]
-            + [pl.BlockSpec(memory_space=pltpu.VMEM)] * 5,
+            + [pl.BlockSpec(memory_space=pltpu.VMEM)] * 9,
             out_specs=tuple([pl.BlockSpec(memory_space=pltpu.VMEM)] * 3),
             scratch_shapes=scratch,
+            compiler_params=pltpu.CompilerParams(vmem_limit_bytes=VMEM_MAIN),
             name="block_grads",
-        )(limit, img, w_qkv, w_proj, logits, gain)
+        )(limit, tok, cot, below, right, corner, w_qkv, w_proj, logits, gain)
 
     return call
 
@@ -467,6 +531,7 @@
         in_specs=[pl.BlockSpec(memory_space=pltpu.SMEM), vmem, vmem, vmem],
         out_specs=(vmem,) * 5,
         scratch_shapes=[pltpu.VMEM((2 * core_rows, LANES), F32)],
+        compiler_params=pltpu.CompilerParams(vmem_limit_bytes=VMEM_LAST),
         name="finish",
     )(limit, ours, theirs, logits)
 
@@ -498,25 +563,55 @@
     return move
 
 
+FACE = ("hc", "wa", "ba")
+
+
+def over(turn, by, crossed):
+    def move(where, sizes):
+        axis = 2 - (turn + (where[0] if crossed else 0)) % 2
+        where = list(where)
+        where[axis] = (where[axis] + by) % sizes[axis]
+        return where
+
+    return move
+
+
+def along(by):
+    return lambda where, sizes: [(where[0] + by) % sizes[0]]
+
+
+def hand_out(blocks, place, axes, move):
+    count = blocks.shape[0]
+    total = lax.dynamic_index_in_dim(blocks, place, 0, keepdims=False).astype(F32)
+    for by in range(count - 1, 0, -1):
+        sent = lax.dynamic_index_in_dim(blocks, (place + by) % count, 0, keepdims=False)
+        total = total + lax.ppermute(sent, axes, route(axes, move(by))).astype(F32)
+    return total.astype(BF16)
+
+
 def shards(tokens, cotangent, w_qkv, w_proj, table_logits, logit_scale, gain):
     images, rows, cols, depth = tokens.shape
     heads = logit_scale.shape[0]
     edge = WIN // 2
     both = jnp.concatenate([tokens, cotangent], 0)
     below = lax.ppermute(both[:, :edge], GRID, route(GRID, step(-1, 0)))
-    beside = lax.ppermute(both[:, :, :edge], GRID, route(GRID, step(0, -1)))
-    corner = lax.ppermute(both[:, :edge, :edge], GRID, route(GRID, step(-1, -1)))
-    main = jnp.concatenate([both[:, edge:, edge:], beside[:, edge:]], 2)
-    last = jnp.concatenate([below[:, :, edge:], corner], 2)
-    moved = jnp.concatenate([main, last], 1)
+    left = both[:, :, :edge].reshape(2, rows * edge, depth)
+    right = lax.ppermute(left, GRID, route(GRID, step(0, -1)))
+    tip = left[:, : edge * edge]
+    corner = lax.ppermute(tip, GRID, route(GRID, step(-1, -1)))
 
     cores, tall, across = lax.axis_size("hc"), lax.axis_size("hz"), lax.axis_size("wa")
+    images_over = lax.axis_size("ba")
     owners = cores * tall * across
     used = 2 * depth // LANES * depth + 2 * heads + depth // LANES + 1
     unit = 8 * owners
     sent = -(-used // unit) * unit
-    call = make_kernel(rows, cols, depth, heads, sent)
-    d_moved, mine, given = call(logit_scale, moved, w_qkv, w_proj, table_logits, gain)
+    crossed = images_over == across
+    order = (images_over, across, crossed)
+    call = make_kernel(rows, cols, depth, heads, sent, across, order)
+    d_moved, mine, given = call(
+        logit_scale, tokens, cotangent, below, right, corner, w_qkv, w_proj, table_logits, gain
+    )
 
     right = lax.ppermute(d_moved[: rows - edge, cols - edge :], GRID, route(GRID, step(0, 1)))
     lower = lax.ppermute(d_moved[rows - edge :, : cols - edge], GRID, route(GRID, step(1, 0)))
@@ -532,11 +627,15 @@
     taken = lax.ppermute(given, "hc", swap)
     summed = (mine.astype(F32) + taken.astype(F32)).astype(BF16)
     piece = sent // owners
-    summed = summed.reshape(2 * tall * across, piece, LANES)
-    parts = lax.all_to_all(summed, ("ba", "hz", "wa"), 0, 0, tiled=True)
-    total = parts.astype(F32).sum(0).astype(BF16)
+    core, column, image = lax.axis_index("hc"), lax.axis_index("wa"), lax.axis_index("ba")
+    turn = core if crossed else 0
+    moves = (lambda by: over(0, by, crossed)), (lambda by: over(1, by, crossed))
+    summed = hand_out(summed, image + (column - image) * turn, FACE, moves[0])
+    summed = hand_out(summed, column + (image - column) * turn, FACE, moves[1])
+    summed = summed.reshape(tall, piece, LANES)
+    total = hand_out(summed, lax.axis_index("hz"), ("hz",), along)
     spread = jnp.broadcast_to(total[None], (tall * across, piece, LANES))
-    ours = lax.all_to_all(spread, ("hz", "wa"), 0, 0, tiled=True)
+    ours = lax.all_to_all(spread, ("wa", "hz"), 0, 0, tiled=True)
     ours = ours.reshape(sent // cores, LANES)
     theirs = lax.ppermute(ours, "hc", swap)
     d_wq, d_wp, d_table, d_scale, d_gain = finish(

time: 74.4 us -> 62.9 us (0.85)
  blocking collectives: 23.9 us -> 0 us
  waiting for transfers between devices: 12.2 us -> 25.1 us
  starting transfers between devices: 13.6 us -> 21.4 us
  Pallas kernels: 17.2 us -> 11.8 us
  other arithmetic: 3.33 us -> 1.29 us
  local copies, waits for them, and re-layouts: 3.03 us -> 2.19 us
    all_to_all x1 -> x0, blocking collectives: 23.9 us -> none  [shards(): parts = lax.all_to_all(summed, ('ba', 'hz', 'wa'), 0, 0, tiled=True)]
    ppermute x2 -> x7, waiting for transfers between devices: 2.68 us -> 16 us  [the longest x5 13 us: hand_out(): total = total + lax.ppermute(sent, axes, route(axes, move(by))).astype(F32)]
    ppermute x2 -> x7, starting transfers between devices: 1.98 us -> 8.86 us  [the longest x5 6.94 us: hand_out(): total = total + lax.ppermute(sent, axes, route(axes, move(by))).astype(F32)]
    pallas_call x1, Pallas kernels: 15 us -> 10 us  [call(): pl.pallas_call(kernel, out_shape=(jax.ShapeDtypeStruct((rows, cols, depth...]
    ppermute x1, starting transfers between devices: 0.06 us -> 1.73 us  [shards(): lax.ppermute(d_moved[rows - edge:, cols - edge:], GRID, route(GRID, step(...]
    ppermute x1, starting transfers between devices: 1.57 us -> 0.06 us  [shards(): lax.ppermute(d_moved[rows - edge:, :cols - edge], GRID, route(GRID, step(...]
    convert_element_type x1, other arithmetic: 1.24 us -> 0.16 us  [shards(): summed = (mine.astype(F32) + taken.astype(F32)).astype(BF16)]
    concatenate x1 -> x0, other arithmetic: 1.03 us -> none  [shards(): moved = jnp.concatenate([main, last], 1)]
  transfers between devices with their start and end apart: 9 -> 14, of which waited for: 6 -> 10; matrix products, arithmetic and copies ran while one was open for 2% -> 2% of each run, Pallas kernels for 0% -> 0%
where the time goes in v3:
time: 62.9 us; the launch traced here: 62.6 us
  waiting for transfers between devices  25.1 us (40%)
  starting transfers between devices  21.4 us (34%)
  Pallas kernels  11.8 us (19%)
  local copies, waits for them, and re-layouts  2.19 us (3%)
  other arithmetic  1.29 us (2%)
  between operations  0.86 us (1%)
    ppermute x5, waiting for transfers between devices, hand_out(): total = total + lax.ppermute(sent, axes, route(axes, move(by))).astype(F32)  13 us
    pallas_call x1, Pallas kernels, call(): pl.pallas_call(kernel, out_shape=(jax.ShapeDtypeStruct((rows, cols, depth...  10 us
    ppermute x5, starting transfers between devices, hand_out(): total = total + lax.ppermute(sent, axes, route(axes, move(by))).astype(F32)  6.94 us
    all_to_all x1, waiting for transfers between devices, shards(): ours = lax.all_to_all(spread, ('wa', 'hz'), 0, 0, tiled=True)  5.05 us
    ppermute x1, starting transfers between devices, shards(): below = lax.ppermute(both[:, :edge], GRID, route(GRID, step(-1, 0)))  4.57 us
    all_to_all x1, starting transfers between devices, shards(): ours = lax.all_to_all(spread, ('wa', 'hz'), 0, 0, tiled=True)  4.12 us
    ppermute x1, waiting for transfers between devices, shards(): corner = lax.ppermute(tip, GRID, route(GRID, step(-1, -1)))  3.02 us
    ppermute x1, waiting for transfers between devices, shards(): taken = lax.ppermute(given, 'hc', swap)  2.26 us
  transfers between devices with their start and end apart: 14, of which 10 were waited for; matrix products, arithmetic and copies ran while one was open for 2% of the time, Pallas kernels for 0%

profile of v3, /device:TPU:0, one launch (start us, length us, event | category | flops | bytes accessed | tf_op | source)
XLA Modules:
  0.0 62.6 jit_solution(8640122171779662040)
XLA Ops:
  0.6 1.1 %constant_dynamic-update-slice_fusion.1 = bf16[2,16,32,384]{3,2,1,0:T(8,128)(2,1)S(1)} fusion(bf16[1,16,32,384]{3,2,1,0:T(8,128)(2,1)} %tok.1), kind=kLoop, calls=%fused_computation.18 | loop fusion | bytes 786432
  1.7 0.0 copy-done
  1.8 0.1 constant_dynamic-update-slice_fusion
  1.9 4.6 %collective-permute-start = (bf16[2,4,32,384]{3,2,1,0:T(8,128)(2,1)S(1)}, bf16[2,4,32,384]{3,2,1,0:T(8,128)(2,1)S(1)}, u32[]{:S(2)}, u32[]{:S(2)}) collective-permute-start(bf16[2,4,32,384]{3,2,1,0:T(8,128)(2,1)S(1)} %slice.28), channel_id=1, source_target_pairs={{0,28},{2,30},{4,0},{6,2},{8,4},{10,6},{12,8},{14,10},{16,12},{18,... | collective-permute-start | bytes 589832 | tf_op jit(solution)/shard_map/ppermute | solution.py:597
  6.5 1.6 %collective-permute-start.1 = (bf16[2,64,384]{2,1,0:T(8,128)(2,1)S(1)}, bf16[2,64,384]{2,1,0:T(8,128)(2,1)S(1)}, u32[]{:S(2)}, u32[]{:S(2)}) collective-permute-start(bf16[2,64,384]{2,1,0:T(8,128)(2,1)S(1)} %reshape.58), channel_id=1, source_target_pairs={{0,2},{2,0},{4,6},{6,4},{8,10},{10,8},{12,14},{14,12},{16,18},{18,... | collective-permute-start | bytes 294920 | tf_op jit(solution)/shard_map/ppermute | solution.py:599
  8.1 0.3 collective-permute-start.2
  8.5 3.0 %collective-permute-done.2.corner = bf16[2,16,384]{2,1,0:T(8,128)(2,1)S(1)} collective-permute-done((bf16[2,16,384]{2,1,0:T(8,128)(2,1)S(1)}, bf16[2,16,384]{2,1,0:T(8,128)(2,1)S(1)}, u32[]{:S(2)}, u32[]{:S(2)}) %collective-permute-start.2) | collective-permute-done | bytes 24608 | tf_op jit(solution)/shard_map/ppermute | solution.py:601
  11.6 10.0 %block_grads.1 = (bf16[16,32,384]{2,1,0:T(8,128)(2,1)S(1)}, bf16[2,2,608,128]{3,2,1,0:T(8,128)(2,1)S(1)}, bf16[2,2,608,128]{3,2,1,0:T(8,128)(2,1)}) custom-call(f32[12]{0:T(128)S(1)} %copy-done.5, bf16[1,16,32,384]{3,2,1,0:T(8,128)(2,1)S(1)} %copy-done.1, bf16[1,16,32,384]{3,2,1,0:T(8,128)(2,1)S(1)} %copy-done, ...), custom_call_target="tpu_custom_call" | custom-call | tf_op jit(solution)/shard_map/block_grads/pallas_call | solution.py:473
  21.6 2.3 %collective-permute-done.6 = bf16[2,2,608,128]{3,2,1,0:T(8,128)(2,1)S(1)} collective-permute-done((bf16[2,2,608,128]{3,2,1,0:T(8,128)(2,1)}, bf16[2,2,608,128]{3,2,1,0:T(8,128)(2,1)S(1)}, u32[]{:S(2)}, u32[]{:S(2)}) %collective-permute-start.6) | collective-permute-done | bytes 622624 | tf_op jit(solution)/shard_map/ppermute | solution.py:627
  23.9 0.2 add_convert_fusion
  24.1 1.6 %collective-permute-start.7 = (bf16[2,608,128]{2,1,0:T(8,128)(2,1)S(1)}, bf16[2,608,128]{2,1,0:T(8,128)(2,1)S(1)}, u32[]{:S(2)}, u32[]{:S(2)}) collective-permute-start(bf16[2,608,128]{2,1,0:T(8,128)(2,1)S(1)} %dynamic-slice_bitcast_fusion), channel_id=1, source_target_pairs={{0,1},{1,0},{2,3},{3,2},{4,6},{5,7},{6,4},{7,5},{8,9},{9,8},{10,11... | collective-permute-start | bytes 933896 | tf_op jit(solution)/shard_map/ppermute | solution.py:588
  25.6 5.4 %collective-permute-done.7 = bf16[2,608,128]{2,1,0:T(8,128)(2,1)S(1)} collective-permute-done((bf16[2,608,128]{2,1,0:T(8,128)(2,1)S(1)}, bf16[2,608,128]{2,1,0:T(8,128)(2,1)S(1)}, u32[]{:S(2)}, u32[]{:S(2)}) %collective-permute-start.7) | collective-permute-done | bytes 311328 | tf_op jit(solution)/shard_map/ppermute | solution.py:588
  31.0 0.1 fusion
  31.2 1.5 %collective-permute-start.8 = (bf16[608,128]{1,0:T(8,128)(2,1)S(1)}, bf16[608,128]{1,0:T(8,128)(2,1)S(1)}, u32[]{:S(2)}, u32[]{:S(2)}) collective-permute-start(bf16[608,128]{1,0:T(8,128)(2,1)S(1)} %dynamic-slice_bitcast_fusion.1), channel_id=1, source_target_pairs={{0,2},{1,3},{2,0},{3,1},{4,5},{5,4},{6,7},{7,6},{8,10},{9,11},{10,... | collective-permute-start | bytes 466952 | tf_op jit(solution)/shard_map/ppermute | solution.py:588
  32.7 3.8 %collective-permute-done.8 = bf16[608,128]{1,0:T(8,128)(2,1)S(1)} collective-permute-done((bf16[608,128]{1,0:T(8,128)(2,1)S(1)}, bf16[608,128]{1,0:T(8,128)(2,1)S(1)}, u32[]{:S(2)}, u32[]{:S(2)}) %collective-permute-start.8) | collective-permute-done | bytes 155680 | tf_op jit(solution)/shard_map/ppermute | solution.py:588
  36.5 0.1 collective-permute-start.11
  36.6 3.7 %collective-permute-start.10 = (bf16[152,128]{1,0:T(8,128)(2,1)S(1)}, bf16[152,128]{1,0:T(8,128)(2,1)S(1)}, u32[]{:S(2)}, u32[]{:S(2)}) collective-permute-start(bf16[152,128]{1,0:T(8,128)(2,1)S(1)} %get-tuple-element.24), channel_id=1, source_target_pairs={{0,16},{8,24},{16,0},{24,8},{1,17},{9,25},{17,1},{25,9},{2,18},{10... | collective-permute-start | bytes 116744 | tf_op jit(solution)/shard_map/ppermute | solution.py:588
  40.2 0.2 collective-permute-start.9
  40.4 2.1 %collective-permute-done.11 = bf16[152,128]{1,0:T(8,128)(2,1)S(1)} collective-permute-done((bf16[152,128]{1,0:T(8,128)(2,1)S(1)}, bf16[152,128]{1,0:T(8,128)(2,1)S(1)}, u32[]{:S(2)}, u32[]{:S(2)}) %collective-permute-start.11) | collective-permute-done | bytes 38944 | tf_op jit(solution)/shard_map/ppermute | solution.py:588
  42.5 0.6 collective-permute-done.10
  43.0 1.2 %collective-permute-done.9 = bf16[152,128]{1,0:T(8,128)(2,1)S(1)} collective-permute-done((bf16[152,128]{1,0:T(8,128)(2,1)S(1)}, bf16[152,128]{1,0:T(8,128)(2,1)S(1)}, u32[]{:S(2)}, u32[]{:S(2)}) %collective-permute-start.9) | collective-permute-done | bytes 38944 | tf_op jit(solution)/shard_map/ppermute | solution.py:588
  44.3 0.8 %broadcast_in_dim.2 = bf16[8,152,128]{2,1,0:T(8,128)(2,1)} broadcast(bf16[152,128]{1,0:T(8,128)(2,1)S(1)} %fusion.4), dimensions={1,2} | broadcast | bytes 350208 | tf_op jit(solution)/shard_map/broadcast_in_dim | solution.py:637
  45.0 4.1 %all-to-all-start = ((bf16[8,152,128]{2,1,0:T(8,128)(2,1)}), bf16[8,152,128]{2,1,0:T(8,128)(2,1)S(1)}, u32[]{:S(2)}, u32[]{:S(2)}) async-start(bf16[8,152,128]{2,1,0:T(8,128)(2,1)} %broadcast_in_dim.2), calls=%async_computation | async-start | bytes 622592 | tf_op jit(solution)/shard_map/all_to_all | solution.py:638
  49.2 2.1 %collective-permute-start.5 = (bf16[12,4,384]{2,1,0:T(4,128)(2,1)S(1)}, bf16[12,4,384]{2,1,0:T(4,128)(2,1)S(1)}, u32[]{:S(2)}, u32[]{:S(2)}) collective-permute-start(bf16[12,4,384]{2,1,0:T(4,128)(2,1)S(1)} %slice.26), channel_id=1, source_target_pairs={{0,2},{2,0},{4,6},{6,4},{8,10},{10,8},{12,14},{14,12},{16,18},{18,... | collective-permute-start | bytes 110600 | tf_op jit(solution)/shard_map/ppermute | solution.py:616
  51.3 0.1 collective-permute-start.4
  51.4 1.7 %collective-permute-start.3 = (bf16[4,4,384]{2,1,0:T(4,128)(2,1)S(1)}, bf16[4,4,384]{2,1,0:T(4,128)(2,1)S(1)}, u32[]{:S(2)}, u32[]{:S(2)}) collective-permute-start(bf16[4,4,384]{2,1,0:T(4,128)(2,1)S(1)} %slice.24), channel_id=1, source_target_pairs={{0,6},{2,4},{4,10},{6,8},{8,14},{10,12},{12,18},{14,16},{16,22},{1... | collective-permute-start | bytes 36872 | tf_op jit(solution)/shard_map/ppermute | solution.py:618
  53.1 1.0 %collective-permute-done.5 = bf16[12,4,384]{2,1,0:T(4,128)(2,1)S(1)} collective-permute-done((bf16[12,4,384]{2,1,0:T(4,128)(2,1)S(1)}, bf16[12,4,384]{2,1,0:T(4,128)(2,1)S(1)}, u32[]{:S(2)}, u32[]{:S(2)}) %collective-permute-start.5) | collective-permute-done | bytes 36896 | tf_op jit(solution)/shard_map/ppermute | solution.py:616
  54.1 0.1 maximum_bitcast_fusion
  54.2 5.1 %all-to-all-done = bf16[8,152,128]{2,1,0:T(8,128)(2,1)S(1)} async-done(((bf16[8,152,128]{2,1,0:T(8,128)(2,1)}), bf16[8,152,128]{2,1,0:T(8,128)(2,1)S(1)}, u32[]{:S(2)}, u32[]{:S(2)}) %all-to-all-start) | async-done | bytes 311328 | tf_op jit(solution)/shard_map/all_to_all | solution.py:638
  59.3 0.8 %add_convert_fusion.1 = bf16[1,16,32,384]{3,2,1,0:T(8,128)(2,1)} fusion(bf16[1,16,32,384]{3,2,1,0:T(8,128)(2,1)S(1)} %copy-done, bf16[1,12,32,384]{3,2,1,0:T(8,128)(2,1)S(1)} %maximum_bitcast_fusion, bf16[1,4,32,384]{3,2,1,0:T(8,128)(2,1)S(1)} %maximum_bitcast_fusion.1), kind=kLoop, calls=%fused_computation.1 | loop fusion | flops 983040 | bytes 1179648 | tf_op jit(solution)/shard_map/convert_element_type | solution.py:624
  60.2 0.7 %collective-permute-done.12.theirs = bf16[1216,128]{1,0:T(8,128)(2,1)S(1)} collective-permute-done((bf16[1216,128]{1,0:T(8,128)(2,1)S(1)}, bf16[1216,128]{1,0:T(8,128)(2,1)S(1)}, u32[]{:S(2)}, u32[]{:S(2)}) %collective-permute-start.12) | collective-permute-done | bytes 311328 | tf_op jit(solution)/shard_map/ppermute | solution.py:640
  60.9 1.8 %finish.1 = (f32[576,384]{1,0:T(8,128)}, f32[192,384]{1,0:T(8,128)}, f32[12,225]{1,0:T(8,128)}, f32[12]{0:T(128)}, f32[384]{0:T(512)}) custom-call(f32[12]{0:T(128)S(1)} %copy-done.5, bf16[1216,128]{1,0:T(8,128)(2,1)S(1)} %bitcast.28, bf16[1216,128]{1,0:T(8,128)(2,1)S(1)} %collective-permute-done.12.theirs, f32[12,225]{1,0:T(8,128)S(1)} %copy-done.4), custom_call_target="tpu_custom_call" | custom-call | tf_op jit(solution)/shard_map/finish/pallas_call | solution.py:522
  (33 shorter events, 0.4 us)
Async XLA Ops:
  0.6 1.1 %copy-start = (bf16[1,16,32,384]{3,2,1,0:T(8,128)(2,1)S(1)}, bf16[1,16,32,384]{3,2,1,0:T(8,128)(2,1)}, u32[]{:S(2)}) copy-start(bf16[1,16,32,384]{3,2,1,0:T(8,128)(2,1)} %cot.1) | copy-start | bytes 1179652
  1.7 9.8 %copy-start.1 = (bf16[1,16,32,384]{3,2,1,0:T(8,128)(2,1)S(1)}, bf16[1,16,32,384]{3,2,1,0:T(8,128)(2,1)}, u32[]{:S(2)}) copy-start(bf16[1,16,32,384]{3,2,1,0:T(8,128)(2,1)} %tok.1) | copy-start | bytes 1179652
  1.8 9.8 %copy-start.2 = (bf16[384,1152]{1,0:T(8,128)(2,1)S(1)}, bf16[384,1152]{1,0:T(8,128)(2,1)}, u32[]{:S(2)}) copy-start(bf16[384,1152]{1,0:T(8,128)(2,1)} %w_qkv.1) | copy-start | bytes 2654212
  1.8 9.8 %copy-start.3 = (bf16[384,384]{1,0:T(8,128)(2,1)S(1)}, bf16[384,384]{1,0:T(8,128)(2,1)}, u32[]{:S(2)}) copy-start(bf16[384,384]{1,0:T(8,128)(2,1)} %w_proj.1) | copy-start | bytes 884740
  1.8 9.8 %copy-start.4 = (f32[12,225]{1,0:T(8,128)S(1)}, f32[12,225]{1,0:T(8,128)}, u32[]{:S(2)}) copy-start(f32[12,225]{1,0:T(8,128)} %logits.3) | copy-start | bytes 32404
  1.8 9.7 %copy-start.5 = (f32[12]{0:T(128)S(1)}, f32[12]{0:T(128)}, u32[]{:S(2)}) copy-start(f32[12]{0:T(128)} %limit.3) | copy-start | bytes 148
  1.8 9.7 %copy-start.6 = (f32[384]{0:T(512)S(1)}, f32[384]{0:T(512)}, u32[]{:S(2)}) copy-start(f32[384]{0:T(512)} %gain.1) | copy-start | bytes 4612
  1.9 9.6 %collective-permute-start = (bf16[2,4,32,384]{3,2,1,0:T(8,128)(2,1)S(1)}, bf16[2,4,32,384]{3,2,1,0:T(8,128)(2,1)S(1)}, u32[]{:S(2)}, u32[]{:S(2)}) collective-permute-start(bf16[2,4,32,384]{3,2,1,0:T(8,128)(2,1)S(1)} %slice.28), channel_id=1, source_target_pairs={{0,28},{2,30},{4,0},{6,2},{8,4},{10,6},{12,8},{14,10},{16,12},{18,... | collective-permute-start | bytes 589832 | tf_op jit(solution)/shard_map/ppermute | solution.py:597
  6.5 4.9 %collective-permute-start.1 = (bf16[2,64,384]{2,1,0:T(8,128)(2,1)S(1)}, bf16[2,64,384]{2,1,0:T(8,128)(2,1)S(1)}, u32[]{:S(2)}, u32[]{:S(2)}) collective-permute-start(bf16[2,64,384]{2,1,0:T(8,128)(2,1)S(1)} %reshape.58), channel_id=1, source_target_pairs={{0,2},{2,0},{4,6},{6,4},{8,10},{10,8},{12,14},{14,12},{16,18},{18,... | collective-permute-start | bytes 294920 | tf_op jit(solution)/shard_map/ppermute | solution.py:599
  8.1 3.4 %collective-permute-start.2 = (bf16[2,16,384]{2,1,0:T(8,128)(2,1)S(1)}, bf16[2,16,384]{2,1,0:T(8,128)(2,1)S(1)}, u32[]{:S(2)}, u32[]{:S(2)}) collective-permute-start(bf16[2,16,384]{2,1,0:T(8,128)(2,1)S(1)} %slice.30), channel_id=1, source_target_pairs={{0,30},{2,28},{4,2},{6,0},{8,6},{10,4},{12,10},{14,8},{16,14},{18,... | collective-permute-start | bytes 73736 | tf_op jit(solution)/shard_map/ppermute | solution.py:601
  21.6 2.3 %collective-permute-start.6 = (bf16[2,2,608,128]{3,2,1,0:T(8,128)(2,1)}, bf16[2,2,608,128]{3,2,1,0:T(8,128)(2,1)S(1)}, u32[]{:S(2)}, u32[]{:S(2)}) collective-permute-start(bf16[2,2,608,128]{3,2,1,0:T(8,128)(2,1)} %get-tuple-element.16), channel_id=1, source_target_pairs={{0,4},{4,0},{1,5},{5,1},{2,6},{6,2},{3,7},{7,3},{8,12},{12,8},{9,1... | collective-permute-start | bytes 1867784 | tf_op jit(solution)/shard_map/ppermute | solution.py:627
  24.1 7.0 %collective-permute-start.7 = (bf16[2,608,128]{2,1,0:T(8,128)(2,1)S(1)}, bf16[2,608,128]{2,1,0:T(8,128)(2,1)S(1)}, u32[]{:S(2)}, u32[]{:S(2)}) collective-permute-start(bf16[2,608,128]{2,1,0:T(8,128)(2,1)S(1)} %dynamic-slice_bitcast_fusion), channel_id=1, source_target_pairs={{0,1},{1,0},{2,3},{3,2},{4,6},{5,7},{6,4},{7,5},{8,9},{9,8},{10,11... | collective-permute-start | bytes 933896 | tf_op jit(solution)/shard_map/ppermute | solution.py:588
  31.2 5.3 %collective-permute-start.8 = (bf16[608,128]{1,0:T(8,128)(2,1)S(1)}, bf16[608,128]{1,0:T(8,128)(2,1)S(1)}, u32[]{:S(2)}, u32[]{:S(2)}) collective-permute-start(bf16[608,128]{1,0:T(8,128)(2,1)S(1)} %dynamic-slice_bitcast_fusion.1), channel_id=1, source_target_pairs={{0,2},{1,3},{2,0},{3,1},{4,5},{5,4},{6,7},{7,6},{8,10},{9,11},{10,... | collective-permute-start | bytes 466952 | tf_op jit(solution)/shard_map/ppermute | solution.py:588
  36.5 5.9 %collective-permute-start.11 = (bf16[152,128]{1,0:T(8,128)(2,1)S(1)}, bf16[152,128]{1,0:T(8,128)(2,1)S(1)}, u32[]{:S(2)}, u32[]{:S(2)}) collective-permute-start(bf16[152,128]{1,0:T(8,128)(2,1)S(1)} %get-tuple-element.23), channel_id=1, source_target_pairs={{0,8},{8,16},{16,24},{24,0},{1,9},{9,17},{17,25},{25,1},{2,10},{10... | collective-permute-start | bytes 116744 | tf_op jit(solution)/shard_map/ppermute | solution.py:588
  36.6 6.4 %collective-permute-start.10 = (bf16[152,128]{1,0:T(8,128)(2,1)S(1)}, bf16[152,128]{1,0:T(8,128)(2,1)S(1)}, u32[]{:S(2)}, u32[]{:S(2)}) collective-permute-start(bf16[152,128]{1,0:T(8,128)(2,1)S(1)} %get-tuple-element.24), channel_id=1, source_target_pairs={{0,16},{8,24},{16,0},{24,8},{1,17},{9,25},{17,1},{25,9},{2,18},{10... | collective-permute-start | bytes 116744 | tf_op jit(solution)/shard_map/ppermute | solution.py:588
  40.2 4.0 %collective-permute-start.9 = (bf16[152,128]{1,0:T(8,128)(2,1)S(1)}, bf16[152,128]{1,0:T(8,128)(2,1)S(1)}, u32[]{:S(2)}, u32[]{:S(2)}) collective-permute-start(bf16[152,128]{1,0:T(8,128)(2,1)S(1)} %get-tuple-element.22), channel_id=1, source_target_pairs={{0,24},{8,0},{16,8},{24,16},{1,25},{9,1},{17,9},{25,17},{2,26},{10... | collective-permute-start | bytes 116744 | tf_op jit(solution)/shard_map/ppermute | solution.py:588
  45.0 14.3 %all-to-all-start = ((bf16[8,152,128]{2,1,0:T(8,128)(2,1)}), bf16[8,152,128]{2,1,0:T(8,128)(2,1)S(1)}, u32[]{:S(2)}, u32[]{:S(2)}) async-start(bf16[8,152,128]{2,1,0:T(8,128)(2,1)} %broadcast_in_dim.2), calls=%async_computation | async-start | bytes 622592 | tf_op jit(solution)/shard_map/all_to_all | solution.py:638
  49.2 5.0 %collective-permute-start.5 = (bf16[12,4,384]{2,1,0:T(4,128)(2,1)S(1)}, bf16[12,4,384]{2,1,0:T(4,128)(2,1)S(1)}, u32[]{:S(2)}, u32[]{:S(2)}) collective-permute-start(bf16[12,4,384]{2,1,0:T(4,128)(2,1)S(1)} %slice.26), channel_id=1, source_target_pairs={{0,2},{2,0},{4,6},{6,4},{8,10},{10,8},{12,14},{14,12},{16,18},{18,... | collective-permute-start | bytes 110600 | tf_op jit(solution)/shard_map/ppermute | solution.py:616
  51.3 8.0 %collective-permute-start.4 = (bf16[4,28,384]{2,1,0:T(8,128)(2,1)S(1)}, bf16[4,28,384]{2,1,0:T(8,128)(2,1)S(1)}, u32[]{:S(2)}, u32[]{:S(2)}) collective-permute-start(bf16[4,28,384]{2,1,0:T(8,128)(2,1)S(1)} %slice.25), channel_id=1, source_target_pairs={{0,4},{2,6},{4,8},{6,10},{8,12},{10,14},{12,16},{14,18},{16,20},{1... | collective-permute-start | bytes 258056 | tf_op jit(solution)/shard_map/ppermute | solution.py:617
  51.4 7.9 %collective-permute-start.3 = (bf16[4,4,384]{2,1,0:T(4,128)(2,1)S(1)}, bf16[4,4,384]{2,1,0:T(4,128)(2,1)S(1)}, u32[]{:S(2)}, u32[]{:S(2)}) collective-permute-start(bf16[4,4,384]{2,1,0:T(4,128)(2,1)S(1)} %slice.24), channel_id=1, source_target_pairs={{0,6},{2,4},{4,10},{6,8},{8,14},{10,12},{12,18},{14,16},{16,22},{1... | collective-permute-start | bytes 36872 | tf_op jit(solution)/shard_map/ppermute | solution.py:618
  59.3 1.6 %collective-permute-start.12 = (bf16[1216,128]{1,0:T(8,128)(2,1)S(1)}, bf16[1216,128]{1,0:T(8,128)(2,1)S(1)}, u32[]{:S(2)}, u32[]{:S(2)}) collective-permute-start(bf16[1216,128]{1,0:T(8,128)(2,1)S(1)} %bitcast.27), channel_id=1, source_target_pairs={{0,4},{4,0},{1,5},{5,1},{2,6},{6,2},{3,7},{7,3},{8,12},{12,8},{9,1... | collective-permute-start | bytes 933896 | tf_op jit(solution)/shard_map/ppermute | solution.py:640

commit v4 on v3

--- a/solution.py
+++ b/solution.py
@@ -168,7 +168,7 @@
             for i in range(rows):
                 if i + edge < rows:
                     row = own[0, i + edge].astype(F32)
-                    side = edges[(i + edge) * edge : (i + edge + 1) * edge]
+                    side = edges[i * edge : (i + 1) * edge]
                 else:
                     row = below[which, i + edge - rows].astype(F32)
                     side = ends[(i + edge - rows) * edge : (i + edge - rows + 1) * edge]
@@ -594,10 +594,11 @@
     heads = logit_scale.shape[0]
     edge = WIN // 2
     both = jnp.concatenate([tokens, cotangent], 0)
-    below = lax.ppermute(both[:, :edge], GRID, route(GRID, step(-1, 0)))
-    left = both[:, :, :edge].reshape(2, rows * edge, depth)
+    top = both[:, :edge]
+    left = both[:, edge:, :edge].reshape(2, (rows - edge) * edge, depth)
+    tip = both[:, :edge, :edge].reshape(2, edge * edge, depth)
+    below = lax.ppermute(top, GRID, route(GRID, step(-1, 0)))
     right = lax.ppermute(left, GRID, route(GRID, step(0, -1)))
-    tip = left[:, : edge * edge]
     corner = lax.ppermute(tip, GRID, route(GRID, step(-1, -1)))
 
     cores, tall, across = lax.axis_size("hc"), lax.axis_size("hz"), lax.axis_size("wa")
@@ -624,7 +625,8 @@
     d_tokens = (cotangent.astype(F32) + back.astype(F32)).astype(BF16)
 
     swap = route(("hc",), lambda where, sizes: [1 - where[0]])
-    taken = lax.ppermute(given, "hc", swap)
+    one = jnp.where(lax.axis_index("hc") < 0, 0.0, 1.0).astype(BF16)
+    taken = lax.ppermute(given * one, "hc", swap)
     summed = (mine.astype(F32) + taken.astype(F32)).astype(BF16)
     piece = sent // owners
     core, column, image = lax.axis_index("hc"), lax.axis_index("wa"), lax.axis_index("ba")

time: 62.9 us -> 61.8 us (0.983)
  Pallas kernels: 11.8 us -> 11 us
    pallas_call x1, Pallas kernels: 10 us -> 9.25 us  [call(): pl.pallas_call(kernel, out_shape=(jax.ShapeDtypeStruct((rows, cols, depth...]
where the time goes in v4:
time: 61.8 us; the launch traced here: 61.5 us
  waiting for transfers between devices  24.9 us (40%)
  starting transfers between devices  21.2 us (34%)
  Pallas kernels  11 us (18%)
  local copies, waits for them, and re-layouts  2.19 us (4%)
  other arithmetic  1.34 us (2%)
  between operations  0.92 us (1%)
    ppermute x5, waiting for transfers between devices, hand_out(): total = total + lax.ppermute(sent, axes, route(axes, move(by))).astype(F32)  13.2 us
    pallas_call x1, Pallas kernels, call(): pl.pallas_call(kernel, out_shape=(jax.ShapeDtypeStruct((rows, cols, depth...  9.25 us
    ppermute x5, starting transfers between devices, hand_out(): total = total + lax.ppermute(sent, axes, route(axes, move(by))).astype(F32)  6.76 us
    all_to_all x1, waiting for transfers between devices, shards(): ours = lax.all_to_all(spread, ('wa', 'hz'), 0, 0, tiled=True)  5.05 us
    ppermute x1, starting transfers between devices, shards(): below = lax.ppermute(top, GRID, route(GRID, step(-1, 0)))  4.57 us
    all_to_all x1, starting transfers between devices, shards(): ours = lax.all_to_all(spread, ('wa', 'hz'), 0, 0, tiled=True)  3.91 us
    ppermute x1, waiting for transfers between devices, shards(): corner = lax.ppermute(tip, GRID, route(GRID, step(-1, -1)))  2.91 us
    ppermute x1, starting transfers between devices, shards(): lax.ppermute(d_moved[:rows - edge, cols - edge:], GRID, route(GRID, step(...  2.09 us
  transfers between devices with their start and end apart: 14, of which 10 were waited for; matrix products, arithmetic and copies ran while one was open for 2% of the time, Pallas kernels for 0%

profile of v4, /device:TPU:0, one launch (start us, length us, event | category | flops | bytes accessed | tf_op | source)
XLA Modules:
  0.0 61.5 jit_solution(14012238561380219118)
XLA Ops:
  0.7 1.1 %constant_dynamic-update-slice_fusion.1 = bf16[2,16,32,384]{3,2,1,0:T(8,128)(2,1)S(1)} fusion(bf16[1,16,32,384]{3,2,1,0:T(8,128)(2,1)} %tok.1), kind=kLoop, calls=%fused_computation.19 | loop fusion | bytes 786432
  1.8 0.1 constant_dynamic-update-slice_fusion
  1.9 4.6 %collective-permute-start = (bf16[2,4,32,384]{3,2,1,0:T(8,128)(2,1)S(1)}, bf16[2,4,32,384]{3,2,1,0:T(8,128)(2,1)S(1)}, u32[]{:S(2)}, u32[]{:S(2)}) collective-permute-start(bf16[2,4,32,384]{3,2,1,0:T(8,128)(2,1)S(1)} %slice.28), channel_id=1, source_target_pairs={{0,28},{2,30},{4,0},{6,2},{8,4},{10,6},{12,8},{14,10},{16,12},{18,... | collective-permute-start | bytes 589832 | tf_op jit(solution)/shard_map/ppermute | solution.py:600
  6.5 1.6 %collective-permute-start.1 = (bf16[2,48,384]{2,1,0:T(8,128)(2,1)S(1)}, bf16[2,48,384]{2,1,0:T(8,128)(2,1)S(1)}, u32[]{:S(2)}, u32[]{:S(2)}) collective-permute-start(bf16[2,48,384]{2,1,0:T(8,128)(2,1)S(1)} %reshape.61), channel_id=1, source_target_pairs={{0,2},{2,0},{4,6},{6,4},{8,10},{10,8},{12,14},{14,12},{16,18},{18,... | collective-permute-start | bytes 221192 | tf_op jit(solution)/shard_map/ppermute | solution.py:601
  8.2 0.4 collective-permute-start.2
  8.5 2.9 %collective-permute-done.2.corner = bf16[2,16,384]{2,1,0:T(8,128)(2,1)S(1)} collective-permute-done((bf16[2,16,384]{2,1,0:T(8,128)(2,1)S(1)}, bf16[2,16,384]{2,1,0:T(8,128)(2,1)S(1)}, u32[]{:S(2)}, u32[]{:S(2)}) %collective-permute-start.2) | collective-permute-done | bytes 24608 | tf_op jit(solution)/shard_map/ppermute | solution.py:602
  11.5 9.3 %block_grads.1 = (bf16[16,32,384]{2,1,0:T(8,128)(2,1)S(1)}, bf16[2,2,608,128]{3,2,1,0:T(8,128)(2,1)S(1)}, bf16[2,2,608,128]{3,2,1,0:T(8,128)(2,1)S(1)}) custom-call(f32[12]{0:T(128)S(1)} %copy-done.5, bf16[1,16,32,384]{3,2,1,0:T(8,128)(2,1)S(1)} %copy-done.1, bf16[1,16,32,384]{3,2,1,0:T(8,128)(2,1)S(1)} %copy-done, ...), custom_call_target="tpu_custom_call" | custom-call | tf_op jit(solution)/shard_map/block_grads/pallas_call | solution.py:473
  20.8 0.1 collective-permute-start.6
  20.9 2.0 %collective-permute-done.6 = bf16[2,2,608,128]{3,2,1,0:T(8,128)(2,1)S(1)} collective-permute-done((bf16[2,2,608,128]{3,2,1,0:T(8,128)(2,1)S(1)}, bf16[2,2,608,128]{3,2,1,0:T(8,128)(2,1)S(1)}, u32[]{:S(2)}, u32[]{:S(2)}) %collective-permute-start.6) | collective-permute-done | bytes 622624 | tf_op jit(solution)/shard_map/ppermute | solution.py:629
  22.9 0.2 add_convert_fusion
  23.2 1.6 %collective-permute-start.7 = (bf16[2,608,128]{2,1,0:T(8,128)(2,1)S(1)}, bf16[2,608,128]{2,1,0:T(8,128)(2,1)S(1)}, u32[]{:S(2)}, u32[]{:S(2)}) collective-permute-start(bf16[2,608,128]{2,1,0:T(8,128)(2,1)S(1)} %dynamic-slice_bitcast_fusion), channel_id=1, source_target_pairs={{0,1},{1,0},{2,3},{3,2},{4,6},{5,7},{6,4},{7,5},{8,9},{9,8},{10,11... | collective-permute-start | bytes 933896 | tf_op jit(solution)/shard_map/ppermute | solution.py:588
  24.7 5.4 %collective-permute-done.7 = bf16[2,608,128]{2,1,0:T(8,128)(2,1)S(1)} collective-permute-done((bf16[2,608,128]{2,1,0:T(8,128)(2,1)S(1)}, bf16[2,608,128]{2,1,0:T(8,128)(2,1)S(1)}, u32[]{:S(2)}, u32[]{:S(2)}) %collective-permute-start.7) | collective-permute-done | bytes 311328 | tf_op jit(solution)/shard_map/ppermute | solution.py:588
  30.1 0.1 fusion
  30.2 1.3 %collective-permute-start.8 = (bf16[608,128]{1,0:T(8,128)(2,1)S(1)}, bf16[608,128]{1,0:T(8,128)(2,1)S(1)}, u32[]{:S(2)}, u32[]{:S(2)}) collective-permute-start(bf16[608,128]{1,0:T(8,128)(2,1)S(1)} %dynamic-slice_bitcast_fusion.1), channel_id=1, source_target_pairs={{0,2},{1,3},{2,0},{3,1},{4,5},{5,4},{6,7},{7,6},{8,10},{9,11},{10,... | collective-permute-start | bytes 466952 | tf_op jit(solution)/shard_map/ppermute | solution.py:588
  31.6 4.0 %collective-permute-done.8 = bf16[608,128]{1,0:T(8,128)(2,1)S(1)} collective-permute-done((bf16[608,128]{1,0:T(8,128)(2,1)S(1)}, bf16[608,128]{1,0:T(8,128)(2,1)S(1)}, u32[]{:S(2)}, u32[]{:S(2)}) %collective-permute-start.8) | collective-permute-done | bytes 155680 | tf_op jit(solution)/shard_map/ppermute | solution.py:588
  35.6 0.1 collective-permute-start.11
  35.7 3.7 %collective-permute-start.10 = (bf16[152,128]{1,0:T(8,128)(2,1)S(1)}, bf16[152,128]{1,0:T(8,128)(2,1)S(1)}, u32[]{:S(2)}, u32[]{:S(2)}) collective-permute-start(bf16[152,128]{1,0:T(8,128)(2,1)S(1)} %get-tuple-element.24), channel_id=1, source_target_pairs={{0,16},{8,24},{16,0},{24,8},{1,17},{9,25},{17,1},{25,9},{2,18},{10... | collective-permute-start | bytes 116744 | tf_op jit(solution)/shard_map/ppermute | solution.py:588
  39.4 0.1 collective-permute-start.9
  39.5 2.1 %collective-permute-done.11 = bf16[152,128]{1,0:T(8,128)(2,1)S(1)} collective-permute-done((bf16[152,128]{1,0:T(8,128)(2,1)S(1)}, bf16[152,128]{1,0:T(8,128)(2,1)S(1)}, u32[]{:S(2)}, u32[]{:S(2)}) %collective-permute-start.11) | collective-permute-done | bytes 38944 | tf_op jit(solution)/shard_map/ppermute | solution.py:588
  41.5 0.6 collective-permute-done.10
  42.1 1.2 %collective-permute-done.9 = bf16[152,128]{1,0:T(8,128)(2,1)S(1)} collective-permute-done((bf16[152,128]{1,0:T(8,128)(2,1)S(1)}, bf16[152,128]{1,0:T(8,128)(2,1)S(1)}, u32[]{:S(2)}, u32[]{:S(2)}) %collective-permute-start.9) | collective-permute-done | bytes 38944 | tf_op jit(solution)/shard_map/ppermute | solution.py:588
  43.4 0.8 %broadcast_in_dim.2 = bf16[8,152,128]{2,1,0:T(8,128)(2,1)} broadcast(bf16[152,128]{1,0:T(8,128)(2,1)S(1)} %fusion.4), dimensions={1,2} | broadcast | bytes 350208 | tf_op jit(solution)/shard_map/broadcast_in_dim | solution.py:639
  44.1 3.9 %all-to-all-start = ((bf16[8,152,128]{2,1,0:T(8,128)(2,1)}), bf16[8,152,128]{2,1,0:T(8,128)(2,1)S(1)}, u32[]{:S(2)}, u32[]{:S(2)}) async-start(bf16[8,152,128]{2,1,0:T(8,128)(2,1)} %broadcast_in_dim.2), calls=%async_computation | async-start | bytes 622592 | tf_op jit(solution)/shard_map/all_to_all | solution.py:640
  48.1 2.1 %collective-permute-start.5 = (bf16[12,4,384]{2,1,0:T(4,128)(2,1)S(1)}, bf16[12,4,384]{2,1,0:T(4,128)(2,1)S(1)}, u32[]{:S(2)}, u32[]{:S(2)}) collective-permute-start(bf16[12,4,384]{2,1,0:T(4,128)(2,1)S(1)} %slice.26), channel_id=1, source_target_pairs={{0,2},{2,0},{4,6},{6,4},{8,10},{10,8},{12,14},{14,12},{16,18},{18,... | collective-permute-start | bytes 110600 | tf_op jit(solution)/shard_map/ppermute | solution.py:617
  50.2 0.1 collective-permute-start.4
  50.3 1.7 %collective-permute-start.3 = (bf16[4,4,384]{2,1,0:T(4,128)(2,1)S(1)}, bf16[4,4,384]{2,1,0:T(4,128)(2,1)S(1)}, u32[]{:S(2)}, u32[]{:S(2)}) collective-permute-start(bf16[4,4,384]{2,1,0:T(4,128)(2,1)S(1)} %slice.24), channel_id=1, source_target_pairs={{0,6},{2,4},{4,10},{6,8},{8,14},{10,12},{12,18},{14,16},{16,22},{1... | collective-permute-start | bytes 36872 | tf_op jit(solution)/shard_map/ppermute | solution.py:619
  52.0 1.0 %collective-permute-done.5 = bf16[12,4,384]{2,1,0:T(4,128)(2,1)S(1)} collective-permute-done((bf16[12,4,384]{2,1,0:T(4,128)(2,1)S(1)}, bf16[12,4,384]{2,1,0:T(4,128)(2,1)S(1)}, u32[]{:S(2)}, u32[]{:S(2)}) %collective-permute-start.5) | collective-permute-done | bytes 36896 | tf_op jit(solution)/shard_map/ppermute | solution.py:617
  53.0 0.1 maximum_bitcast_fusion
  53.1 5.1 %all-to-all-done = bf16[8,152,128]{2,1,0:T(8,128)(2,1)S(1)} async-done(((bf16[8,152,128]{2,1,0:T(8,128)(2,1)}), bf16[8,152,128]{2,1,0:T(8,128)(2,1)S(1)}, u32[]{:S(2)}, u32[]{:S(2)}) %all-to-all-start) | async-done | bytes 311328 | tf_op jit(solution)/shard_map/all_to_all | solution.py:640
  58.2 0.8 %add_convert_fusion.1 = bf16[1,16,32,384]{3,2,1,0:T(8,128)(2,1)} fusion(bf16[1,16,32,384]{3,2,1,0:T(8,128)(2,1)S(1)} %copy-done, bf16[1,12,32,384]{3,2,1,0:T(8,128)(2,1)S(1)} %maximum_bitcast_fusion, bf16[1,4,32,384]{3,2,1,0:T(8,128)(2,1)S(1)} %maximum_bitcast_fusion.1), kind=kLoop, calls=%fused_computation.1 | loop fusion | flops 983040 | bytes 1179648 | tf_op jit(solution)/shard_map/convert_element_type | solution.py:625
  59.1 0.7 %collective-permute-done.12.theirs = bf16[1216,128]{1,0:T(8,128)(2,1)S(1)} collective-permute-done((bf16[1216,128]{1,0:T(8,128)(2,1)S(1)}, bf16[1216,128]{1,0:T(8,128)(2,1)S(1)}, u32[]{:S(2)}, u32[]{:S(2)}) %collective-permute-start.12) | collective-permute-done | bytes 311328 | tf_op jit(solution)/shard_map/ppermute | solution.py:642
  59.8 1.8 %finish.1 = (f32[576,384]{1,0:T(8,128)}, f32[192,384]{1,0:T(8,128)}, f32[12,225]{1,0:T(8,128)}, f32[12]{0:T(128)}, f32[384]{0:T(512)}) custom-call(f32[12]{0:T(128)S(1)} %copy-done.5, bf16[1216,128]{1,0:T(8,128)(2,1)S(1)} %bitcast.28, bf16[1216,128]{1,0:T(8,128)(2,1)S(1)} %collective-permute-done.12.theirs, f32[12,225]{1,0:T(8,128)S(1)} %copy-done.4), custom_call_target="tpu_custom_call" | custom-call | tf_op jit(solution)/shard_map/finish/pallas_call | solution.py:522
  (35 shorter events, 0.4 us)
Async XLA Ops:
  0.6 1.1 %copy-start = (bf16[1,16,32,384]{3,2,1,0:T(8,128)(2,1)S(1)}, bf16[1,16,32,384]{3,2,1,0:T(8,128)(2,1)}, u32[]{:S(2)}) copy-start(bf16[1,16,32,384]{3,2,1,0:T(8,128)(2,1)} %cot.1) | copy-start | bytes 1179652
  0.6 10.8 %copy-start.4 = (f32[12,225]{1,0:T(8,128)S(1)}, f32[12,225]{1,0:T(8,128)}, u32[]{:S(2)}) copy-start(f32[12,225]{1,0:T(8,128)} %logits.3) | copy-start | bytes 32404
  1.8 9.7 %copy-start.1 = (bf16[1,16,32,384]{3,2,1,0:T(8,128)(2,1)S(1)}, bf16[1,16,32,384]{3,2,1,0:T(8,128)(2,1)}, u32[]{:S(2)}) copy-start(bf16[1,16,32,384]{3,2,1,0:T(8,128)(2,1)} %tok.1) | copy-start | bytes 1179652
  1.8 9.7 %copy-start.2 = (bf16[384,1152]{1,0:T(8,128)(2,1)S(1)}, bf16[384,1152]{1,0:T(8,128)(2,1)}, u32[]{:S(2)}) copy-start(bf16[384,1152]{1,0:T(8,128)(2,1)} %w_qkv.1) | copy-start | bytes 2654212
  1.8 9.7 %copy-start.3 = (bf16[384,384]{1,0:T(8,128)(2,1)S(1)}, bf16[384,384]{1,0:T(8,128)(2,1)}, u32[]{:S(2)}) copy-start(bf16[384,384]{1,0:T(8,128)(2,1)} %w_proj.1) | copy-start | bytes 884740
  1.8 9.7 %copy-start.5 = (f32[12]{0:T(128)S(1)}, f32[12]{0:T(128)}, u32[]{:S(2)}) copy-start(f32[12]{0:T(128)} %limit.3) | copy-start | bytes 148
  1.8 9.7 %copy-start.6 = (f32[384]{0:T(512)S(1)}, f32[384]{0:T(512)}, u32[]{:S(2)}) copy-start(f32[384]{0:T(512)} %gain.1) | copy-start | bytes 4612
  1.9 9.6 %collective-permute-start = (bf16[2,4,32,384]{3,2,1,0:T(8,128)(2,1)S(1)}, bf16[2,4,32,384]{3,2,1,0:T(8,128)(2,1)S(1)}, u32[]{:S(2)}, u32[]{:S(2)}) collective-permute-start(bf16[2,4,32,384]{3,2,1,0:T(8,128)(2,1)S(1)} %slice.28), channel_id=1, source_target_pairs={{0,28},{2,30},{4,0},{6,2},{8,4},{10,6},{12,8},{14,10},{16,12},{18,... | collective-permute-start | bytes 589832 | tf_op jit(solution)/shard_map/ppermute | solution.py:600
  6.5 4.9 %collective-permute-start.1 = (bf16[2,48,384]{2,1,0:T(8,128)(2,1)S(1)}, bf16[2,48,384]{2,1,0:T(8,128)(2,1)S(1)}, u32[]{:S(2)}, u32[]{:S(2)}) collective-permute-start(bf16[2,48,384]{2,1,0:T(8,128)(2,1)S(1)} %reshape.61), channel_id=1, source_target_pairs={{0,2},{2,0},{4,6},{6,4},{8,10},{10,8},{12,14},{14,12},{16,18},{18,... | collective-permute-start | bytes 221192 | tf_op jit(solution)/shard_map/ppermute | solution.py:601
  8.2 3.3 %collective-permute-start.2 = (bf16[2,16,384]{2,1,0:T(8,128)(2,1)S(1)}, bf16[2,16,384]{2,1,0:T(8,128)(2,1)S(1)}, u32[]{:S(2)}, u32[]{:S(2)}) collective-permute-start(bf16[2,16,384]{2,1,0:T(8,128)(2,1)S(1)} %reshape.62), channel_id=1, source_target_pairs={{0,30},{2,28},{4,2},{6,0},{8,6},{10,4},{12,10},{14,8},{16,14},{18,... | collective-permute-start | bytes 73736 | tf_op jit(solution)/shard_map/ppermute | solution.py:602
  20.8 2.1 %collective-permute-start.6 = (bf16[2,2,608,128]{3,2,1,0:T(8,128)(2,1)S(1)}, bf16[2,2,608,128]{3,2,1,0:T(8,128)(2,1)S(1)}, u32[]{:S(2)}, u32[]{:S(2)}) collective-permute-start(bf16[2,2,608,128]{3,2,1,0:T(8,128)(2,1)S(1)} %broadcast_multiply_fusion), channel_id=1, source_target_pairs={{0,4},{4,0},{1,5},{5,1},{2,6},{6,2},{3,7},{7,3},{8,12},{12,8},{9,1... | collective-permute-start | bytes 1867784 | tf_op jit(solution)/shard_map/ppermute | solution.py:629
  23.2 7.0 %collective-permute-start.7 = (bf16[2,608,128]{2,1,0:T(8,128)(2,1)S(1)}, bf16[2,608,128]{2,1,0:T(8,128)(2,1)S(1)}, u32[]{:S(2)}, u32[]{:S(2)}) collective-permute-start(bf16[2,608,128]{2,1,0:T(8,128)(2,1)S(1)} %dynamic-slice_bitcast_fusion), channel_id=1, source_target_pairs={{0,1},{1,0},{2,3},{3,2},{4,6},{5,7},{6,4},{7,5},{8,9},{9,8},{10,11... | collective-permute-start | bytes 933896 | tf_op jit(solution)/shard_map/ppermute | solution.py:588
  30.2 5.3 %collective-permute-start.8 = (bf16[608,128]{1,0:T(8,128)(2,1)S(1)}, bf16[608,128]{1,0:T(8,128)(2,1)S(1)}, u32[]{:S(2)}, u32[]{:S(2)}) collective-permute-start(bf16[608,128]{1,0:T(8,128)(2,1)S(1)} %dynamic-slice_bitcast_fusion.1), channel_id=1, source_target_pairs={{0,2},{1,3},{2,0},{3,1},{4,5},{5,4},{6,7},{7,6},{8,10},{9,11},{10,... | collective-permute-start | bytes 466952 | tf_op jit(solution)/shard_map/ppermute | solution.py:588
  35.6 5.9 %collective-permute-start.11 = (bf16[152,128]{1,0:T(8,128)(2,1)S(1)}, bf16[152,128]{1,0:T(8,128)(2,1)S(1)}, u32[]{:S(2)}, u32[]{:S(2)}) collective-permute-start(bf16[152,128]{1,0:T(8,128)(2,1)S(1)} %get-tuple-element.23), channel_id=1, source_target_pairs={{0,8},{8,16},{16,24},{24,0},{1,9},{9,17},{17,25},{25,1},{2,10},{10... | collective-permute-start | bytes 116744 | tf_op jit(solution)/shard_map/ppermute | solution.py:588
  35.7 6.5 %collective-permute-start.10 = (bf16[152,128]{1,0:T(8,128)(2,1)S(1)}, bf16[152,128]{1,0:T(8,128)(2,1)S(1)}, u32[]{:S(2)}, u32[]{:S(2)}) collective-permute-start(bf16[152,128]{1,0:T(8,128)(2,1)S(1)} %get-tuple-element.24), channel_id=1, source_target_pairs={{0,16},{8,24},{16,0},{24,8},{1,17},{9,25},{17,1},{25,9},{2,18},{10... | collective-permute-start | bytes 116744 | tf_op jit(solution)/shard_map/ppermute | solution.py:588
  39.4 4.0 %collective-permute-start.9 = (bf16[152,128]{1,0:T(8,128)(2,1)S(1)}, bf16[152,128]{1,0:T(8,128)(2,1)S(1)}, u32[]{:S(2)}, u32[]{:S(2)}) collective-permute-start(bf16[152,128]{1,0:T(8,128)(2,1)S(1)} %get-tuple-element.22), channel_id=1, source_target_pairs={{0,24},{8,0},{16,8},{24,16},{1,25},{9,1},{17,9},{25,17},{2,26},{10... | collective-permute-start | bytes 116744 | tf_op jit(solution)/shard_map/ppermute | solution.py:588
  44.1 14.1 %all-to-all-start = ((bf16[8,152,128]{2,1,0:T(8,128)(2,1)}), bf16[8,152,128]{2,1,0:T(8,128)(2,1)S(1)}, u32[]{:S(2)}, u32[]{:S(2)}) async-start(bf16[8,152,128]{2,1,0:T(8,128)(2,1)} %broadcast_in_dim.2), calls=%async_computation | async-start | bytes 622592 | tf_op jit(solution)/shard_map/all_to_all | solution.py:640
  48.1 5.0 %collective-permute-start.5 = (bf16[12,4,384]{2,1,0:T(4,128)(2,1)S(1)}, bf16[12,4,384]{2,1,0:T(4,128)(2,1)S(1)}, u32[]{:S(2)}, u32[]{:S(2)}) collective-permute-start(bf16[12,4,384]{2,1,0:T(4,128)(2,1)S(1)} %slice.26), channel_id=1, source_target_pairs={{0,2},{2,0},{4,6},{6,4},{8,10},{10,8},{12,14},{14,12},{16,18},{18,... | collective-permute-start | bytes 110600 | tf_op jit(solution)/shard_map/ppermute | solution.py:617
  50.2 8.0 %collective-permute-start.4 = (bf16[4,28,384]{2,1,0:T(8,128)(2,1)S(1)}, bf16[4,28,384]{2,1,0:T(8,128)(2,1)S(1)}, u32[]{:S(2)}, u32[]{:S(2)}) collective-permute-start(bf16[4,28,384]{2,1,0:T(8,128)(2,1)S(1)} %slice.25), channel_id=1, source_target_pairs={{0,4},{2,6},{4,8},{6,10},{8,12},{10,14},{12,16},{14,18},{16,20},{1... | collective-permute-start | bytes 258056 | tf_op jit(solution)/shard_map/ppermute | solution.py:618
  50.3 7.9 %collective-permute-start.3 = (bf16[4,4,384]{2,1,0:T(4,128)(2,1)S(1)}, bf16[4,4,384]{2,1,0:T(4,128)(2,1)S(1)}, u32[]{:S(2)}, u32[]{:S(2)}) collective-permute-start(bf16[4,4,384]{2,1,0:T(4,128)(2,1)S(1)} %slice.24), channel_id=1, source_target_pairs={{0,6},{2,4},{4,10},{6,8},{8,14},{10,12},{12,18},{14,16},{16,22},{1... | collective-permute-start | bytes 36872 | tf_op jit(solution)/shard_map/ppermute | solution.py:619
  58.2 1.6 %collective-permute-start.12 = (bf16[1216,128]{1,0:T(8,128)(2,1)S(1)}, bf16[1216,128]{1,0:T(8,128)(2,1)S(1)}, u32[]{:S(2)}, u32[]{:S(2)}) collective-permute-start(bf16[1216,128]{1,0:T(8,128)(2,1)S(1)} %bitcast.27), channel_id=1, source_target_pairs={{0,4},{4,0},{1,5},{5,1},{2,6},{6,2},{3,7},{7,3},{8,12},{12,8},{9,1... | collective-permute-start | bytes 933896 | tf_op jit(solution)/shard_map/ppermute | solution.py:642

commit v5 on v4

--- a/solution.py
+++ b/solution.py
@@ -71,8 +71,8 @@
 
 
 def pipeline(items, stages):
-    for start in range(len(items) + len(stages) - 1):
-        for back, stage in enumerate(stages):
+    for start in range(len(items) + len(stages)):
+        for back, stage in zip((0, 2, 3), stages):
             if 0 <= start - back < len(items):
                 stage(*items[start - back])
 

time: 61.8 us -> 61.6 us (level)
  no operation moved by 1% of the time
where the time goes in v5:
time: 61.6 us; the launch traced here: 61.4 us
  waiting for transfers between devices  24.9 us (40%)
  starting transfers between devices  21.2 us (34%)
  Pallas kernels  10.9 us (18%)
  local copies, waits for them, and re-layouts  2.19 us (4%)
  other arithmetic  1.34 us (2%)
  between operations  0.92 us (1%)
    ppermute x5, waiting for transfers between devices, hand_out(): total = total + lax.ppermute(sent, axes, route(axes, move(by))).astype(F32)  13.2 us
    pallas_call x1, Pallas kernels, call(): pl.pallas_call(kernel, out_shape=(jax.ShapeDtypeStruct((rows, cols, depth...  9.11 us
    ppermute x5, starting transfers between devices, hand_out(): total = total + lax.ppermute(sent, axes, route(axes, move(by))).astype(F32)  6.76 us
    all_to_all x1, waiting for transfers between devices, shards(): ours = lax.all_to_all(spread, ('wa', 'hz'), 0, 0, tiled=True)  5.05 us
    ppermute x1, starting transfers between devices, shards(): below = lax.ppermute(top, GRID, route(GRID, step(-1, 0)))  4.57 us
    all_to_all x1, starting transfers between devices, shards(): ours = lax.all_to_all(spread, ('wa', 'hz'), 0, 0, tiled=True)  3.92 us
    ppermute x1, waiting for transfers between devices, shards(): corner = lax.ppermute(tip, GRID, route(GRID, step(-1, -1)))  2.91 us
    ppermute x1, starting transfers between devices, shards(): lax.ppermute(d_moved[:rows - edge, cols - edge:], GRID, route(GRID, step(...  2.09 us
  transfers between devices with their start and end apart: 14, of which 10 were waited for; matrix products, arithmetic and copies ran while one was open for 2% of the time, Pallas kernels for 0%

profile of v5, /device:TPU:0, one launch (start us, length us, event | category | flops | bytes accessed | tf_op | source)
XLA Modules:
  0.0 61.4 jit_solution(12724941917336373545)
XLA Ops:
  0.7 1.1 %constant_dynamic-update-slice_fusion.1 = bf16[2,16,32,384]{3,2,1,0:T(8,128)(2,1)S(1)} fusion(bf16[1,16,32,384]{3,2,1,0:T(8,128)(2,1)} %tok.1), kind=kLoop, calls=%fused_computation.19 | loop fusion | bytes 786432
  1.8 0.1 constant_dynamic-update-slice_fusion
  1.9 4.6 %collective-permute-start = (bf16[2,4,32,384]{3,2,1,0:T(8,128)(2,1)S(1)}, bf16[2,4,32,384]{3,2,1,0:T(8,128)(2,1)S(1)}, u32[]{:S(2)}, u32[]{:S(2)}) collective-permute-start(bf16[2,4,32,384]{3,2,1,0:T(8,128)(2,1)S(1)} %slice.28), channel_id=1, source_target_pairs={{0,28},{2,30},{4,0},{6,2},{8,4},{10,6},{12,8},{14,10},{16,12},{18,... | collective-permute-start | bytes 589832 | tf_op jit(solution)/shard_map/ppermute | solution.py:600
  6.5 1.6 %collective-permute-start.1 = (bf16[2,48,384]{2,1,0:T(8,128)(2,1)S(1)}, bf16[2,48,384]{2,1,0:T(8,128)(2,1)S(1)}, u32[]{:S(2)}, u32[]{:S(2)}) collective-permute-start(bf16[2,48,384]{2,1,0:T(8,128)(2,1)S(1)} %reshape.61), channel_id=1, source_target_pairs={{0,2},{2,0},{4,6},{6,4},{8,10},{10,8},{12,14},{14,12},{16,18},{18,... | collective-permute-start | bytes 221192 | tf_op jit(solution)/shard_map/ppermute | solution.py:601
  8.2 0.4 collective-permute-start.2
  8.5 2.9 %collective-permute-done.2.corner = bf16[2,16,384]{2,1,0:T(8,128)(2,1)S(1)} collective-permute-done((bf16[2,16,384]{2,1,0:T(8,128)(2,1)S(1)}, bf16[2,16,384]{2,1,0:T(8,128)(2,1)S(1)}, u32[]{:S(2)}, u32[]{:S(2)}) %collective-permute-start.2) | collective-permute-done | bytes 24608 | tf_op jit(solution)/shard_map/ppermute | solution.py:602
  11.5 9.1 %block_grads.1 = (bf16[16,32,384]{2,1,0:T(8,128)(2,1)S(1)}, bf16[2,2,608,128]{3,2,1,0:T(8,128)(2,1)S(1)}, bf16[2,2,608,128]{3,2,1,0:T(8,128)(2,1)S(1)}) custom-call(f32[12]{0:T(128)S(1)} %copy-done.5, bf16[1,16,32,384]{3,2,1,0:T(8,128)(2,1)S(1)} %copy-done.1, bf16[1,16,32,384]{3,2,1,0:T(8,128)(2,1)S(1)} %copy-done, ...), custom_call_target="tpu_custom_call" | custom-call | tf_op jit(solution)/shard_map/block_grads/pallas_call | solution.py:473
  20.7 0.1 collective-permute-start.6
  20.8 2.0 %collective-permute-done.6 = bf16[2,2,608,128]{3,2,1,0:T(8,128)(2,1)S(1)} collective-permute-done((bf16[2,2,608,128]{3,2,1,0:T(8,128)(2,1)S(1)}, bf16[2,2,608,128]{3,2,1,0:T(8,128)(2,1)S(1)}, u32[]{:S(2)}, u32[]{:S(2)}) %collective-permute-start.6) | collective-permute-done | bytes 622624 | tf_op jit(solution)/shard_map/ppermute | solution.py:629
  22.8 0.2 add_convert_fusion
  23.0 1.6 %collective-permute-start.7 = (bf16[2,608,128]{2,1,0:T(8,128)(2,1)S(1)}, bf16[2,608,128]{2,1,0:T(8,128)(2,1)S(1)}, u32[]{:S(2)}, u32[]{:S(2)}) collective-permute-start(bf16[2,608,128]{2,1,0:T(8,128)(2,1)S(1)} %dynamic-slice_bitcast_fusion), channel_id=1, source_target_pairs={{0,1},{1,0},{2,3},{3,2},{4,6},{5,7},{6,4},{7,5},{8,9},{9,8},{10,11... | collective-permute-start | bytes 933896 | tf_op jit(solution)/shard_map/ppermute | solution.py:588
  24.6 5.4 %collective-permute-done.7 = bf16[2,608,128]{2,1,0:T(8,128)(2,1)S(1)} collective-permute-done((bf16[2,608,128]{2,1,0:T(8,128)(2,1)S(1)}, bf16[2,608,128]{2,1,0:T(8,128)(2,1)S(1)}, u32[]{:S(2)}, u32[]{:S(2)}) %collective-permute-start.7) | collective-permute-done | bytes 311328 | tf_op jit(solution)/shard_map/ppermute | solution.py:588
  30.0 0.1 fusion
  30.1 1.3 %collective-permute-start.8 = (bf16[608,128]{1,0:T(8,128)(2,1)S(1)}, bf16[608,128]{1,0:T(8,128)(2,1)S(1)}, u32[]{:S(2)}, u32[]{:S(2)}) collective-permute-start(bf16[608,128]{1,0:T(8,128)(2,1)S(1)} %dynamic-slice_bitcast_fusion.1), channel_id=1, source_target_pairs={{0,2},{1,3},{2,0},{3,1},{4,5},{5,4},{6,7},{7,6},{8,10},{9,11},{10,... | collective-permute-start | bytes 466952 | tf_op jit(solution)/shard_map/ppermute | solution.py:588
  31.4 4.0 %collective-permute-done.8 = bf16[608,128]{1,0:T(8,128)(2,1)S(1)} collective-permute-done((bf16[608,128]{1,0:T(8,128)(2,1)S(1)}, bf16[608,128]{1,0:T(8,128)(2,1)S(1)}, u32[]{:S(2)}, u32[]{:S(2)}) %collective-permute-start.8) | collective-permute-done | bytes 155680 | tf_op jit(solution)/shard_map/ppermute | solution.py:588
  35.5 0.1 collective-permute-start.11
  35.5 3.7 %collective-permute-start.10 = (bf16[152,128]{1,0:T(8,128)(2,1)S(1)}, bf16[152,128]{1,0:T(8,128)(2,1)S(1)}, u32[]{:S(2)}, u32[]{:S(2)}) collective-permute-start(bf16[152,128]{1,0:T(8,128)(2,1)S(1)} %get-tuple-element.24), channel_id=1, source_target_pairs={{0,16},{8,24},{16,0},{24,8},{1,17},{9,25},{17,1},{25,9},{2,18},{10... | collective-permute-start | bytes 116744 | tf_op jit(solution)/shard_map/ppermute | solution.py:588
  39.2 0.1 collective-permute-start.9
  39.3 2.1 %collective-permute-done.11 = bf16[152,128]{1,0:T(8,128)(2,1)S(1)} collective-permute-done((bf16[152,128]{1,0:T(8,128)(2,1)S(1)}, bf16[152,128]{1,0:T(8,128)(2,1)S(1)}, u32[]{:S(2)}, u32[]{:S(2)}) %collective-permute-start.11) | collective-permute-done | bytes 38944 | tf_op jit(solution)/shard_map/ppermute | solution.py:588
  41.4 0.6 collective-permute-done.10
  42.0 1.2 %collective-permute-done.9 = bf16[152,128]{1,0:T(8,128)(2,1)S(1)} collective-permute-done((bf16[152,128]{1,0:T(8,128)(2,1)S(1)}, bf16[152,128]{1,0:T(8,128)(2,1)S(1)}, u32[]{:S(2)}, u32[]{:S(2)}) %collective-permute-start.9) | collective-permute-done | bytes 38944 | tf_op jit(solution)/shard_map/ppermute | solution.py:588
  43.2 0.8 %broadcast_in_dim.2 = bf16[8,152,128]{2,1,0:T(8,128)(2,1)} broadcast(bf16[152,128]{1,0:T(8,128)(2,1)S(1)} %fusion.4), dimensions={1,2} | broadcast | bytes 350208 | tf_op jit(solution)/shard_map/broadcast_in_dim | solution.py:639
  44.0 3.9 %all-to-all-start = ((bf16[8,152,128]{2,1,0:T(8,128)(2,1)}), bf16[8,152,128]{2,1,0:T(8,128)(2,1)S(1)}, u32[]{:S(2)}, u32[]{:S(2)}) async-start(bf16[8,152,128]{2,1,0:T(8,128)(2,1)} %broadcast_in_dim.2), calls=%async_computation | async-start | bytes 622592 | tf_op jit(solution)/shard_map/all_to_all | solution.py:640
  47.9 2.1 %collective-permute-start.5 = (bf16[12,4,384]{2,1,0:T(4,128)(2,1)S(1)}, bf16[12,4,384]{2,1,0:T(4,128)(2,1)S(1)}, u32[]{:S(2)}, u32[]{:S(2)}) collective-permute-start(bf16[12,4,384]{2,1,0:T(4,128)(2,1)S(1)} %slice.26), channel_id=1, source_target_pairs={{0,2},{2,0},{4,6},{6,4},{8,10},{10,8},{12,14},{14,12},{16,18},{18,... | collective-permute-start | bytes 110600 | tf_op jit(solution)/shard_map/ppermute | solution.py:617
  50.1 0.1 collective-permute-start.4
  50.1 1.7 %collective-permute-start.3 = (bf16[4,4,384]{2,1,0:T(4,128)(2,1)S(1)}, bf16[4,4,384]{2,1,0:T(4,128)(2,1)S(1)}, u32[]{:S(2)}, u32[]{:S(2)}) collective-permute-start(bf16[4,4,384]{2,1,0:T(4,128)(2,1)S(1)} %slice.24), channel_id=1, source_target_pairs={{0,6},{2,4},{4,10},{6,8},{8,14},{10,12},{12,18},{14,16},{16,22},{1... | collective-permute-start | bytes 36872 | tf_op jit(solution)/shard_map/ppermute | solution.py:619
  51.9 1.0 %collective-permute-done.5 = bf16[12,4,384]{2,1,0:T(4,128)(2,1)S(1)} collective-permute-done((bf16[12,4,384]{2,1,0:T(4,128)(2,1)S(1)}, bf16[12,4,384]{2,1,0:T(4,128)(2,1)S(1)}, u32[]{:S(2)}, u32[]{:S(2)}) %collective-permute-start.5) | collective-permute-done | bytes 36896 | tf_op jit(solution)/shard_map/ppermute | solution.py:617
  52.9 0.1 maximum_bitcast_fusion
  53.0 5.1 %all-to-all-done = bf16[8,152,128]{2,1,0:T(8,128)(2,1)S(1)} async-done(((bf16[8,152,128]{2,1,0:T(8,128)(2,1)}), bf16[8,152,128]{2,1,0:T(8,128)(2,1)S(1)}, u32[]{:S(2)}, u32[]{:S(2)}) %all-to-all-start) | async-done | bytes 311328 | tf_op jit(solution)/shard_map/all_to_all | solution.py:640
  58.1 0.8 %add_convert_fusion.1 = bf16[1,16,32,384]{3,2,1,0:T(8,128)(2,1)} fusion(bf16[1,16,32,384]{3,2,1,0:T(8,128)(2,1)S(1)} %copy-done, bf16[1,12,32,384]{3,2,1,0:T(8,128)(2,1)S(1)} %maximum_bitcast_fusion, bf16[1,4,32,384]{3,2,1,0:T(8,128)(2,1)S(1)} %maximum_bitcast_fusion.1), kind=kLoop, calls=%fused_computation.1 | loop fusion | flops 983040 | bytes 1179648 | tf_op jit(solution)/shard_map/convert_element_type | solution.py:625
  58.9 0.7 %collective-permute-done.12.theirs = bf16[1216,128]{1,0:T(8,128)(2,1)S(1)} collective-permute-done((bf16[1216,128]{1,0:T(8,128)(2,1)S(1)}, bf16[1216,128]{1,0:T(8,128)(2,1)S(1)}, u32[]{:S(2)}, u32[]{:S(2)}) %collective-permute-start.12) | collective-permute-done | bytes 311328 | tf_op jit(solution)/shard_map/ppermute | solution.py:642
  59.7 1.8 %finish.1 = (f32[576,384]{1,0:T(8,128)}, f32[192,384]{1,0:T(8,128)}, f32[12,225]{1,0:T(8,128)}, f32[12]{0:T(128)}, f32[384]{0:T(512)}) custom-call(f32[12]{0:T(128)S(1)} %copy-done.5, bf16[1216,128]{1,0:T(8,128)(2,1)S(1)} %bitcast.28, bf16[1216,128]{1,0:T(8,128)(2,1)S(1)} %collective-permute-done.12.theirs, f32[12,225]{1,0:T(8,128)S(1)} %copy-done.4), custom_call_target="tpu_custom_call" | custom-call | tf_op jit(solution)/shard_map/finish/pallas_call | solution.py:522
  (35 shorter events, 0.4 us)
Async XLA Ops:
  0.6 1.1 %copy-start = (bf16[1,16,32,384]{3,2,1,0:T(8,128)(2,1)S(1)}, bf16[1,16,32,384]{3,2,1,0:T(8,128)(2,1)}, u32[]{:S(2)}) copy-start(bf16[1,16,32,384]{3,2,1,0:T(8,128)(2,1)} %cot.1) | copy-start | bytes 1179652
  0.6 10.8 %copy-start.4 = (f32[12,225]{1,0:T(8,128)S(1)}, f32[12,225]{1,0:T(8,128)}, u32[]{:S(2)}) copy-start(f32[12,225]{1,0:T(8,128)} %logits.3) | copy-start | bytes 32404
  1.8 9.7 %copy-start.1 = (bf16[1,16,32,384]{3,2,1,0:T(8,128)(2,1)S(1)}, bf16[1,16,32,384]{3,2,1,0:T(8,128)(2,1)}, u32[]{:S(2)}) copy-start(bf16[1,16,32,384]{3,2,1,0:T(8,128)(2,1)} %tok.1) | copy-start | bytes 1179652
  1.8 9.7 %copy-start.2 = (bf16[384,1152]{1,0:T(8,128)(2,1)S(1)}, bf16[384,1152]{1,0:T(8,128)(2,1)}, u32[]{:S(2)}) copy-start(bf16[384,1152]{1,0:T(8,128)(2,1)} %w_qkv.1) | copy-start | bytes 2654212
  1.8 9.7 %copy-start.3 = (bf16[384,384]{1,0:T(8,128)(2,1)S(1)}, bf16[384,384]{1,0:T(8,128)(2,1)}, u32[]{:S(2)}) copy-start(bf16[384,384]{1,0:T(8,128)(2,1)} %w_proj.1) | copy-start | bytes 884740
  1.8 9.7 %copy-start.5 = (f32[12]{0:T(128)S(1)}, f32[12]{0:T(128)}, u32[]{:S(2)}) copy-start(f32[12]{0:T(128)} %limit.3) | copy-start | bytes 148
  1.8 9.7 %copy-start.6 = (f32[384]{0:T(512)S(1)}, f32[384]{0:T(512)}, u32[]{:S(2)}) copy-start(f32[384]{0:T(512)} %gain.1) | copy-start | bytes 4612
  1.9 9.6 %collective-permute-start = (bf16[2,4,32,384]{3,2,1,0:T(8,128)(2,1)S(1)}, bf16[2,4,32,384]{3,2,1,0:T(8,128)(2,1)S(1)}, u32[]{:S(2)}, u32[]{:S(2)}) collective-permute-start(bf16[2,4,32,384]{3,2,1,0:T(8,128)(2,1)S(1)} %slice.28), channel_id=1, source_target_pairs={{0,28},{2,30},{4,0},{6,2},{8,4},{10,6},{12,8},{14,10},{16,12},{18,... | collective-permute-start | bytes 589832 | tf_op jit(solution)/shard_map/ppermute | solution.py:600
  6.5 4.9 %collective-permute-start.1 = (bf16[2,48,384]{2,1,0:T(8,128)(2,1)S(1)}, bf16[2,48,384]{2,1,0:T(8,128)(2,1)S(1)}, u32[]{:S(2)}, u32[]{:S(2)}) collective-permute-start(bf16[2,48,384]{2,1,0:T(8,128)(2,1)S(1)} %reshape.61), channel_id=1, source_target_pairs={{0,2},{2,0},{4,6},{6,4},{8,10},{10,8},{12,14},{14,12},{16,18},{18,... | collective-permute-start | bytes 221192 | tf_op jit(solution)/shard_map/ppermute | solution.py:601
  8.2 3.3 %collective-permute-start.2 = (bf16[2,16,384]{2,1,0:T(8,128)(2,1)S(1)}, bf16[2,16,384]{2,1,0:T(8,128)(2,1)S(1)}, u32[]{:S(2)}, u32[]{:S(2)}) collective-permute-start(bf16[2,16,384]{2,1,0:T(8,128)(2,1)S(1)} %reshape.62), channel_id=1, source_target_pairs={{0,30},{2,28},{4,2},{6,0},{8,6},{10,4},{12,10},{14,8},{16,14},{18,... | collective-permute-start | bytes 73736 | tf_op jit(solution)/shard_map/ppermute | solution.py:602
  20.7 2.1 %collective-permute-start.6 = (bf16[2,2,608,128]{3,2,1,0:T(8,128)(2,1)S(1)}, bf16[2,2,608,128]{3,2,1,0:T(8,128)(2,1)S(1)}, u32[]{:S(2)}, u32[]{:S(2)}) collective-permute-start(bf16[2,2,608,128]{3,2,1,0:T(8,128)(2,1)S(1)} %broadcast_multiply_fusion), channel_id=1, source_target_pairs={{0,4},{4,0},{1,5},{5,1},{2,6},{6,2},{3,7},{7,3},{8,12},{12,8},{9,1... | collective-permute-start | bytes 1867784 | tf_op jit(solution)/shard_map/ppermute | solution.py:629
  23.0 7.0 %collective-permute-start.7 = (bf16[2,608,128]{2,1,0:T(8,128)(2,1)S(1)}, bf16[2,608,128]{2,1,0:T(8,128)(2,1)S(1)}, u32[]{:S(2)}, u32[]{:S(2)}) collective-permute-start(bf16[2,608,128]{2,1,0:T(8,128)(2,1)S(1)} %dynamic-slice_bitcast_fusion), channel_id=1, source_target_pairs={{0,1},{1,0},{2,3},{3,2},{4,6},{5,7},{6,4},{7,5},{8,9},{9,8},{10,11... | collective-permute-start | bytes 933896 | tf_op jit(solution)/shard_map/ppermute | solution.py:588
  30.1 5.3 %collective-permute-start.8 = (bf16[608,128]{1,0:T(8,128)(2,1)S(1)}, bf16[608,128]{1,0:T(8,128)(2,1)S(1)}, u32[]{:S(2)}, u32[]{:S(2)}) collective-permute-start(bf16[608,128]{1,0:T(8,128)(2,1)S(1)} %dynamic-slice_bitcast_fusion.1), channel_id=1, source_target_pairs={{0,2},{1,3},{2,0},{3,1},{4,5},{5,4},{6,7},{7,6},{8,10},{9,11},{10,... | collective-permute-start | bytes 466952 | tf_op jit(solution)/shard_map/ppermute | solution.py:588
  35.5 5.9 %collective-permute-start.11 = (bf16[152,128]{1,0:T(8,128)(2,1)S(1)}, bf16[152,128]{1,0:T(8,128)(2,1)S(1)}, u32[]{:S(2)}, u32[]{:S(2)}) collective-permute-start(bf16[152,128]{1,0:T(8,128)(2,1)S(1)} %get-tuple-element.23), channel_id=1, source_target_pairs={{0,8},{8,16},{16,24},{24,0},{1,9},{9,17},{17,25},{25,1},{2,10},{10... | collective-permute-start | bytes 116744 | tf_op jit(solution)/shard_map/ppermute | solution.py:588
  35.5 6.5 %collective-permute-start.10 = (bf16[152,128]{1,0:T(8,128)(2,1)S(1)}, bf16[152,128]{1,0:T(8,128)(2,1)S(1)}, u32[]{:S(2)}, u32[]{:S(2)}) collective-permute-start(bf16[152,128]{1,0:T(8,128)(2,1)S(1)} %get-tuple-element.24), channel_id=1, source_target_pairs={{0,16},{8,24},{16,0},{24,8},{1,17},{9,25},{17,1},{25,9},{2,18},{10... | collective-permute-start | bytes 116744 | tf_op jit(solution)/shard_map/ppermute | solution.py:588
  39.2 4.0 %collective-permute-start.9 = (bf16[152,128]{1,0:T(8,128)(2,1)S(1)}, bf16[152,128]{1,0:T(8,128)(2,1)S(1)}, u32[]{:S(2)}, u32[]{:S(2)}) collective-permute-start(bf16[152,128]{1,0:T(8,128)(2,1)S(1)} %get-tuple-element.22), channel_id=1, source_target_pairs={{0,24},{8,0},{16,8},{24,16},{1,25},{9,1},{17,9},{25,17},{2,26},{10... | collective-permute-start | bytes 116744 | tf_op jit(solution)/shard_map/ppermute | solution.py:588
  44.0 14.1 %all-to-all-start = ((bf16[8,152,128]{2,1,0:T(8,128)(2,1)}), bf16[8,152,128]{2,1,0:T(8,128)(2,1)S(1)}, u32[]{:S(2)}, u32[]{:S(2)}) async-start(bf16[8,152,128]{2,1,0:T(8,128)(2,1)} %broadcast_in_dim.2), calls=%async_computation | async-start | bytes 622592 | tf_op jit(solution)/shard_map/all_to_all | solution.py:640
  47.9 5.0 %collective-permute-start.5 = (bf16[12,4,384]{2,1,0:T(4,128)(2,1)S(1)}, bf16[12,4,384]{2,1,0:T(4,128)(2,1)S(1)}, u32[]{:S(2)}, u32[]{:S(2)}) collective-permute-start(bf16[12,4,384]{2,1,0:T(4,128)(2,1)S(1)} %slice.26), channel_id=1, source_target_pairs={{0,2},{2,0},{4,6},{6,4},{8,10},{10,8},{12,14},{14,12},{16,18},{18,... | collective-permute-start | bytes 110600 | tf_op jit(solution)/shard_map/ppermute | solution.py:617
  50.1 8.0 %collective-permute-start.4 = (bf16[4,28,384]{2,1,0:T(8,128)(2,1)S(1)}, bf16[4,28,384]{2,1,0:T(8,128)(2,1)S(1)}, u32[]{:S(2)}, u32[]{:S(2)}) collective-permute-start(bf16[4,28,384]{2,1,0:T(8,128)(2,1)S(1)} %slice.25), channel_id=1, source_target_pairs={{0,4},{2,6},{4,8},{6,10},{8,12},{10,14},{12,16},{14,18},{16,20},{1... | collective-permute-start | bytes 258056 | tf_op jit(solution)/shard_map/ppermute | solution.py:618
  50.1 7.9 %collective-permute-start.3 = (bf16[4,4,384]{2,1,0:T(4,128)(2,1)S(1)}, bf16[4,4,384]{2,1,0:T(4,128)(2,1)S(1)}, u32[]{:S(2)}, u32[]{:S(2)}) collective-permute-start(bf16[4,4,384]{2,1,0:T(4,128)(2,1)S(1)} %slice.24), channel_id=1, source_target_pairs={{0,6},{2,4},{4,10},{6,8},{8,14},{10,12},{12,18},{14,16},{16,22},{1... | collective-permute-start | bytes 36872 | tf_op jit(solution)/shard_map/ppermute | solution.py:619
  58.0 1.6 %collective-permute-start.12 = (bf16[1216,128]{1,0:T(8,128)(2,1)S(1)}, bf16[1216,128]{1,0:T(8,128)(2,1)S(1)}, u32[]{:S(2)}, u32[]{:S(2)}) collective-permute-start(bf16[1216,128]{1,0:T(8,128)(2,1)S(1)} %bitcast.27), channel_id=1, source_target_pairs={{0,4},{4,0},{1,5},{5,1},{2,6},{6,2},{3,7},{7,3},{8,12},{12,8},{9,1... | collective-permute-start | bytes 933896 | tf_op jit(solution)/shard_map/ppermute | solution.py:642

commit v6 on v5

--- a/solution.py
+++ b/solution.py
@@ -493,15 +493,20 @@
     small_at = groups * body
     span = 2 * WIN - 1
 
-    def kernel(limit, ours, theirs, logits, d_wq, d_wp, d_table, d_scale, d_gain, whole):
+    def kernel(limit, ours, theirs, logits, d_wq, d_wp, d_table, d_scale, d_gain, whole, wq, wp, sems):
         core = lax.axis_index("hc")
         whole[pl.ds(pl.multiple_of(core * core_rows, 8), core_rows), :] = ours[...].astype(F32)
         other = pl.multiple_of((1 - core) * core_rows, 8)
         whole[pl.ds(other, core_rows), :] = theirs[...].astype(F32)
+        copies = []
         for j in range(groups):
             tile = slice(j * LANES, (j + 1) * LANES)
-            d_wq[:, tile] = whole[j * body : j * body + half_q, :]
-            d_wp[:, tile] = whole[j * body + half_q : (j + 1) * body, :]
+            wq[:, tile] = whole[j * body : j * body + half_q, :]
+            wp[:, tile] = whole[j * body + half_q : (j + 1) * body, :]
+            for k, (src, dst) in enumerate(((wq, d_wq), (wp, d_wp))):
+                copy = pltpu.make_async_copy(src.at[:, tile], dst.at[:, tile], sems.at[k, j])
+                copy.start()
+                copies.append(copy)
         small = whole[small_at : small_at + 32, :]
         near_map, far_map = table_maps(span, 2 * LANES)
         table = dot_nt(small[:16].astype(BF16), near_map)
@@ -517,6 +522,8 @@
             kept = jnp.where(lane == h, jnp.where(limit[h] < SCALE_CAP, 1.0, 0.0), kept)
         row = small[2 * heads + groups : 2 * heads + groups + 1, :] * kept
         d_scale[...] = row[:, :heads].reshape(heads)
+        for copy in copies:
+            copy.wait()
 
     vmem = pl.BlockSpec(memory_space=pltpu.VMEM)
     return pl.pallas_call(
@@ -529,8 +536,13 @@
             jax.ShapeDtypeStruct((depth,), F32),
         ),
         in_specs=[pl.BlockSpec(memory_space=pltpu.SMEM), vmem, vmem, vmem],
-        out_specs=(vmem,) * 5,
-        scratch_shapes=[pltpu.VMEM((2 * core_rows, LANES), F32)],
+        out_specs=(pl.BlockSpec(memory_space=pl.ANY),) * 2 + (vmem,) * 3,
+        scratch_shapes=[
+            pltpu.VMEM((2 * core_rows, LANES), F32),
+            pltpu.VMEM((half_q, depth), F32),
+            pltpu.VMEM((half_p, depth), F32),
+            pltpu.SemaphoreType.DMA((2, groups)),
+        ],
         compiler_params=pltpu.CompilerParams(vmem_limit_bytes=VMEM_LAST),
         name="finish",
     )(limit, ours, theirs, logits)

time: 61.6 us -> 62.3 us (1.011)
    pallas_call x1, Pallas kernels: 1.75 us -> 2.39 us  [finish(): pl.pallas_call(kernel, out_shape=(jax.ShapeDtypeStruct((half_q, depth), F...]
where the time goes in v6:
time: 62.3 us; the launch traced here: 62 us
  waiting for transfers between devices  24.9 us (40%)
  starting transfers between devices  21.2 us (34%)
  Pallas kernels  11.5 us (18%)
  local copies, waits for them, and re-layouts  2.19 us (4%)
  other arithmetic  1.34 us (2%)
  between operations  0.92 us (1%)
    ppermute x5, waiting for transfers between devices, hand_out(): total = total + lax.ppermute(sent, axes, route(axes, move(by))).astype(F32)  13.2 us
    pallas_call x1, Pallas kernels, call(): pl.pallas_call(kernel, out_shape=(jax.ShapeDtypeStruct((rows, cols, depth...  9.11 us
    ppermute x5, starting transfers between devices, hand_out(): total = total + lax.ppermute(sent, axes, route(axes, move(by))).astype(F32)  6.76 us
    all_to_all x1, waiting for transfers between devices, shards(): ours = lax.all_to_all(spread, ('wa', 'hz'), 0, 0, tiled=True)  5.05 us
    ppermute x1, starting transfers between devices, shards(): below = lax.ppermute(top, GRID, route(GRID, step(-1, 0)))  4.57 us
    all_to_all x1, starting transfers between devices, shards(): ours = lax.all_to_all(spread, ('wa', 'hz'), 0, 0, tiled=True)  3.92 us
    ppermute x1, waiting for transfers between devices, shards(): corner = lax.ppermute(tip, GRID, route(GRID, step(-1, -1)))  2.91 us
    pallas_call x1, Pallas kernels, finish(): pl.pallas_call(kernel, out_shape=(jax.ShapeDtypeStruct((half_q, depth), F...  2.39 us
  transfers between devices with their start and end apart: 14, of which 10 were waited for; matrix products, arithmetic and copies ran while one was open for 2% of the time, Pallas kernels for 0%

profile of v6, /device:TPU:0, one launch (start us, length us, event | category | flops | bytes accessed | tf_op | source)
XLA Modules:
  0.0 62.0 jit_solution(1720889046309119470)
XLA Ops:
  0.7 1.1 %constant_dynamic-update-slice_fusion.1 = bf16[2,16,32,384]{3,2,1,0:T(8,128)(2,1)S(1)} fusion(bf16[1,16,32,384]{3,2,1,0:T(8,128)(2,1)} %tok.1), kind=kLoop, calls=%fused_computation.19 | loop fusion | bytes 786432
  1.8 0.1 constant_dynamic-update-slice_fusion
  1.9 4.6 %collective-permute-start = (bf16[2,4,32,384]{3,2,1,0:T(8,128)(2,1)S(1)}, bf16[2,4,32,384]{3,2,1,0:T(8,128)(2,1)S(1)}, u32[]{:S(2)}, u32[]{:S(2)}) collective-permute-start(bf16[2,4,32,384]{3,2,1,0:T(8,128)(2,1)S(1)} %slice.28), channel_id=1, source_target_pairs={{0,28},{2,30},{4,0},{6,2},{8,4},{10,6},{12,8},{14,10},{16,12},{18,... | collective-permute-start | bytes 589832 | tf_op jit(solution)/shard_map/ppermute | solution.py:612
  6.5 1.6 %collective-permute-start.1 = (bf16[2,48,384]{2,1,0:T(8,128)(2,1)S(1)}, bf16[2,48,384]{2,1,0:T(8,128)(2,1)S(1)}, u32[]{:S(2)}, u32[]{:S(2)}) collective-permute-start(bf16[2,48,384]{2,1,0:T(8,128)(2,1)S(1)} %reshape.61), channel_id=1, source_target_pairs={{0,2},{2,0},{4,6},{6,4},{8,10},{10,8},{12,14},{14,12},{16,18},{18,... | collective-permute-start | bytes 221192 | tf_op jit(solution)/shard_map/ppermute | solution.py:613
  8.2 0.4 collective-permute-start.2
  8.5 2.9 %collective-permute-done.2.corner = bf16[2,16,384]{2,1,0:T(8,128)(2,1)S(1)} collective-permute-done((bf16[2,16,384]{2,1,0:T(8,128)(2,1)S(1)}, bf16[2,16,384]{2,1,0:T(8,128)(2,1)S(1)}, u32[]{:S(2)}, u32[]{:S(2)}) %collective-permute-start.2) | collective-permute-done | bytes 24608 | tf_op jit(solution)/shard_map/ppermute | solution.py:614
  11.5 9.1 %block_grads.1 = (bf16[16,32,384]{2,1,0:T(8,128)(2,1)S(1)}, bf16[2,2,608,128]{3,2,1,0:T(8,128)(2,1)S(1)}, bf16[2,2,608,128]{3,2,1,0:T(8,128)(2,1)S(1)}) custom-call(f32[12]{0:T(128)S(1)} %copy-done.5, bf16[1,16,32,384]{3,2,1,0:T(8,128)(2,1)S(1)} %copy-done.1, bf16[1,16,32,384]{3,2,1,0:T(8,128)(2,1)S(1)} %copy-done, ...), custom_call_target="tpu_custom_call" | custom-call | tf_op jit(solution)/shard_map/block_grads/pallas_call | solution.py:473
  20.7 0.1 collective-permute-start.6
  20.8 2.0 %collective-permute-done.6 = bf16[2,2,608,128]{3,2,1,0:T(8,128)(2,1)S(1)} collective-permute-done((bf16[2,2,608,128]{3,2,1,0:T(8,128)(2,1)S(1)}, bf16[2,2,608,128]{3,2,1,0:T(8,128)(2,1)S(1)}, u32[]{:S(2)}, u32[]{:S(2)}) %collective-permute-start.6) | collective-permute-done | bytes 622624 | tf_op jit(solution)/shard_map/ppermute | solution.py:641
  22.8 0.2 add_convert_fusion
  23.0 1.6 %collective-permute-start.7 = (bf16[2,608,128]{2,1,0:T(8,128)(2,1)S(1)}, bf16[2,608,128]{2,1,0:T(8,128)(2,1)S(1)}, u32[]{:S(2)}, u32[]{:S(2)}) collective-permute-start(bf16[2,608,128]{2,1,0:T(8,128)(2,1)S(1)} %dynamic-slice_bitcast_fusion), channel_id=1, source_target_pairs={{0,1},{1,0},{2,3},{3,2},{4,6},{5,7},{6,4},{7,5},{8,9},{9,8},{10,11... | collective-permute-start | bytes 933896 | tf_op jit(solution)/shard_map/ppermute | solution.py:600
  24.6 5.4 %collective-permute-done.7 = bf16[2,608,128]{2,1,0:T(8,128)(2,1)S(1)} collective-permute-done((bf16[2,608,128]{2,1,0:T(8,128)(2,1)S(1)}, bf16[2,608,128]{2,1,0:T(8,128)(2,1)S(1)}, u32[]{:S(2)}, u32[]{:S(2)}) %collective-permute-start.7) | collective-permute-done | bytes 311328 | tf_op jit(solution)/shard_map/ppermute | solution.py:600
  30.0 0.1 fusion
  30.1 1.3 %collective-permute-start.8 = (bf16[608,128]{1,0:T(8,128)(2,1)S(1)}, bf16[608,128]{1,0:T(8,128)(2,1)S(1)}, u32[]{:S(2)}, u32[]{:S(2)}) collective-permute-start(bf16[608,128]{1,0:T(8,128)(2,1)S(1)} %dynamic-slice_bitcast_fusion.1), channel_id=1, source_target_pairs={{0,2},{1,3},{2,0},{3,1},{4,5},{5,4},{6,7},{7,6},{8,10},{9,11},{10,... | collective-permute-start | bytes 466952 | tf_op jit(solution)/shard_map/ppermute | solution.py:600
  31.4 4.0 %collective-permute-done.8 = bf16[608,128]{1,0:T(8,128)(2,1)S(1)} collective-permute-done((bf16[608,128]{1,0:T(8,128)(2,1)S(1)}, bf16[608,128]{1,0:T(8,128)(2,1)S(1)}, u32[]{:S(2)}, u32[]{:S(2)}) %collective-permute-start.8) | collective-permute-done | bytes 155680 | tf_op jit(solution)/shard_map/ppermute | solution.py:600
  35.5 0.1 collective-permute-start.11
  35.5 3.7 %collective-permute-start.10 = (bf16[152,128]{1,0:T(8,128)(2,1)S(1)}, bf16[152,128]{1,0:T(8,128)(2,1)S(1)}, u32[]{:S(2)}, u32[]{:S(2)}) collective-permute-start(bf16[152,128]{1,0:T(8,128)(2,1)S(1)} %get-tuple-element.24), channel_id=1, source_target_pairs={{0,16},{8,24},{16,0},{24,8},{1,17},{9,25},{17,1},{25,9},{2,18},{10... | collective-permute-start | bytes 116744 | tf_op jit(solution)/shard_map/ppermute | solution.py:600
  39.2 0.1 collective-permute-start.9
  39.3 2.1 %collective-permute-done.11 = bf16[152,128]{1,0:T(8,128)(2,1)S(1)} collective-permute-done((bf16[152,128]{1,0:T(8,128)(2,1)S(1)}, bf16[152,128]{1,0:T(8,128)(2,1)S(1)}, u32[]{:S(2)}, u32[]{:S(2)}) %collective-permute-start.11) | collective-permute-done | bytes 38944 | tf_op jit(solution)/shard_map/ppermute | solution.py:600
  41.4 0.6 collective-permute-done.10
  42.0 1.2 %collective-permute-done.9 = bf16[152,128]{1,0:T(8,128)(2,1)S(1)} collective-permute-done((bf16[152,128]{1,0:T(8,128)(2,1)S(1)}, bf16[152,128]{1,0:T(8,128)(2,1)S(1)}, u32[]{:S(2)}, u32[]{:S(2)}) %collective-permute-start.9) | collective-permute-done | bytes 38944 | tf_op jit(solution)/shard_map/ppermute | solution.py:600
  43.2 0.8 %broadcast_in_dim.2 = bf16[8,152,128]{2,1,0:T(8,128)(2,1)} broadcast(bf16[152,128]{1,0:T(8,128)(2,1)S(1)} %fusion.4), dimensions={1,2} | broadcast | bytes 350208 | tf_op jit(solution)/shard_map/broadcast_in_dim | solution.py:651
  44.0 3.9 %all-to-all-start = ((bf16[8,152,128]{2,1,0:T(8,128)(2,1)}), bf16[8,152,128]{2,1,0:T(8,128)(2,1)S(1)}, u32[]{:S(2)}, u32[]{:S(2)}) async-start(bf16[8,152,128]{2,1,0:T(8,128)(2,1)} %broadcast_in_dim.2), calls=%async_computation | async-start | bytes 622592 | tf_op jit(solution)/shard_map/all_to_all | solution.py:652
  47.9 2.1 %collective-permute-start.5 = (bf16[12,4,384]{2,1,0:T(4,128)(2,1)S(1)}, bf16[12,4,384]{2,1,0:T(4,128)(2,1)S(1)}, u32[]{:S(2)}, u32[]{:S(2)}) collective-permute-start(bf16[12,4,384]{2,1,0:T(4,128)(2,1)S(1)} %slice.26), channel_id=1, source_target_pairs={{0,2},{2,0},{4,6},{6,4},{8,10},{10,8},{12,14},{14,12},{16,18},{18,... | collective-permute-start | bytes 110600 | tf_op jit(solution)/shard_map/ppermute | solution.py:629
  50.1 0.1 collective-permute-start.4
  50.1 1.7 %collective-permute-start.3 = (bf16[4,4,384]{2,1,0:T(4,128)(2,1)S(1)}, bf16[4,4,384]{2,1,0:T(4,128)(2,1)S(1)}, u32[]{:S(2)}, u32[]{:S(2)}) collective-permute-start(bf16[4,4,384]{2,1,0:T(4,128)(2,1)S(1)} %slice.24), channel_id=1, source_target_pairs={{0,6},{2,4},{4,10},{6,8},{8,14},{10,12},{12,18},{14,16},{16,22},{1... | collective-permute-start | bytes 36872 | tf_op jit(solution)/shard_map/ppermute | solution.py:631
  51.9 1.0 %collective-permute-done.5 = bf16[12,4,384]{2,1,0:T(4,128)(2,1)S(1)} collective-permute-done((bf16[12,4,384]{2,1,0:T(4,128)(2,1)S(1)}, bf16[12,4,384]{2,1,0:T(4,128)(2,1)S(1)}, u32[]{:S(2)}, u32[]{:S(2)}) %collective-permute-start.5) | collective-permute-done | bytes 36896 | tf_op jit(solution)/shard_map/ppermute | solution.py:629
  52.9 0.1 maximum_bitcast_fusion
  53.0 5.1 %all-to-all-done = bf16[8,152,128]{2,1,0:T(8,128)(2,1)S(1)} async-done(((bf16[8,152,128]{2,1,0:T(8,128)(2,1)}), bf16[8,152,128]{2,1,0:T(8,128)(2,1)S(1)}, u32[]{:S(2)}, u32[]{:S(2)}) %all-to-all-start) | async-done | bytes 311328 | tf_op jit(solution)/shard_map/all_to_all | solution.py:652
  58.1 0.8 %add_convert_fusion.1 = bf16[1,16,32,384]{3,2,1,0:T(8,128)(2,1)} fusion(bf16[1,16,32,384]{3,2,1,0:T(8,128)(2,1)S(1)} %copy-done, bf16[1,12,32,384]{3,2,1,0:T(8,128)(2,1)S(1)} %maximum_bitcast_fusion, bf16[1,4,32,384]{3,2,1,0:T(8,128)(2,1)S(1)} %maximum_bitcast_fusion.1), kind=kLoop, calls=%fused_computation.1 | loop fusion | flops 983040 | bytes 1179648 | tf_op jit(solution)/shard_map/convert_element_type | solution.py:637
  58.9 0.7 %collective-permute-done.12.theirs = bf16[1216,128]{1,0:T(8,128)(2,1)S(1)} collective-permute-done((bf16[1216,128]{1,0:T(8,128)(2,1)S(1)}, bf16[1216,128]{1,0:T(8,128)(2,1)S(1)}, u32[]{:S(2)}, u32[]{:S(2)}) %collective-permute-start.12) | collective-permute-done | bytes 311328 | tf_op jit(solution)/shard_map/ppermute | solution.py:654
  59.7 2.4 %finish.1 = (f32[576,384]{1,0:T(8,128)}, f32[192,384]{1,0:T(8,128)}, f32[12,225]{1,0:T(8,128)}, f32[12]{0:T(128)}, f32[384]{0:T(512)}) custom-call(f32[12]{0:T(128)S(1)} %copy-done.5, bf16[1216,128]{1,0:T(8,128)(2,1)S(1)} %bitcast.28, bf16[1216,128]{1,0:T(8,128)(2,1)S(1)} %collective-permute-done.12.theirs, f32[12,225]{1,0:T(8,128)S(1)} %copy-done.4), custom_call_target="tpu_custom_call" | custom-call | tf_op jit(solution)/shard_map/finish/pallas_call | solution.py:529
  (35 shorter events, 0.4 us)
Async XLA Ops:
  0.6 1.1 %copy-start = (bf16[1,16,32,384]{3,2,1,0:T(8,128)(2,1)S(1)}, bf16[1,16,32,384]{3,2,1,0:T(8,128)(2,1)}, u32[]{:S(2)}) copy-start(bf16[1,16,32,384]{3,2,1,0:T(8,128)(2,1)} %cot.1) | copy-start | bytes 1179652
  0.6 10.8 %copy-start.4 = (f32[12,225]{1,0:T(8,128)S(1)}, f32[12,225]{1,0:T(8,128)}, u32[]{:S(2)}) copy-start(f32[12,225]{1,0:T(8,128)} %logits.3) | copy-start | bytes 32404
  1.8 9.7 %copy-start.1 = (bf16[1,16,32,384]{3,2,1,0:T(8,128)(2,1)S(1)}, bf16[1,16,32,384]{3,2,1,0:T(8,128)(2,1)}, u32[]{:S(2)}) copy-start(bf16[1,16,32,384]{3,2,1,0:T(8,128)(2,1)} %tok.1) | copy-start | bytes 1179652
  1.8 9.7 %copy-start.2 = (bf16[384,1152]{1,0:T(8,128)(2,1)S(1)}, bf16[384,1152]{1,0:T(8,128)(2,1)}, u32[]{:S(2)}) copy-start(bf16[384,1152]{1,0:T(8,128)(2,1)} %w_qkv.1) | copy-start | bytes 2654212
  1.8 9.7 %copy-start.3 = (bf16[384,384]{1,0:T(8,128)(2,1)S(1)}, bf16[384,384]{1,0:T(8,128)(2,1)}, u32[]{:S(2)}) copy-start(bf16[384,384]{1,0:T(8,128)(2,1)} %w_proj.1) | copy-start | bytes 884740
  1.8 9.7 %copy-start.5 = (f32[12]{0:T(128)S(1)}, f32[12]{0:T(128)}, u32[]{:S(2)}) copy-start(f32[12]{0:T(128)} %limit.3) | copy-start | bytes 148
  1.8 9.7 %copy-start.6 = (f32[384]{0:T(512)S(1)}, f32[384]{0:T(512)}, u32[]{:S(2)}) copy-start(f32[384]{0:T(512)} %gain.1) | copy-start | bytes 4612
  1.9 9.6 %collective-permute-start = (bf16[2,4,32,384]{3,2,1,0:T(8,128)(2,1)S(1)}, bf16[2,4,32,384]{3,2,1,0:T(8,128)(2,1)S(1)}, u32[]{:S(2)}, u32[]{:S(2)}) collective-permute-start(bf16[2,4,32,384]{3,2,1,0:T(8,128)(2,1)S(1)} %slice.28), channel_id=1, source_target_pairs={{0,28},{2,30},{4,0},{6,2},{8,4},{10,6},{12,8},{14,10},{16,12},{18,... | collective-permute-start | bytes 589832 | tf_op jit(solution)/shard_map/ppermute | solution.py:612
  6.5 4.9 %collective-permute-start.1 = (bf16[2,48,384]{2,1,0:T(8,128)(2,1)S(1)}, bf16[2,48,384]{2,1,0:T(8,128)(2,1)S(1)}, u32[]{:S(2)}, u32[]{:S(2)}) collective-permute-start(bf16[2,48,384]{2,1,0:T(8,128)(2,1)S(1)} %reshape.61), channel_id=1, source_target_pairs={{0,2},{2,0},{4,6},{6,4},{8,10},{10,8},{12,14},{14,12},{16,18},{18,... | collective-permute-start | bytes 221192 | tf_op jit(solution)/shard_map/ppermute | solution.py:613
  8.2 3.3 %collective-permute-start.2 = (bf16[2,16,384]{2,1,0:T(8,128)(2,1)S(1)}, bf16[2,16,384]{2,1,0:T(8,128)(2,1)S(1)}, u32[]{:S(2)}, u32[]{:S(2)}) collective-permute-start(bf16[2,16,384]{2,1,0:T(8,128)(2,1)S(1)} %reshape.62), channel_id=1, source_target_pairs={{0,30},{2,28},{4,2},{6,0},{8,6},{10,4},{12,10},{14,8},{16,14},{18,... | collective-permute-start | bytes 73736 | tf_op jit(solution)/shard_map/ppermute | solution.py:614
  20.7 2.1 %collective-permute-start.6 = (bf16[2,2,608,128]{3,2,1,0:T(8,128)(2,1)S(1)}, bf16[2,2,608,128]{3,2,1,0:T(8,128)(2,1)S(1)}, u32[]{:S(2)}, u32[]{:S(2)}) collective-permute-start(bf16[2,2,608,128]{3,2,1,0:T(8,128)(2,1)S(1)} %broadcast_multiply_fusion), channel_id=1, source_target_pairs={{0,4},{4,0},{1,5},{5,1},{2,6},{6,2},{3,7},{7,3},{8,12},{12,8},{9,1... | collective-permute-start | bytes 1867784 | tf_op jit(solution)/shard_map/ppermute | solution.py:641
  23.0 7.0 %collective-permute-start.7 = (bf16[2,608,128]{2,1,0:T(8,128)(2,1)S(1)}, bf16[2,608,128]{2,1,0:T(8,128)(2,1)S(1)}, u32[]{:S(2)}, u32[]{:S(2)}) collective-permute-start(bf16[2,608,128]{2,1,0:T(8,128)(2,1)S(1)} %dynamic-slice_bitcast_fusion), channel_id=1, source_target_pairs={{0,1},{1,0},{2,3},{3,2},{4,6},{5,7},{6,4},{7,5},{8,9},{9,8},{10,11... | collective-permute-start | bytes 933896 | tf_op jit(solution)/shard_map/ppermute | solution.py:600
  30.1 5.3 %collective-permute-start.8 = (bf16[608,128]{1,0:T(8,128)(2,1)S(1)}, bf16[608,128]{1,0:T(8,128)(2,1)S(1)}, u32[]{:S(2)}, u32[]{:S(2)}) collective-permute-start(bf16[608,128]{1,0:T(8,128)(2,1)S(1)} %dynamic-slice_bitcast_fusion.1), channel_id=1, source_target_pairs={{0,2},{1,3},{2,0},{3,1},{4,5},{5,4},{6,7},{7,6},{8,10},{9,11},{10,... | collective-permute-start | bytes 466952 | tf_op jit(solution)/shard_map/ppermute | solution.py:600
  35.5 5.9 %collective-permute-start.11 = (bf16[152,128]{1,0:T(8,128)(2,1)S(1)}, bf16[152,128]{1,0:T(8,128)(2,1)S(1)}, u32[]{:S(2)}, u32[]{:S(2)}) collective-permute-start(bf16[152,128]{1,0:T(8,128)(2,1)S(1)} %get-tuple-element.23), channel_id=1, source_target_pairs={{0,8},{8,16},{16,24},{24,0},{1,9},{9,17},{17,25},{25,1},{2,10},{10... | collective-permute-start | bytes 116744 | tf_op jit(solution)/shard_map/ppermute | solution.py:600
  35.5 6.5 %collective-permute-start.10 = (bf16[152,128]{1,0:T(8,128)(2,1)S(1)}, bf16[152,128]{1,0:T(8,128)(2,1)S(1)}, u32[]{:S(2)}, u32[]{:S(2)}) collective-permute-start(bf16[152,128]{1,0:T(8,128)(2,1)S(1)} %get-tuple-element.24), channel_id=1, source_target_pairs={{0,16},{8,24},{16,0},{24,8},{1,17},{9,25},{17,1},{25,9},{2,18},{10... | collective-permute-start | bytes 116744 | tf_op jit(solution)/shard_map/ppermute | solution.py:600
  39.2 4.0 %collective-permute-start.9 = (bf16[152,128]{1,0:T(8,128)(2,1)S(1)}, bf16[152,128]{1,0:T(8,128)(2,1)S(1)}, u32[]{:S(2)}, u32[]{:S(2)}) collective-permute-start(bf16[152,128]{1,0:T(8,128)(2,1)S(1)} %get-tuple-element.22), channel_id=1, source_target_pairs={{0,24},{8,0},{16,8},{24,16},{1,25},{9,1},{17,9},{25,17},{2,26},{10... | collective-permute-start | bytes 116744 | tf_op jit(solution)/shard_map/ppermute | solution.py:600
  44.0 14.1 %all-to-all-start = ((bf16[8,152,128]{2,1,0:T(8,128)(2,1)}), bf16[8,152,128]{2,1,0:T(8,128)(2,1)S(1)}, u32[]{:S(2)}, u32[]{:S(2)}) async-start(bf16[8,152,128]{2,1,0:T(8,128)(2,1)} %broadcast_in_dim.2), calls=%async_computation | async-start | bytes 622592 | tf_op jit(solution)/shard_map/all_to_all | solution.py:652
  47.9 5.0 %collective-permute-start.5 = (bf16[12,4,384]{2,1,0:T(4,128)(2,1)S(1)}, bf16[12,4,384]{2,1,0:T(4,128)(2,1)S(1)}, u32[]{:S(2)}, u32[]{:S(2)}) collective-permute-start(bf16[12,4,384]{2,1,0:T(4,128)(2,1)S(1)} %slice.26), channel_id=1, source_target_pairs={{0,2},{2,0},{4,6},{6,4},{8,10},{10,8},{12,14},{14,12},{16,18},{18,... | collective-permute-start | bytes 110600 | tf_op jit(solution)/shard_map/ppermute | solution.py:629
  50.1 8.0 %collective-permute-start.4 = (bf16[4,28,384]{2,1,0:T(8,128)(2,1)S(1)}, bf16[4,28,384]{2,1,0:T(8,128)(2,1)S(1)}, u32[]{:S(2)}, u32[]{:S(2)}) collective-permute-start(bf16[4,28,384]{2,1,0:T(8,128)(2,1)S(1)} %slice.25), channel_id=1, source_target_pairs={{0,4},{2,6},{4,8},{6,10},{8,12},{10,14},{12,16},{14,18},{16,20},{1... | collective-permute-start | bytes 258056 | tf_op jit(solution)/shard_map/ppermute | solution.py:630
  50.1 7.9 %collective-permute-start.3 = (bf16[4,4,384]{2,1,0:T(4,128)(2,1)S(1)}, bf16[4,4,384]{2,1,0:T(4,128)(2,1)S(1)}, u32[]{:S(2)}, u32[]{:S(2)}) collective-permute-start(bf16[4,4,384]{2,1,0:T(4,128)(2,1)S(1)} %slice.24), channel_id=1, source_target_pairs={{0,6},{2,4},{4,10},{6,8},{8,14},{10,12},{12,18},{14,16},{16,22},{1... | collective-permute-start | bytes 36872 | tf_op jit(solution)/shard_map/ppermute | solution.py:631
  58.0 1.6 %collective-permute-start.12 = (bf16[1216,128]{1,0:T(8,128)(2,1)S(1)}, bf16[1216,128]{1,0:T(8,128)(2,1)S(1)}, u32[]{:S(2)}, u32[]{:S(2)}) collective-permute-start(bf16[1216,128]{1,0:T(8,128)(2,1)S(1)} %bitcast.27), channel_id=1, source_target_pairs={{0,4},{4,0},{1,5},{5,1},{2,6},{6,2},{3,7},{7,3},{8,12},{12,8},{9,1... | collective-permute-start | bytes 933896 | tf_op jit(solution)/shard_map/ppermute | solution.py:654
